TPU v7x, 32 devices: a whole 2x2x4 slice. The times are simulated.
32 devices in a mesh: replica: 4 (over x, core), shard: 8 (over z, y).
Axes of the slice: x: 2, y: 2, z: 4, core: 2. Of those that a mesh axis runs over, the one named last changes fastest.
Arguments:
- tokens: bfloat16 [8, 1024, 768], P('replica', 'shard'), may hold values from -6 to 6
- gain_one: bfloat16 [2, 768], P(None, 'shard'), may hold values from 0.099609375 to 1.8984375
- shift_one: bfloat16 [2, 768], P(None, 'shard'), may hold values from -4 to 4
- query_key_value_weight: bfloat16 [2, 768, 2304], P(None, 'shard'), may hold values from -0.21875 to 0.21875
- b_query: bfloat16 [2, 768], P(None, 'shard'), may hold values from -4 to 4
- b_value: bfloat16 [2, 768], P(None, 'shard'), may hold values from -4 to 4
- output_weight: bfloat16 [2, 768, 768], P(None, 'shard'), may hold values from -3.5 to 3.5
- output_proj_bias: bfloat16 [2, 768], P(None, 'shard'), may hold values from -4 to 4
- gain_two: bfloat16 [2, 768], P(None, 'shard'), may hold values from 0.099609375 to 1.8984375
- shift_two: bfloat16 [2, 768], P(None, 'shard'), may hold values from -4 to 4
- up_weight: bfloat16 [2, 768, 3072], P(None, 'shard'), may hold values from -0.21875 to 0.21875
- up_bias: bfloat16 [2, 3072], P(None, 'shard'), may hold values from -4 to 4
- down_weight: bfloat16 [2, 3072, 768], P(None, 'shard'), may hold values from -0.109375 to 0.109375
- down_bias: bfloat16 [2, 768], P(None, 'shard'), may hold values from -4 to 4
- cotangent: bfloat16 [8, 1024, 768], P('replica', 'shard'), may hold values from -6 to 6
Outputs:
- output: bfloat16 [8, 1024, 768], P('replica', 'shard')
- grad_tokens: float32 [8, 1024, 768], P('replica', 'shard')
- grad_gain_one: float32 [2, 768], P(None, 'shard')
- grad_shift_one: float32 [2, 768], P(None, 'shard')
- query_key_value_gradient: float32 [2, 768, 2304], P(None, 'shard')
- grad_b_query: float32 [2, 768], P(None, 'shard')
- grad_b_value: float32 [2, 768], P(None, 'shard')
- output_weight_gradient: float32 [2, 768, 768], P(None, 'shard')
- grad_b_out: float32 [2, 768], P(None, 'shard')
- grad_gain_two: float32 [2, 768], P(None, 'shard')
- grad_shift_two: float32 [2, 768], P(None, 'shard')
- up_weight_gradient: float32 [2, 768, 3072], P(None, 'shard')
- grad_b_up: float32 [2, 3072], P(None, 'shard')
- down_weight_gradient: float32 [2, 3072, 768], P(None, 'shard')
- grad_b_down: float32 [2, 768], P(None, 'shard')
All inputs are finite; a program needn't handle non-finite values.
Results may differ from a plain program's by a relative error of at most 0.015.
The roundings to bfloat16 on the way count: a program that leaves them out, or rounds other values in their place, can miss the bound.
Values may be sent and summed in bfloat16 or wider, within the bound.
A program may use at most 256 MiB of HBM per device.

v0:
```python
import jax
import jax.numpy as jnp
from jax import lax
from jax.sharding import PartitionSpec as P

HEADS = 12


epsilon = 1e-05
masked_value = -1e30


def norm_rows(values, gain, shift):
    centre = values - jnp.mean(values, -1, keepdims=True)
    spread = jnp.mean(centre * centre, -1, keepdims=True)
    return centre * lax.rsqrt(spread + epsilon) * gain + shift


def fetch_forward(stacked, depth_index):
    (
        gain_one,
        shift_one,
        query_key_value_weight,
        b_query,
        b_value,
        output_weight,
        output_proj_bias,
        gain_two,
        shift_two,
        up_weight,
        up_bias,
        down_weight,
        down_bias,
    ) = tuple((array[depth_index] for array in stacked))
    return (
        lax.all_gather(gain_one, "shard", axis=0, tiled=True),
        lax.all_gather(shift_one, "shard", axis=0, tiled=True),
        lax.all_gather(query_key_value_weight, "shard", axis=0, tiled=True),
        lax.all_gather(b_query, "shard", axis=0, tiled=True),
        lax.all_gather(b_value, "shard", axis=0, tiled=True),
        lax.all_gather(output_weight, "shard", axis=0, tiled=True),
        lax.all_gather(output_proj_bias, "shard", axis=0, tiled=True),
        lax.all_gather(gain_two, "shard", axis=0, tiled=True),
        lax.all_gather(shift_two, "shard", axis=0, tiled=True),
        lax.all_gather(up_weight, "shard", axis=0, tiled=True),
        lax.all_gather(up_bias, "shard", axis=0, tiled=True),
        lax.all_gather(down_weight, "shard", axis=0, tiled=True),
        lax.all_gather(down_bias, "shard", axis=0, tiled=True),
    )


def fetch_again(stacked, depth_index):
    (
        gain_one,
        shift_one,
        query_key_value_weight,
        b_query,
        b_value,
        output_weight,
        output_proj_bias,
        gain_two,
        shift_two,
        up_weight,
        up_bias,
        down_weight,
        down_bias,
    ) = tuple((array[depth_index] for array in stacked))
    return (
        lax.all_gather(gain_one, "shard", axis=0, tiled=True),
        lax.all_gather(shift_one, "shard", axis=0, tiled=True),
        lax.all_gather(query_key_value_weight, "shard", axis=0, tiled=True),
        lax.all_gather(b_query, "shard", axis=0, tiled=True),
        lax.all_gather(b_value, "shard", axis=0, tiled=True),
        lax.all_gather(output_weight, "shard", axis=0, tiled=True),
        lax.all_gather(output_proj_bias, "shard", axis=0, tiled=True),
        lax.all_gather(gain_two, "shard", axis=0, tiled=True),
        lax.all_gather(shift_two, "shard", axis=0, tiled=True),
        lax.all_gather(up_weight, "shard", axis=0, tiled=True),
        lax.all_gather(up_bias, "shard", axis=0, tiled=True),
        lax.all_gather(down_weight, "shard", axis=0, tiled=True),
        lax.all_gather(down_bias, "shard", axis=0, tiled=True),
    )


def split_heads(values):
    return values.reshape(values.shape[0], values.shape[1], HEADS, values.shape[2] // HEADS)


def masked_scores(query, keys, causal):
    query_heads = split_heads(query)
    key_heads = split_heads(keys)
    scale = query_heads.shape[-1] ** (-0.5)
    scores = (
        jnp.einsum("sqhe,skhe->shqk", query_heads, key_heads, preferred_element_type=jnp.float32)
        * scale
    )
    return (jnp.where(causal[None, None, :, :], scores, masked_value), scale)


def forward_block(current, full, causal):
    (
        gain_one,
        shift_one,
        query_key_value_weight,
        b_query,
        b_value,
        output_weight,
        output_proj_bias,
        gain_two,
        shift_two,
        up_weight,
        up_bias,
        down_weight,
        down_bias,
    ) = full
    width = current.shape[-1]
    normalized_input = norm_rows(
        current, gain_one.astype(jnp.float32), shift_one.astype(jnp.float32)
    ).astype(jnp.bfloat16)
    mixture_output = jnp.einsum(
        "rbu,ua->rba", normalized_input, query_key_value_weight, preferred_element_type=jnp.float32
    )
    query = (mixture_output[..., :width] + b_query.astype(jnp.float32)).astype(jnp.bfloat16)
    key_part = mixture_output[..., width : 2 * width].astype(jnp.bfloat16)
    value_part = (mixture_output[..., 2 * width :] + b_value.astype(jnp.float32)).astype(
        jnp.bfloat16
    )
    keys, values = (
        lax.all_gather(key_part, "shard", axis=1, tiled=True),
        lax.all_gather(value_part, "shard", axis=1, tiled=True),
    )
    scores, scale = masked_scores(query, keys, causal)
    maxima = jnp.max(scores, -1, keepdims=True)
    expo = jnp.exp(scores - maxima)
    totals = jnp.sum(expo, -1, keepdims=True)
    probs = (expo / totals).astype(jnp.bfloat16)
    log_totals = maxima + jnp.log(totals)
    attention_output = jnp.einsum(
        "shqk,skhe->sqhe", probs, split_heads(values), preferred_element_type=jnp.float32
    )
    attention_output = attention_output.reshape(current.shape).astype(jnp.bfloat16)
    residual_branch = jnp.einsum(
        "rbu,ua->rba", attention_output, output_weight, preferred_element_type=jnp.float32
    ) + output_proj_bias.astype(jnp.float32)
    x_mid = current + residual_branch
    shifted_values = norm_rows(
        x_mid, gain_two.astype(jnp.float32), shift_two.astype(jnp.float32)
    ).astype(jnp.bfloat16)
    preactivation_values = jnp.einsum(
        "vjo,op->vjp", shifted_values, up_weight, preferred_element_type=jnp.float32
    ) + up_bias.astype(jnp.float32)
    activation_values = jax.nn.gelu(preactivation_values, approximate=True).astype(jnp.bfloat16)
    result = (
        x_mid
        + jnp.einsum(
            "zxm,mv->zxv", activation_values, down_weight, preferred_element_type=jnp.float32
        )
        + down_bias.astype(jnp.float32)
    )
    saved = (
        current,
        normalized_input,
        query,
        keys,
        values,
        log_totals,
        attention_output,
        x_mid,
        shifted_values,
        preactivation_values,
        activation_values,
    )
    return (result, saved)


def owned_key_sums(query, attention_gradient, keys, values, log_totals, row_dots, scale):
    own_rows = query.shape[1]
    key_start = lax.axis_index("shard") * own_rows
    own_keys = split_heads(lax.dynamic_slice_in_dim(keys, key_start, own_rows, 1))
    own_values = split_heads(lax.dynamic_slice_in_dim(values, key_start, own_rows, 1))
    key_place = key_start + jnp.arange(own_rows, dtype=jnp.int32)
    all_totals, all_dots = (
        lax.all_gather(log_totals, "shard", axis=2, tiled=True),
        lax.all_gather(row_dots, "shard", axis=2, tiled=True),
    )
    zero_sums = jnp.zeros(query.shape, jnp.float32)
    query_piece = lax.all_gather(query, "shard", axis=1, tiled=True)
    d_piece = lax.all_gather(attention_gradient, "shard", axis=1, tiled=True)
    count = query_piece.shape[1]
    query_heads = split_heads(query_piece)
    d_heads = split_heads(d_piece)
    raw_scores = (
        jnp.einsum("sqhe,skhe->shqk", query_heads, own_keys, preferred_element_type=jnp.float32)
        * scale
    )
    query_place = jnp.arange(count, dtype=jnp.int32)
    allowed = query_place[:, None] >= key_place[None, :]
    raw_scores = jnp.where(allowed[None, None, :, :], raw_scores, masked_value)
    piece_probs = jnp.exp(raw_scores - all_totals)
    piece_dp = jnp.einsum(
        "sqhe,skhe->shqk", d_heads, own_values, preferred_element_type=jnp.float32
    )
    piece_ds = (piece_probs * (piece_dp - all_dots) * scale).astype(jnp.bfloat16)
    key_add = jnp.einsum(
        "shqk,sqhe->skhe", piece_ds, query_heads, preferred_element_type=jnp.float32
    )
    value_add = jnp.einsum(
        "shqk,sqhe->skhe",
        piece_probs.astype(jnp.bfloat16),
        d_heads,
        preferred_element_type=jnp.float32,
    )
    return (key_add.reshape(zero_sums.shape), value_add.reshape(zero_sums.shape))


def backward_block(grad_next, full, saved, causal):
    (
        gain_one,
        shift_one,
        query_key_value_weight,
        b_query,
        b_value,
        output_weight,
        output_proj_bias,
        gain_two,
        shift_two,
        up_weight,
        up_bias,
        down_weight,
        down_bias,
    ) = full
    (
        current,
        normalized_input,
        query,
        keys,
        values,
        log_totals,
        attention_output,
        x_mid,
        shifted_values,
        preactivation_values,
        activation_values,
    ) = saved
    feedforward_gradient = grad_next.astype(jnp.bfloat16)
    down_weight_gradient = jnp.einsum(
        "tpn,tpc->nc", activation_values, feedforward_gradient, preferred_element_type=jnp.float32
    )
    grad_b_down = jnp.sum(feedforward_gradient.astype(jnp.float32), (0, 1))
    activation_gradient = jnp.einsum(
        "zva,ba->zvb", feedforward_gradient, down_weight, preferred_element_type=jnp.float32
    )
    gelu_back = jax.vjp(lambda inner: jax.nn.gelu(inner, approximate=True), preactivation_values)[1]
    preactivation_gradient = gelu_back(activation_gradient)[0].astype(jnp.bfloat16)
    up_weight_gradient = jnp.einsum(
        "mkn,mka->na", shifted_values, preactivation_gradient, preferred_element_type=jnp.float32
    )
    grad_b_up = jnp.sum(preactivation_gradient.astype(jnp.float32), (0, 1))
    shifted_gradient = jnp.einsum(
        "wcb,qb->wcq", preactivation_gradient, up_weight, preferred_element_type=jnp.float32
    )
    norm_back = jax.vjp(
        norm_rows, x_mid, gain_two.astype(jnp.float32), shift_two.astype(jnp.float32)
    )[1]
    d_from_norm, grad_gain_two, grad_shift_two = norm_back(shifted_gradient)
    grad_mid = grad_next + d_from_norm
    branch_gradient = grad_mid.astype(jnp.bfloat16)
    output_weight_gradient = jnp.einsum(
        "mgw,mgc->wc", attention_output, branch_gradient, preferred_element_type=jnp.float32
    )
    grad_b_out = jnp.sum(branch_gradient.astype(jnp.float32), (0, 1))
    attention_gradient = jnp.einsum(
        "qmj,tj->qmt", branch_gradient, output_weight, preferred_element_type=jnp.float32
    ).astype(jnp.bfloat16)
    d_att_heads = split_heads(attention_gradient)
    scores, scale = masked_scores(query, keys, causal)
    probs = jnp.exp(scores - log_totals)
    value_heads = split_heads(values)
    d_probs = jnp.einsum(
        "sqhe,skhe->shqk", d_att_heads, value_heads, preferred_element_type=jnp.float32
    )
    row_dots = jnp.sum(d_probs * probs, -1, keepdims=True)
    d_scores = (probs * (d_probs - row_dots) * scale).astype(jnp.bfloat16)
    d_query = jnp.einsum(
        "shqk,skhe->sqhe", d_scores, split_heads(keys), preferred_element_type=jnp.float32
    )
    d_key, d_value = owned_key_sums(
        query, attention_gradient, keys, values, log_totals, row_dots, scale
    )
    d_query = d_query.reshape(query.shape).astype(jnp.bfloat16)
    d_key = d_key.astype(jnp.bfloat16)
    d_value = d_value.astype(jnp.bfloat16)
    mixture_gradient = jnp.concatenate([d_query, d_key, d_value], -1)
    query_key_value_gradient = jnp.einsum(
        "mgw,mgc->wc", normalized_input, mixture_gradient, preferred_element_type=jnp.float32
    )
    grad_b_query = jnp.sum(d_query.astype(jnp.float32), (0, 1))
    grad_b_value = jnp.sum(d_value.astype(jnp.float32), (0, 1))
    normalized_gradient = jnp.einsum(
        "qmj,tj->qmt", mixture_gradient, query_key_value_weight, preferred_element_type=jnp.float32
    )
    first_back = jax.vjp(
        norm_rows, current, gain_one.astype(jnp.float32), shift_one.astype(jnp.float32)
    )[1]
    d_from_first, grad_gain_one, grad_shift_one = first_back(normalized_gradient)
    grad_current = grad_mid + d_from_first
    local_grads = (
        grad_gain_one,
        grad_shift_one,
        query_key_value_gradient,
        grad_b_query,
        grad_b_value,
        output_weight_gradient,
        grad_b_out,
        grad_gain_two,
        grad_shift_two,
        up_weight_gradient,
        grad_b_up,
        down_weight_gradient,
        grad_b_down,
    )
    return (grad_current, local_grads)


def reduce_grads(local_grads):
    (
        grad_gain_one,
        grad_shift_one,
        query_key_value_gradient,
        grad_b_query,
        grad_b_value,
        output_weight_gradient,
        grad_b_out,
        grad_gain_two,
        grad_shift_two,
        up_weight_gradient,
        grad_b_up,
        down_weight_gradient,
        grad_b_down,
    ) = local_grads
    (
        owned_gain_one,
        owned_shift_one,
        owned_w_qkv,
        owned_b_query,
        owned_b_value,
        owned_w_out,
        owned_b_out,
        owned_gain_two,
        owned_shift_two,
        owned_w_up,
        owned_b_up,
        owned_w_down,
        owned_b_down,
    ) = (
        lax.psum_scatter(grad_gain_one, "shard", scatter_dimension=0, tiled=True),
        lax.psum_scatter(grad_shift_one, "shard", scatter_dimension=0, tiled=True),
        lax.psum_scatter(query_key_value_gradient, "shard", scatter_dimension=0, tiled=True),
        lax.psum_scatter(grad_b_query, "shard", scatter_dimension=0, tiled=True),
        lax.psum_scatter(grad_b_value, "shard", scatter_dimension=0, tiled=True),
        lax.psum_scatter(output_weight_gradient, "shard", scatter_dimension=0, tiled=True),
        lax.psum_scatter(grad_b_out, "shard", scatter_dimension=0, tiled=True),
        lax.psum_scatter(grad_gain_two, "shard", scatter_dimension=0, tiled=True),
        lax.psum_scatter(grad_shift_two, "shard", scatter_dimension=0, tiled=True),
        lax.psum_scatter(up_weight_gradient, "shard", scatter_dimension=0, tiled=True),
        lax.psum_scatter(grad_b_up, "shard", scatter_dimension=0, tiled=True),
        lax.psum_scatter(down_weight_gradient, "shard", scatter_dimension=0, tiled=True),
        lax.psum_scatter(grad_b_down, "shard", scatter_dimension=0, tiled=True),
    )
    return lax.psum(
        (
            owned_gain_one,
            owned_shift_one,
            owned_w_qkv,
            owned_b_query,
            owned_b_value,
            owned_w_out,
            owned_b_out,
            owned_gain_two,
            owned_shift_two,
            owned_w_up,
            owned_b_up,
            owned_w_down,
            owned_b_down,
        ),
        "replica",
    )


def per_device(
    tokens,
    gain_one,
    shift_one,
    query_key_value_weight,
    b_query,
    b_value,
    output_weight,
    output_proj_bias,
    gain_two,
    shift_two,
    up_weight,
    up_bias,
    down_weight,
    down_bias,
    cotangent,
):
    stacked = (
        gain_one,
        shift_one,
        query_key_value_weight,
        b_query,
        b_value,
        output_weight,
        output_proj_bias,
        gain_two,
        shift_two,
        up_weight,
        up_bias,
        down_weight,
        down_bias,
    )
    block_count = gain_one.shape[0]
    local_rows = tokens.shape[1]
    shard_count = lax.axis_size("shard")
    query_place = lax.axis_index("shard") * local_rows + jnp.arange(local_rows, dtype=jnp.int32)
    key_place = jnp.arange(local_rows * shard_count, dtype=jnp.int32)
    causal = query_place[:, None] >= key_place[None, :]
    current = tokens.astype(jnp.float32)
    saved_blocks = []
    for depth_index in range(block_count):
        full = fetch_forward(stacked, depth_index)
        current, saved = forward_block(current, full, causal)
        saved_blocks.append(saved)
    output = current.astype(jnp.bfloat16)
    grad_now = cotangent.astype(jnp.float32)
    block_grads = [None] * block_count
    for depth_index in reversed(range(block_count)):
        full = fetch_again(stacked, depth_index)
        grad_now, local_grads = backward_block(grad_now, full, saved_blocks[depth_index], causal)
        block_grads[depth_index] = reduce_grads(local_grads)
    stacked_grads = tuple(
        (
            jnp.stack([block_grads[depth_index][member] for depth_index in range(block_count)])
            for member in range(13)
        )
    )
    return (output, grad_now) + stacked_grads


def solution(mesh):
    in_specs = (
        P("replica", "shard", None),
        P(None, "shard"),
        P(None, "shard"),
        P(None, "shard", None),
        P(None, "shard"),
        P(None, "shard"),
        P(None, "shard", None),
        P(None, "shard"),
        P(None, "shard"),
        P(None, "shard"),
        P(None, "shard", None),
        P(None, "shard"),
        P(None, "shard", None),
        P(None, "shard"),
        P("replica", "shard", None),
    )
    out_specs = (
        P("replica", "shard", None),
        P("replica", "shard", None),
        P(None, "shard"),
        P(None, "shard"),
        P(None, "shard", None),
        P(None, "shard"),
        P(None, "shard"),
        P(None, "shard", None),
        P(None, "shard"),
        P(None, "shard"),
        P(None, "shard"),
        P(None, "shard", None),
        P(None, "shard"),
        P(None, "shard", None),
        P(None, "shard"),
    )
    return jax.shard_map(
        per_device, mesh=mesh, in_specs=in_specs, out_specs=out_specs, check_vma=False
    )
```

profile of v0, /device:TPU:0, one launch (start us, length us, event | category | flops | bytes accessed | tf_op | source)
XLA Modules:
  0.0 2347.9 jit_solution(6171002777374202452)
XLA Ops:
  34.4 41.0 %all-reduce.37 = (bf16[768]{0:T(1024)(128)(2,1)S(1)}, bf16[768]{0:T(1024)(128)(2,1)S(1)}, bf16[768]{0:T(1024)(128)(2,1)S(1)}, bf16[768]{0:T(1024)(128)(2,1)S(1)}...) all-reduce(bf16[768]{0:T(1024)(128)(2,1)} %dynamic-update-slice.1, ...), channel_id=3, replica_groups=mesh['replica'=4,'shard'=8] {'shard'}, use_global_device_ids=true, to_apply=%add.1 | all-reduce | flops 12288 | bytes 49152
  90.4 26.6 %all-gather.10 = bf16[1,3072]{1,0:T(2,128)(2,1)S(1)} all-gather(bf16[1,384]{1,0:T(2,128)(2,1)S(1)} %get-tuple-element.113), channel_id=12, replica_groups=mesh['replica'=4,'shard'=8] {'shard'}, dimensions={1}, use_global_device_ids=true | all-gather | bytes 6912 | tf_op jit(solution)/shard_map/all_gather | solution.py:46
  117.3 24.7 %all-gather.49.cloned.1.call-done = bf16[2,1024,768]{2,1,0:T(8,128)(2,1)} async-done(((bf16[2,128,768]{2,1,0:T(8,128)(2,1)}), bf16[2,1024,768]{2,1,0:T(8,128)(2,1)}) %all-gather.49.cloned.1.call-update) | async-done | bytes 3145744 | tf_op jit(solution)/shard_map/all_gather | solution.py:129
  146.6 56.9 %all-gather.47.cloned.1.call-done = bf16[2,1024,768]{2,1,0:T(8,128)(2,1)} async-done(((bf16[2,128,768]{2,1,0:T(8,128)(2,1)}), bf16[2,1024,768]{2,1,0:T(8,128)(2,1)}) %all-gather.47.cloned.1.call-update) | async-done | bytes 3145744 | tf_op jit(solution)/shard_map/all_gather | solution.py:130
  221.7 23.7 %all-gather.65.cloned.1.call-done = bf16[1,768,768]{2,1,0:T(8,128)(2,1)} async-done(((bf16[1,96,768]{2,1,0:T(8,128)(2,1)}), bf16[1,768,768]{2,1,0:T(8,128)(2,1)}) %all-gather.65.cloned.1.call-update) | async-done | bytes 1179664 | tf_op jit(solution)/shard_map/all_gather | solution.py:41
  247.5 78.5 %all-gather.67.cloned.1.call-done = bf16[1,768,3072]{2,1,0:T(8,128)(2,1)} async-done(((bf16[1,96,3072]{2,1,0:T(8,128)(2,1)}), bf16[1,768,3072]{2,1,0:T(8,128)(2,1)}) %all-gather.67.cloned.1.call-update) | async-done | bytes 4718608 | tf_op jit(solution)/shard_map/all_gather | solution.py:45
  331.5 74.9 %all-gather.69.cloned.1.call-done = bf16[1,3072,768]{2,1,0:T(8,128)(2,1)} async-done(((bf16[1,384,768]{2,1,0:T(8,128)(2,1)}), bf16[1,3072,768]{2,1,0:T(8,128)(2,1)}) %all-gather.69.cloned.1.call-update) | async-done | bytes 4718608 | tf_op jit(solution)/shard_map/all_gather | solution.py:47
  411.9 60.2 %all-gather.71.cloned.1.call-done = bf16[1,768,2304]{2,1,0:T(8,128)(2,1)} async-done(((bf16[1,96,2304]{2,1,0:T(8,128)(2,1)}), bf16[1,768,2304]{2,1,0:T(8,128)(2,1)}) %all-gather.71.cloned.1.call-update) | async-done | bytes 3538960 | tf_op jit(solution)/shard_map/all_gather | solution.py:38
  481.8 26.4 %all-gather.23 = bf16[1,3072]{1,0:T(2,128)(2,1)S(1)} all-gather(bf16[1,384]{1,0:T(2,128)(2,1)S(1)} %get-tuple-element.112), channel_id=25, replica_groups=mesh['replica'=4,'shard'=8] {'shard'}, dimensions={1}, use_global_device_ids=true | all-gather | bytes 6912 | tf_op jit(solution)/shard_map/all_gather | solution.py:46
  508.9 27.6 %all-gather.53.cloned.1.call-done = bf16[2,1024,768]{2,1,0:T(8,128)(2,1)} async-done(((bf16[2,128,768]{2,1,0:T(8,128)(2,1)}), bf16[2,1024,768]{2,1,0:T(8,128)(2,1)}) %all-gather.53.cloned.1.call-update) | async-done | bytes 3145744 | tf_op jit(solution)/shard_map/all_gather | solution.py:129
  553.3 44.7 %all-gather.51.cloned.1.call-done = bf16[2,1024,768]{2,1,0:T(8,128)(2,1)} async-done(((bf16[2,128,768]{2,1,0:T(8,128)(2,1)}), bf16[2,1024,768]{2,1,0:T(8,128)(2,1)}) %all-gather.51.cloned.1.call-update) | async-done | bytes 3145744 | tf_op jit(solution)/shard_map/all_gather | solution.py:130
  602.6 7.5 fusion.91
  610.1 29.5 %all-gather.73.cloned.1.call-done = bf16[1,768,768]{2,1,0:T(8,128)(2,1)} async-done(((bf16[1,96,768]{2,1,0:T(8,128)(2,1)}), bf16[1,768,768]{2,1,0:T(8,128)(2,1)}) %all-gather.73.cloned.1.call-update) | async-done | bytes 1179664 | tf_op jit(solution)/shard_map/all_gather | solution.py:41
  641.7 78.7 %all-gather.75.cloned.1.call-done = bf16[1,768,3072]{2,1,0:T(8,128)(2,1)} async-done(((bf16[1,96,3072]{2,1,0:T(8,128)(2,1)}), bf16[1,768,3072]{2,1,0:T(8,128)(2,1)}) %all-gather.75.cloned.1.call-update) | async-done | bytes 4718608 | tf_op jit(solution)/shard_map/all_gather | solution.py:45
  720.4 5.5 fusion.45
  726.0 74.8 %all-gather.77.cloned.1.call-done = bf16[1,3072,768]{2,1,0:T(8,128)(2,1)} async-done(((bf16[1,384,768]{2,1,0:T(8,128)(2,1)}), bf16[1,3072,768]{2,1,0:T(8,128)(2,1)}) %all-gather.77.cloned.1.call-update) | async-done | bytes 4718608 | tf_op jit(solution)/shard_map/all_gather | solution.py:47
  800.8 7.5 convert_reduce_fusion
  816.8 31.6 %all-gather.26 = f32[2,12,1024]{2,1,0:T(8,128)S(1)} all-gather(f32[2,12,128]{2,1,0:T(8,128)S(1)} %log_add_fusion.1), channel_id=28, replica_groups=mesh['replica'=4,'shard'=8] {'shard'}, dimensions={2}, use_global_device_ids=true | all-gather | bytes 110592 | tf_op jit(solution)/shard_map/all_gather | solution.py:183
  848.4 10.8 multiply_reduce_fusion.1
  859.2 33.0 %all-gather.27 = f32[2,12,1024]{2,1,0:T(8,128)} all-gather(f32[2,12,128]{2,1,0:T(8,128)S(1)} %get-tuple-element.143), channel_id=29, replica_groups=mesh['replica'=4,'shard'=8] {'shard'}, dimensions={2}, use_global_device_ids=true | all-gather | bytes 110592 | tf_op jit(solution)/shard_map/all_gather | solution.py:184
  892.1 11.6 convert_reduce_fusion.9
  913.5 8.4 fusion.169
  929.5 14.0 fusion.95
  944.7 9.9 convert_reduce_fusion.7
  962.6 6.0 convert_reduce_fusion.1
  981.1 6.6 convolution_bitcast_fusion.2
  987.8 7.7 convolution_bitcast_fusion
  995.7 5.5 convolution_bitcast_fusion.4
  1001.3 6.6 convolution_bitcast_fusion.3
  1007.9 7.7 convolution_bitcast_fusion.1
  1022.9 31.5 %all-gather.28 = f32[2,12,1024]{2,1,0:T(8,128)S(1)} all-gather(f32[2,12,128]{2,1,0:T(8,128)S(1)} %log_add_fusion), channel_id=30, replica_groups=mesh['replica'=4,'shard'=8] {'shard'}, dimensions={2}, use_global_device_ids=true | all-gather | bytes 110592 | tf_op jit(solution)/shard_map/all_gather | solution.py:183
  1054.4 8.4 fusion.170
  1063.0 10.8 multiply_reduce_fusion
  1073.9 11.3 convert_reduce_fusion.10
  1085.4 31.1 %all-gather.29 = f32[2,12,1024]{2,1,0:T(8,128)S(1)} all-gather(f32[2,12,128]{2,1,0:T(8,128)S(1)} %get-tuple-element.147), channel_id=31, replica_groups=mesh['replica'=4,'shard'=8] {'shard'}, dimensions={2}, use_global_device_ids=true | all-gather | bytes 110592 | tf_op jit(solution)/shard_map/all_gather | solution.py:184
  1121.3 12.7 fusion.93
  1134.3 9.0 convert_reduce_fusion.8
  1158.8 35.2 %reduce-scatter.13.cloned.1.call-done = f32[96,768]{1,0:T(8,128)} async-done(((f32[768,768]{1,0:T(8,128)}), f32[96,768]{1,0:T(8,128)}) %reduce-scatter.13.cloned.1.call-update) | async-done | bytes 294928 | tf_op jit(solution)/shard_map/reduce_scatter | solution.py:361
  1194.0 164.9 %reduce-scatter.19.cloned.1.call-done = f32[96,3072]{1,0:T(8,128)} async-done(((f32[768,3072]{1,0:T(8,128)}), f32[96,3072]{1,0:T(8,128)}) %reduce-scatter.19.cloned.1.call-update) | async-done | bytes 1179664 | tf_op jit(solution)/shard_map/reduce_scatter | solution.py:365
  1358.9 164.7 %reduce-scatter.23.cloned.1.call-done = f32[384,768]{1,0:T(8,128)} async-done(((f32[3072,768]{1,0:T(8,128)}), f32[384,768]{1,0:T(8,128)}) %reduce-scatter.23.cloned.1.call-update) | async-done | bytes 1179664 | tf_op jit(solution)/shard_map/reduce_scatter | solution.py:367
  1523.6 132.0 %reduce-scatter.11.cloned.1.call-done = f32[96,2304]{1,0:T(8,128)} async-done(((f32[768,2304]{1,0:T(8,128)}), f32[96,2304]{1,0:T(8,128)}) %reduce-scatter.11.cloned.1.call-update) | async-done | bytes 884752 | tf_op jit(solution)/shard_map/reduce_scatter | solution.py:358
  1655.6 164.8 %reduce-scatter.17.cloned.1.call-done = f32[96,3072]{1,0:T(8,128)} async-done(((f32[768,3072]{1,0:T(8,128)}), f32[96,3072]{1,0:T(8,128)}) %reduce-scatter.17.cloned.1.call-update) | async-done | bytes 1179664 | tf_op jit(solution)/shard_map/reduce_scatter | solution.py:365
  1820.5 164.8 %reduce-scatter.21.cloned.1.call-done = f32[384,768]{1,0:T(8,128)} async-done(((f32[3072,768]{1,0:T(8,128)}), f32[384,768]{1,0:T(8,128)}) %reduce-scatter.21.cloned.1.call-update) | async-done | bytes 1179664 | tf_op jit(solution)/shard_map/reduce_scatter | solution.py:367
  1985.3 131.8 %reduce-scatter.9.cloned.1.call-done = f32[96,2304]{1,0:T(8,128)} async-done(((f32[768,2304]{1,0:T(8,128)}), f32[96,2304]{1,0:T(8,128)}) %reduce-scatter.9.cloned.1.call-update) | async-done | bytes 884752 | tf_op jit(solution)/shard_map/reduce_scatter | solution.py:358
  2117.2 6.1 fusion.88
  2124.5 74.6 %all-reduce.41.cloned.1.call-done = (f32[768]{0:T(1024)}, f32[768]{0:T(1024)}, f32[768]{0:T(1024)}, f32[768]{0:T(1024)}, f32[768]{0:T(1024)}, /*index=5*/f32[768...) async-done(((f32[768]{0:T(1024)}, f32[768]{0:T(1024)}, ...) | async-done | bytes 73744
  2212.7 11.8 all-reduce.35
  2229.6 104.4 %all-reduce.43.cloned.1.call-done = (f32[1,96,2304]{2,1,0:T(8,128)}, f32[1,96,2304]{2,1,0:T(8,128)}, f32[1,96,768]{2,1,0:T(8,128)}, f32[1,96,768]{2,1,0:T(8,128)...) async-done(((f32[1,96,2304]{2,1,0:T(8,128)}, f32[1,96,2304]{2,1,0:T(8,128)}, f32[1,96,768]{2,1,0:T(8,128)}, ...) | async-done | bytes 7077904 | tf_op jit(solution)/shard_map/psum | solution.py:370
  (368 shorter events, 212.6 us)
Async XLA Ops:
  7.2 71.7 %copy-start.2 = (bf16[2,128,768]{2,1,0:T(8,128)(2,1)S(1)}, bf16[2,128,768]{2,1,0:T(8,128)(2,1)}, u32[]{:S(2)}) copy-start(bf16[2,128,768]{2,1,0:T(8,128)(2,1)} %param.15) | copy-start | bytes 1179652
  7.2 71.7 %all-gather.63.cloned.1.call-start = ((), (), s32[]{:S(2)}) async-start(), calls=%async_computation.24 | async-start | bytes 3981312 | tf_op jit(solution)/shard_map/all_gather | solution.py:38
  9.4 132.6 %all-gather.49.cloned.1.call-start = ((), (), s32[]{:S(2)}) async-start(), calls=%async_computation.9 | async-start | bytes 3538944 | tf_op jit(solution)/shard_map/all_gather | solution.py:129
  82.9 120.6 %all-gather.47.cloned.1.call-start = ((), (), s32[]{:S(2)}) async-start(), calls=%async_computation.8 | async-start | bytes 3538944 | tf_op jit(solution)/shard_map/all_gather | solution.py:130
  83.8 33.3 %copy-start.18 = (bf16[2,128,768]{2,1,0:T(8,128)(2,1)}, bf16[2,128,768]{2,1,0:T(8,128)(2,1)S(1)}, u32[]{:S(2)}) copy-start(bf16[2,128,768]{2,1,0:T(8,128)(2,1)S(1)} %get-tuple-element.101) | copy-start | bytes 1179652
  83.9 161.5 %all-gather.65.cloned.1.call-start = ((), (), s32[]{:S(2)}) async-start(), calls=%async_computation.25 | async-start | bytes 1327104 | tf_op jit(solution)/shard_map/all_gather | solution.py:41
  85.8 240.2 %all-gather.67.cloned.1.call-start = ((), (), s32[]{:S(2)}) async-start(), calls=%async_computation.26 | async-start | bytes 5308416 | tf_op jit(solution)/shard_map/all_gather | solution.py:45
  88.2 318.1 %all-gather.69.cloned.1.call-start = ((), (), s32[]{:S(2)}) async-start(), calls=%async_computation.27 | async-start | bytes 5308416 | tf_op jit(solution)/shard_map/all_gather | solution.py:47
  89.4 382.7 %all-gather.71.cloned.1.call-start = ((), (), s32[]{:S(2)}) async-start(), calls=%async_computation.28 | async-start | bytes 3981312 | tf_op jit(solution)/shard_map/all_gather | solution.py:38
  90.2 446.3 %all-gather.53.cloned.1.call-start = ((), (), s32[]{:S(2)}) async-start(), calls=%async_computation.11 | async-start | bytes 3538944 | tf_op jit(solution)/shard_map/all_gather | solution.py:129
  221.7 109.8 %copy-start.29 = (bf16[2,12,64,128]{3,2,1,0:T(8,128)(2,1)}, bf16[2,12,64,128]{3,2,1,0:T(8,128)(2,1)S(1)}, u32[]{:S(2)}) copy-start(bf16[2,12,64,128]{3,2,1,0:T(8,128)(2,1)S(1)} %fusion.92) | copy-start | bytes 1179652
  477.5 120.5 %all-gather.51.cloned.1.call-start = ((), (), s32[]{:S(2)}) async-start(), calls=%async_computation.10 | async-start | bytes 3538944 | tf_op jit(solution)/shard_map/all_gather | solution.py:130
  479.8 28.6 %copy-start.19 = (bf16[2,128,768]{2,1,0:T(8,128)(2,1)}, bf16[2,128,768]{2,1,0:T(8,128)(2,1)S(1)}, u32[]{:S(2)}) copy-start(bf16[2,128,768]{2,1,0:T(8,128)(2,1)S(1)} %get-tuple-element.99) | copy-start | bytes 1179652
  479.8 159.8 %all-gather.73.cloned.1.call-start = ((), (), s32[]{:S(2)}) async-start(), calls=%async_computation.29 | async-start | bytes 1327104 | tf_op jit(solution)/shard_map/all_gather | solution.py:41
  480.4 240.1 %all-gather.75.cloned.1.call-start = ((), (), s32[]{:S(2)}) async-start(), calls=%async_computation.30 | async-start | bytes 5308416 | tf_op jit(solution)/shard_map/all_gather | solution.py:45
  481.1 319.7 %all-gather.77.cloned.1.call-start = ((), (), s32[]{:S(2)}) async-start(), calls=%async_computation.31 | async-start | bytes 5308416 | tf_op jit(solution)/shard_map/all_gather | solution.py:47
  481.7 427.1 %all-gather.55.cloned.1.call-start = ((), (), s32[]{:S(2)}) async-start(), calls=%async_computation.12 | async-start | bytes 3538944 | tf_op jit(solution)/shard_map/all_gather | solution.py:187
  508.4 416.4 %all-gather.57.cloned.1.call-start = ((), (), s32[]{:S(2)}) async-start(), calls=%async_computation.13 | async-start | bytes 3538944 | tf_op jit(solution)/shard_map/all_gather | solution.py:188
  610.1 110.3 %copy-start.30 = (bf16[2,12,64,128]{3,2,1,0:T(8,128)(2,1)}, bf16[2,12,64,128]{3,2,1,0:T(8,128)(2,1)S(1)}, u32[]{:S(2)}) copy-start(bf16[2,12,64,128]{3,2,1,0:T(8,128)(2,1)S(1)} %fusion.91) | copy-start | bytes 1179652
  720.4 80.3 %copy-start.16 = (bf16[2,128,768]{2,1,0:T(8,128)(2,1)S(1)}, bf16[2,128,768]{2,1,0:T(8,128)(2,1)}, u32[]{:S(2)}) copy-start(bf16[2,128,768]{2,1,0:T(8,128)(2,1)} %param.29) | copy-start | bytes 1179652
  800.8 7.5 copy-start.13
  814.5 203.7 %all-gather.59.cloned.1.call-start = ((), (), s32[]{:S(2)}) async-start(), calls=%async_computation.14 | async-start | bytes 3538944 | tf_op jit(solution)/shard_map/all_gather | solution.py:187
  815.3 301.2 %all-gather.61.cloned.1.call-start = ((), (), s32[]{:S(2)}) async-start(), calls=%async_computation.15 | async-start | bytes 3538944 | tf_op jit(solution)/shard_map/all_gather | solution.py:188
  848.4 43.8 %copy-start.6 = (bf16[2,1024,768]{1,2,0:T(8,128)(2,1)S(1)}, bf16[2,1024,768]{1,2,0:T(8,128)(2,1)}, u32[]{:S(2)}) copy-start(bf16[2,1024,768]{1,2,0:T(8,128)(2,1)} %copy.98) | copy-start | bytes 9437188
  903.9 52.7 %copy-start.25 = (bf16[2,128,768]{2,1,0:T(8,128)(2,1)}, bf16[2,128,768]{2,1,0:T(8,128)(2,1)S(1)}, u32[]{:S(2)}) copy-start(bf16[2,128,768]{2,1,0:T(8,128)(2,1)S(1)} %copy.105) | copy-start | bytes 1179652
  921.9 7.6 copy-start.44
  944.7 11.9 copy-start.26
  960.7 8.0 slice-start
  974.9 183.8 %reduce-scatter.15.cloned.1.call-start = ((), (), s32[]{:S(2)}) async-start(), calls=%async_computation.19 | async-start | bytes 2654208 | tf_op jit(solution)/shard_map/reduce_scatter | solution.py:361
  978.0 216.0 %reduce-scatter.13.cloned.1.call-start = ((), (), s32[]{:S(2)}) async-start(), calls=%async_computation.18 | async-start | bytes 2654208 | tf_op jit(solution)/shard_map/reduce_scatter | solution.py:361
  981.0 377.9 %reduce-scatter.19.cloned.1.call-start = ((), (), s32[]{:S(2)}) async-start(), calls=%async_computation.21 | async-start | bytes 10616832 | tf_op jit(solution)/shard_map/reduce_scatter | solution.py:365
  987.8 535.8 %reduce-scatter.23.cloned.1.call-start = ((), (), s32[]{:S(2)}) async-start(), calls=%async_computation.23 | async-start | bytes 10616832 | tf_op jit(solution)/shard_map/reduce_scatter | solution.py:367
  995.5 660.1 %reduce-scatter.11.cloned.1.call-start = ((), (), s32[]{:S(2)}) async-start(), calls=%async_computation.17 | async-start | bytes 7962624 | tf_op jit(solution)/shard_map/reduce_scatter | solution.py:358
  1001.3 819.2 %reduce-scatter.17.cloned.1.call-start = ((), (), s32[]{:S(2)}) async-start(), calls=%async_computation.20 | async-start | bytes 10616832 | tf_op jit(solution)/shard_map/reduce_scatter | solution.py:365
  1007.9 977.4 %reduce-scatter.21.cloned.1.call-start = ((), (), s32[]{:S(2)}) async-start(), calls=%async_computation.22 | async-start | bytes 10616832 | tf_op jit(solution)/shard_map/reduce_scatter | solution.py:367
  1015.7 1101.5 %reduce-scatter.9.cloned.1.call-start = ((), (), s32[]{:S(2)}) async-start(), calls=%async_computation.16 | async-start | bytes 7962624 | tf_op jit(solution)/shard_map/reduce_scatter | solution.py:358
  1054.4 8.4 copy-start.21
  1063.0 10.9 copy-start.5
  1134.2 10.2 copy-start.27
  1134.2 10.2 copy-start.3
  1134.2 10.2 copy-start.40
  1134.3 10.2 copy-start.42
  1134.3 10.2 copy-start.49
  1134.3 10.2 copy-start.51
  1148.7 1050.5 %all-reduce.41.cloned.1.call-start = ((), (), s32[]{:S(2)}) async-start(), calls=%async_computation.32 | async-start | bytes 180224
  1152.0 6.7 copy-start.60
  1156.1 961.0 %copy-start.23 = (f32[2,128,768]{2,1,0:T(8,128)}, f32[2,128,768]{2,1,0:T(8,128)S(1)}, u32[]{:S(2)}) copy-start(f32[2,128,768]{2,1,0:T(8,128)S(1)} %get-tuple-element.149) | copy-start | bytes 2359300
  1157.1 1176.9 %all-reduce.43.cloned.1.call-start = ((), (), s32[]{:S(2)}) async-start(), calls=%async_computation.33 | async-start | bytes 14155776 | tf_op jit(solution)/shard_map/psum | solution.py:370
  (41 other events, 146.1 us)
Sparse Core Ops, SparseCore 0:
  10.8 68.0 all-gather.62
  83.0 58.9 all-gather.48
  144.8 58.6 all-gather.46
  205.5 39.7 all-gather.64
  248.0 77.9 all-gather.66
  328.6 77.6 all-gather.68
  409.1 62.9 all-gather.70
  477.6 58.8 all-gather.52
  539.2 58.6 all-gather.50
  600.0 39.6 all-gather.72
  642.4 77.9 all-gather.74
  723.1 77.6 all-gather.76
  803.5 59.6 all-gather.54
  865.9 58.9 all-gather.56
  926.9 58.6 all-gather.58
  988.2 60.2 all-gather.60
  1052.4 68.7 reduce-scatter.14
  1125.2 68.7 reduce-scatter.12
  1197.6 161.2 reduce-scatter.18
  1362.4 161.2 reduce-scatter.22
  1527.3 128.2 reduce-scatter.10
  1659.2 161.2 reduce-scatter.16
  1824.1 161.1 reduce-scatter.20
  1988.8 128.2 reduce-scatter.8
  2123.4 75.6 all-reduce.40
  2201.8 132.1 all-reduce.42
where the time goes:
time: 2360 us; the launch traced here: 2350 us
  waiting for transfers between devices  1720 us (73%)
  blocking collectives  233 us (10%)
  matrix products  232 us (10%)
  local copies, waits for them, and re-layouts  114 us (5%)
  other arithmetic  32.6 us (1%)
    reduce_scatter x2, waiting for transfers between devices, reduce_grads(): lax.psum_scatter(up_weight_gradient, 'shard', scatter_dimension=0, tiled=...  330 us
    reduce_scatter x2, waiting for transfers between devices, reduce_grads(): lax.psum_scatter(down_weight_gradient, 'shard', scatter_dimension=0, tile...  330 us
    reduce_scatter x2, waiting for transfers between devices, reduce_grads(): lax.psum_scatter(query_key_value_gradient, 'shard', scatter_dimension=0,...  264 us
    all_gather x2, waiting for transfers between devices, fetch_forward(): lax.all_gather(up_weight, 'shard', axis=0, tiled=True)  157 us
    all_gather x2, waiting for transfers between devices, fetch_forward(): lax.all_gather(down_weight, 'shard', axis=0, tiled=True)  150 us
    psum x1, waiting for transfers between devices, reduce_grads(): lax.psum((owned_gain_one, owned_shift_one, owned_w_qkv, owned_b_query, ow...  104 us
    all_gather x2, waiting for transfers between devices, forward_block(): lax.all_gather(value_part, 'shard', axis=1, tiled=True)  102 us
    unnamed x27, waiting for transfers between devices  77.4 us
  transfers between devices with their start and end apart: 26, of which 22 were waited for; matrix products, arithmetic and copies ran while one was open for 15% of the time, Pallas kernels for 0%

commit v1 on v0

v1 whole, which is shorter than its diff:
```python
import functools

import jax
import jax.numpy as jnp
from jax import lax
from jax.experimental import pallas as pl
from jax.experimental.pallas import tpu as pltpu
from jax.sharding import PartitionSpec as P

HEADS = 12
HEAD_DIM = 64
EPSILON = 1e-05
MASKED = -1e30
F32 = jnp.float32
BF16 = jnp.bfloat16
BOTH = ("replica", "shard")
QUERY_ROWS = 256


def dot(a, b, contract):
    return lax.dot_general(a, b, (contract, ((), ())), preferred_element_type=F32)


def norm_rows(values, gain, shift):
    centre = values - jnp.mean(values, -1, keepdims=True)
    spread = jnp.mean(centre * centre, -1, keepdims=True)
    return centre * lax.rsqrt(spread + EPSILON) * gain + shift


def block_probs(q_ref, k_ref, head, first, rows):
    count = first + rows
    query = q_ref[head, first:count, :]
    keys = k_ref[head, 0:count, :]
    scores = dot(query, keys, ((1,), (1,))) * (HEAD_DIM**-0.5)
    row = lax.broadcasted_iota(jnp.int32, (rows, count), 0) + first
    col = lax.broadcasted_iota(jnp.int32, (rows, count), 1)
    scores = jnp.where(row >= col, scores, MASKED)
    expo = jnp.exp(scores - jnp.max(scores, -1, keepdims=True))
    return expo / jnp.sum(expo, -1, keepdims=True), query, keys


def split_heads(source, places):
    for place, target in enumerate(places):
        heads = target.shape[0]
        for head in range(heads):
            start = (place * heads + head) * HEAD_DIM
            target[head] = source[:, start : start + HEAD_DIM]


def attend_kernel(mixed_ref, out_ref, q_ref, k_ref, v_ref, o_ref):
    heads, length, _ = q_ref.shape
    rows = min(QUERY_ROWS, length)
    split_heads(mixed_ref, (q_ref, k_ref, v_ref))

    @pl.loop(0, heads)
    def _(head):
        for first in range(0, length, rows):
            probs, _, _ = block_probs(q_ref, k_ref, head, first, rows)
            o_ref[head, first : first + rows, :] = dot(
                probs.astype(BF16), v_ref[head, 0 : first + rows, :], ((1,), (0,))
            ).astype(BF16)

    for head in range(heads):
        out_ref[:, head * HEAD_DIM : (head + 1) * HEAD_DIM] = o_ref[head]


def attend(mixed, heads):
    length = mixed.shape[0]
    part = pltpu.VMEM((heads, length, HEAD_DIM), BF16)
    return pl.pallas_call(
        attend_kernel,
        out_shape=jax.ShapeDtypeStruct((length, heads * HEAD_DIM), BF16),
        in_specs=[pl.BlockSpec(memory_space=pltpu.VMEM)],
        out_specs=pl.BlockSpec(memory_space=pltpu.VMEM),
        scratch_shapes=[part, part, part, part],
        name="attend",
    )(mixed)


def attend_back_kernel(
    mixed_ref, d_ref, out_ref, q_ref, k_ref, v_ref, do_ref, dq_ref, dk_ref, dv_ref
):
    heads, length, _ = q_ref.shape
    rows = min(QUERY_ROWS, length)
    split_heads(mixed_ref, (q_ref, k_ref, v_ref))
    split_heads(d_ref, (do_ref,))

    @pl.loop(0, heads)
    def _(head):
        dk_ref[head] = jnp.zeros((length, HEAD_DIM), F32)
        dv_ref[head] = jnp.zeros((length, HEAD_DIM), F32)
        for first in range(0, length, rows):
            count = first + rows
            probs, query, keys = block_probs(q_ref, k_ref, head, first, rows)
            d_out = do_ref[head, first:count, :]
            d_probs = dot(d_out, v_ref[head, 0:count, :], ((1,), (1,)))
            row_dot = jnp.sum(d_probs * probs, -1, keepdims=True)
            d_scores = (probs * (d_probs - row_dot) * (HEAD_DIM**-0.5)).astype(BF16)
            dq_ref[head, first:count, :] = dot(d_scores, keys, ((1,), (0,))).astype(BF16)
            dk_ref[head, 0:count, :] += dot(d_scores, query, ((0,), (0,)))
            dv_ref[head, 0:count, :] += dot(probs.astype(BF16), d_out, ((0,), (0,)))

    for head in range(heads):
        for place, part in enumerate((dq_ref, dk_ref, dv_ref)):
            start = (place * heads + head) * HEAD_DIM
            out_ref[:, start : start + HEAD_DIM] = part[head].astype(BF16)


def attend_back(mixed, d_attended, heads):
    length = mixed.shape[0]
    part = pltpu.VMEM((heads, length, HEAD_DIM), BF16)
    wide = pltpu.VMEM((heads, length, HEAD_DIM), F32)
    return pl.pallas_call(
        attend_back_kernel,
        out_shape=jax.ShapeDtypeStruct((length, 3 * heads * HEAD_DIM), BF16),
        in_specs=[pl.BlockSpec(memory_space=pltpu.VMEM)] * 2,
        out_specs=pl.BlockSpec(memory_space=pltpu.VMEM),
        scratch_shapes=[part, part, part, part, part, wide, wide],
        name="attend_back",
    )(mixed, d_attended)


class Place:
    def __init__(self, tokens):
        self.replicas = lax.axis_size("replica")
        self.shards = lax.axis_size("shard")
        self.r = lax.axis_index("replica")
        self.s = lax.axis_index("shard")
        self.held, self.rows, self.width = tokens.shape
        self.heads = -(-HEADS // self.replicas)
        self.padded = self.heads * self.replicas
        assert self.held * self.replicas == self.shards

    def to_sequences(self, blocks):
        held = self.held
        got = []
        for turn in range(held):
            pairs = []
            for r in range(self.replicas):
                for s in range(self.shards):
                    pick = (s + turn) % held
                    target = (s // held) * self.shards + held * r + pick
                    pairs.append((r * self.shards + s, target))
            block = lax.dynamic_index_in_dim(blocks, (self.s + turn) % held, 0, keepdims=False)
            got.append(lax.ppermute(block, BOTH, pairs))
        stacked = jnp.stack(got)
        ordered = [
            lax.dynamic_index_in_dim(stacked, (self.s - u) % held, 0, keepdims=False)
            for u in range(held)
        ]
        return jnp.concatenate(ordered, 0)

    def from_sequences(self, values):
        held, rows = self.held, self.rows
        blocks = values.reshape(held, rows, values.shape[-1])
        got = []
        for turn in range(held):
            pairs = []
            for r in range(self.replicas):
                for s in range(self.shards):
                    pick = (s + turn) % held
                    target = (s // held) * self.shards + held * r + pick
                    pairs.append((target, r * self.shards + s))
            block = lax.dynamic_index_in_dim(blocks, (self.s - turn) % held, 0, keepdims=False)
            got.append(lax.ppermute(block, BOTH, pairs))
        stacked = jnp.stack(got)
        return jnp.stack(
            [
                lax.dynamic_index_in_dim(stacked, (i - self.s) % held, 0, keepdims=False)
                for i in range(held)
            ]
        )

    def to_heads(self, values):
        return lax.all_to_all(values, "replica", 1, 0, tiled=True)

    def to_rows(self, values):
        return lax.all_to_all(values, "replica", 0, 1, tiled=True)

    def mix_columns(self, weight):
        lead = weight.shape[:-1]
        parts = weight.reshape(lead + (3, HEADS, HEAD_DIM))
        extra = [(0, 0)] * len(lead) + [(0, 0), (0, self.padded - HEADS), (0, 0)]
        parts = jnp.pad(parts, extra)
        parts = parts.reshape(lead + (3, self.replicas, self.heads * HEAD_DIM))
        return jnp.swapaxes(parts, -3, -2).reshape(lead + (-1,))

    def unmix_columns(self, values):
        lead = values.shape[:-1]
        parts = values.reshape(lead + (self.replicas, 3, self.heads * HEAD_DIM))
        parts = jnp.swapaxes(parts, -3, -2).reshape(lead + (3, self.padded, HEAD_DIM))
        return parts[..., :HEADS, :].reshape(lead + (-1,))


def gather_vectors(place, vectors):
    layers = vectors[0].shape[0]
    packed = jnp.concatenate(vectors, -1)
    whole = lax.all_gather(packed, "shard", axis=0)
    out, start = [], 0
    for vector in vectors:
        size = vector.shape[1]
        piece = whole[:, :, start : start + size]
        out.append(jnp.swapaxes(piece, 0, 1).reshape(layers, -1).astype(F32))
        start += size
    return out


def gather_weights(place, mix, out_w, up, down):
    full = [
        [lax.all_gather(w[layer], "shard", axis=0, tiled=True) for w in (mix, out_w, up, down)]
        for layer in range(mix.shape[0])
    ]
    return full


def reduce_weights(place, grads):
    return [
        lax.psum(
            lax.psum_scatter(g, "shard", scatter_dimension=0, tiled=True).astype(F32), "replica"
        )
        for g in grads
    ]


def forward_block(place, current, weights, vectors):
    mix, out_w, up, down = weights
    gain_one, shift_one, mix_bias, out_bias, gain_two, shift_two, up_bias, down_bias = vectors
    normed = norm_rows(current, gain_one, shift_one).astype(BF16)
    mixed = (dot(normed, mix, ((1,), (0,))) + mix_bias).astype(BF16)
    mixed = place.to_heads(mixed)
    attended = place.to_rows(attend(mixed, place.heads))[:, : place.width]
    x_mid = current + (dot(attended, out_w, ((1,), (0,))) + out_bias)
    moved = norm_rows(x_mid, gain_two, shift_two).astype(BF16)
    pre = dot(moved, up, ((1,), (0,))) + up_bias
    act = jax.nn.gelu(pre, approximate=True).astype(BF16)
    result = x_mid + dot(act, down, ((1,), (0,))) + down_bias
    return result, (current, normed, mixed, attended, x_mid, moved, pre, act)


def backward_block(place, grad_next, weights, vectors, saved):
    mix, out_w, up, down = weights
    gain_one, shift_one, mix_bias, out_bias, gain_two, shift_two, up_bias, down_bias = vectors
    current, normed, mixed, attended, x_mid, moved, pre, act = saved
    d_ffn = grad_next.astype(BF16)
    grad_down = dot(act, d_ffn, ((0,), (0,))).astype(BF16)
    grad_b_down = jnp.sum(d_ffn.astype(F32), 0)
    d_act = dot(d_ffn, down, ((1,), (1,)))
    gelu_back = jax.vjp(lambda inner: jax.nn.gelu(inner, approximate=True), pre)[1]
    d_pre = gelu_back(d_act)[0].astype(BF16)
    grad_up = dot(moved, d_pre, ((0,), (0,))).astype(BF16)
    grad_b_up = jnp.sum(d_pre.astype(F32), 0)
    d_moved = dot(d_pre, up, ((1,), (1,)))
    norm_back = jax.vjp(norm_rows, x_mid, gain_two, shift_two)[1]
    d_from_norm, grad_gain_two, grad_shift_two = norm_back(d_moved)
    grad_mid = grad_next + d_from_norm
    d_branch = grad_mid.astype(BF16)
    grad_out = dot(attended, d_branch, ((0,), (0,))).astype(BF16)
    grad_b_out = jnp.sum(d_branch.astype(F32), 0)
    d_att = dot(d_branch, out_w, ((1,), (1,))).astype(BF16)
    d_att = jnp.pad(d_att, ((0, 0), (0, place.padded * HEAD_DIM - place.width)))
    d_mixed = place.to_rows(attend_back(mixed, place.to_heads(d_att), place.heads))
    grad_mix = dot(normed, d_mixed, ((0,), (0,))).astype(BF16)
    grad_b_mix = place.unmix_columns(jnp.sum(d_mixed.astype(F32), 0))
    grad_b_query = grad_b_mix[: place.width]
    grad_b_value = grad_b_mix[2 * place.width :]
    d_normed = dot(d_mixed, mix, ((1,), (1,)))
    first_back = jax.vjp(norm_rows, current, gain_one, shift_one)[1]
    d_from_first, grad_gain_one, grad_shift_one = first_back(d_normed)
    grad_current = grad_mid + d_from_first
    grad_vectors = (
        grad_gain_one,
        grad_shift_one,
        grad_b_query,
        grad_b_value,
        grad_b_out,
        grad_gain_two,
        grad_shift_two,
        grad_b_up,
        grad_b_down,
    )
    return grad_current, (grad_mix, grad_out, grad_up, grad_down), grad_vectors


def per_device(
    tokens,
    gain_one,
    shift_one,
    query_key_value_weight,
    b_query,
    b_value,
    output_weight,
    output_proj_bias,
    gain_two,
    shift_two,
    up_weight,
    up_bias,
    down_weight,
    down_bias,
    cotangent,
):
    place = Place(tokens)
    layers = gain_one.shape[0]
    mix_weight = place.mix_columns(query_key_value_weight)
    vectors = gather_vectors(
        place,
        (
            gain_one,
            shift_one,
            b_query,
            b_value,
            output_proj_bias,
            gain_two,
            shift_two,
            up_bias,
            down_bias,
        ),
    )
    g1, s1, bq, bv, bo, g2, s2, bu, bd = vectors
    mix_bias = place.mix_columns(jnp.concatenate([bq, jnp.zeros_like(bq), bv], -1))
    weights = gather_weights(place, mix_weight, output_weight, up_weight, down_weight)

    def layer_vectors(n):
        return (g1[n], s1[n], mix_bias[n], bo[n], g2[n], s2[n], bu[n], bd[n])

    current = place.to_sequences(tokens).astype(F32)
    saved = []
    for n in range(layers):
        current, kept = forward_block(place, current, weights[n], layer_vectors(n))
        saved.append(kept)
    output = place.from_sequences(current.astype(BF16))
    grad_now = place.to_sequences(cotangent).astype(F32)
    weight_grads, vector_grads = [None] * layers, [None] * layers
    for n in reversed(range(layers)):
        grad_now, local, vector_grads[n] = backward_block(
            place, grad_now, weights[n], layer_vectors(n), saved[n]
        )
        weight_grads[n] = reduce_weights(place, local)
    grad_tokens = place.from_sequences(grad_now.astype(BF16)).astype(F32)
    grad_mix, grad_out, grad_up, grad_down = (
        jnp.stack([weight_grads[n][m] for n in range(layers)]) for m in range(4)
    )
    grad_mix = place.unmix_columns(grad_mix)
    sizes = [v.shape[0] for v in vector_grads[0]]
    packed = jnp.stack([jnp.concatenate(v) for v in vector_grads])
    packed = lax.psum(packed, BOTH)
    own, start = [], 0
    for size in sizes:
        part = size // place.shards
        own.append(lax.dynamic_slice_in_dim(packed, start + place.s * part, part, 1))
        start += size
    (
        grad_gain_one,
        grad_shift_one,
        grad_b_query,
        grad_b_value,
        grad_b_out,
        grad_gain_two,
        grad_shift_two,
        grad_b_up,
        grad_b_down,
    ) = own
    return (
        output,
        grad_tokens,
        grad_gain_one,
        grad_shift_one,
        grad_mix,
        grad_b_query,
        grad_b_value,
        grad_out,
        grad_b_out,
        grad_gain_two,
        grad_shift_two,
        grad_up,
        grad_b_up,
        grad_down,
        grad_b_down,
    )


def solution(mesh):
    vector, matrix = P(None, "shard"), P(None, "shard", None)
    rows = P("replica", "shard", None)
    in_specs = (
        rows,
        vector,
        vector,
        matrix,
        vector,
        vector,
        matrix,
        vector,
        vector,
        vector,
        matrix,
        vector,
        matrix,
        vector,
        rows,
    )
    out_specs = (
        rows,
        rows,
        vector,
        vector,
        matrix,
        vector,
        vector,
        matrix,
        vector,
        vector,
        vector,
        matrix,
        vector,
        matrix,
        vector,
    )
    return jax.shard_map(
        per_device, mesh=mesh, in_specs=in_specs, out_specs=out_specs, check_vma=False
    )
```

time: 2360 us -> 1630 us (0.69)
  waiting for transfers between devices: 1720 us -> 1250 us
  blocking collectives: 233 us -> 93.5 us
  matrix products: 232 us -> 95.2 us
  local copies, waits for them, and re-layouts: 114 us -> 65 us
  Pallas kernels: 0 us -> 48.4 us
  starting transfers between devices: 2.07 us -> 28.1 us
    reduce_scatter x8, waiting for transfers between devices: 958 us -> 549 us  [reduce_weights(): lax.psum_scatter(g, 'shard', scatter_dimension=0, tiled=True).astype(F32)]
    all_gather x16 -> x8, waiting for transfers between devices: 577 us -> 377 us  [gather_weights(): lax.all_gather(w[layer], 'shard', axis=0, tiled=True)]
    psum x1 -> x2, waiting for transfers between devices: 104 us -> 270 us  [the longest x1 143 us: reduce_weights(): lax.psum(lax.psum_scatter(g, 'shard', scatter_dimension=0, tiled=True).as...]
    dot_general x38 -> x24, matrix products: 232 us -> 95.2 us  [dot(): lax.dot_general(a, b, (contract, ((), ())), preferred_element_type=F32)]
    all_gather x6 -> x1, blocking collectives: 180 us -> 52.8 us  [gather_vectors(): whole = lax.all_gather(packed, 'shard', axis=0)]
    unnamed x27 -> x18, waiting for transfers between devices: 77.4 us -> 1.48 us
    all_to_all x0 -> x5, waiting for transfers between devices: none -> 51.3 us  [the longest x2 30.2 us: to_heads(): return lax.all_to_all(values, 'replica', 1, 0, tiled=True)]
    pallas_call x0 -> x4, Pallas kernels: none -> 48.4 us  [the longest x2 28.8 us: attend_back(): pl.pallas_call(attend_back_kernel, out_shape=jax.ShapeDtypeStruct((length...]
  transfers between devices with their start and end apart: 26 -> 31, of which waited for: 22 -> 21; matrix products, arithmetic and copies ran while one was open for 15% -> 9% of each run, Pallas kernels for 0% -> 2%
where the time goes in v1:
time: 1630 us; the launch traced here: 1620 us
  waiting for transfers between devices  1250 us (77%)
  matrix products  95.2 us (6%)
  blocking collectives  93.5 us (6%)
  local copies, waits for them, and re-layouts  65 us (4%)
  Pallas kernels  48.4 us (3%)
  other arithmetic  28.4 us (2%)
  starting transfers between devices  28.1 us (2%)
    reduce_scatter x8, waiting for transfers between devices, reduce_weights(): lax.psum_scatter(g, 'shard', scatter_dimension=0, tiled=True).astype(F32)  549 us
    all_gather x8, waiting for transfers between devices, gather_weights(): lax.all_gather(w[layer], 'shard', axis=0, tiled=True)  377 us
    psum x1, waiting for transfers between devices, reduce_weights(): lax.psum(lax.psum_scatter(g, 'shard', scatter_dimension=0, tiled=True).as...  143 us
    psum x1, waiting for transfers between devices, per_device(): packed = lax.psum(packed, BOTH)  126 us
    dot_general x24, matrix products, dot(): lax.dot_general(a, b, (contract, ((), ())), preferred_element_type=F32)  95.2 us
    all_gather x1, blocking collectives, gather_vectors(): whole = lax.all_gather(packed, 'shard', axis=0)  52.8 us
  transfers between devices with their start and end apart: 31, of which 21 were waited for; matrix products, arithmetic and copies ran while one was open for 9% of the time, Pallas kernels for 2%

profile of v1, /device:TPU:0, one launch (start us, length us, event | category | flops | bytes accessed | tf_op | source)
XLA Modules:
  0.0 1623.2 jit_solution(3986108142512245051)
XLA Ops:
  23.1 52.8 %all-gather.7 = bf16[8,2,1152]{2,1,0:T(2,128)(2,1)S(1)} all-gather(bf16[1,2,1152]{2,1,0:T(2,128)(2,1)S(1)} %bitcast.243), channel_id=2, replica_groups=mesh['replica'=4,'shard'=8] {'shard'}, dimensions={0}, use_global_device_ids=true | all-gather | bytes 41472 | tf_op jit(solution)/shard_map/all_gather | solution.py:198
  77.2 18.2 %all-gather.17.cloned.1.call-done = bf16[768,2304]{1,0:T(8,128)(2,1)} async-done(((bf16[96,2304]{1,0:T(8,128)(2,1)}), bf16[768,2304]{1,0:T(8,128)(2,1)}) %all-gather.17.cloned.1.call-update) | async-done | bytes 3538960 | tf_op jit(solution)/shard_map/all_gather | solution.py:210
  95.5 3.2 fusion.22
  100.1 3.5 all-to-all-start
  106.0 13.5 all-to-all-done
  120.9 9.8 attend.2
  132.7 3.7 all-to-all-start.1
  137.7 6.1 all-to-all-done.1
  146.0 72.1 %all-gather.23.cloned.1.call-done = bf16[1,768,3072]{2,1,0:T(8,128)(2,1)} async-done(((bf16[1,96,3072]{2,1,0:T(8,128)(2,1)}), bf16[1,768,3072]{2,1,0:T(8,128)(2,1)}) %all-gather.23.cloned.1.call-update) | async-done | bytes 4718608 | tf_op jit(solution)/shard_map/all_gather | solution.py:210
  218.1 5.4 fusion.16
  223.6 74.9 %all-gather.25.cloned.1.call-done = bf16[1,3072,768]{2,1,0:T(8,128)(2,1)} async-done(((bf16[1,384,768]{2,1,0:T(8,128)(2,1)}), bf16[1,3072,768]{2,1,0:T(8,128)(2,1)}) %all-gather.25.cloned.1.call-update) | async-done | bytes 4718608 | tf_op jit(solution)/shard_map/all_gather | solution.py:210
  298.4 5.3 fusion.110
  304.0 59.4 %all-gather.19.cloned.1.call-done = bf16[768,2304]{1,0:T(8,128)(2,1)} async-done(((bf16[96,2304]{1,0:T(8,128)(2,1)}), bf16[768,2304]{1,0:T(8,128)(2,1)}) %all-gather.19.cloned.1.call-update) | async-done | bytes 3538960 | tf_op jit(solution)/shard_map/all_gather | solution.py:210
  363.5 3.2 fusion.23
  368.1 3.5 all-to-all-start.2
  373.6 16.8 %all-to-all-done.2 = bf16[256,4,576]{0,2,1:T(8,128)(2,1)S(1)} async-done(((bf16[256,4,576]{0,2,1:T(8,128)(2,1)}), bf16[256,4,576]{0,2,1:T(8,128)(2,1)S(1)}, u32[]{:S(2)}, u32[]{:S(2)}) %all-to-all-start.2) | async-done | bytes 1179680 | tf_op jit(solution)/shard_map/all_to_all | solution.py:175
  391.8 9.8 attend.3
  403.6 4.1 all-to-all-start.3
  417.3 75.8 %all-gather.29.cloned.1.call-done = bf16[1,768,3072]{2,1,0:T(8,128)(2,1)} async-done(((bf16[1,96,3072]{2,1,0:T(8,128)(2,1)}), bf16[1,768,3072]{2,1,0:T(8,128)(2,1)}) %all-gather.29.cloned.1.call-update) | async-done | bytes 4718608 | tf_op jit(solution)/shard_map/all_gather | solution.py:210
  493.1 5.6 fusion.19
  498.7 74.9 %all-gather.31.cloned.1.call-done = bf16[1,3072,768]{2,1,0:T(8,128)(2,1)} async-done(((bf16[1,384,768]{2,1,0:T(8,128)(2,1)}), bf16[1,3072,768]{2,1,0:T(8,128)(2,1)}) %all-gather.31.cloned.1.call-update) | async-done | bytes 4718608 | tf_op jit(solution)/shard_map/all_gather | solution.py:210
  573.6 7.6 convert_reduce_fusion
  587.9 11.6 all_to_all.152
  601.5 14.4 attend_back.2
  618.3 3.5 all-to-all-start.5
  624.8 12.8 all-to-all-done.5
  637.7 4.1 multiply_reduce_fusion.1
  643.6 6.4 convert_reduce_fusion.1
  655.2 3.1 convolution_convert_fusion.4
  659.3 6.3 convolution_convert_fusion
  666.3 5.2 convolution_convert_fusion.2
  673.6 9.8 all_to_all.153
  684.4 14.4 attend_back.3
  701.2 19.3 %all_to_all.154 = bf16[4,256,576]{1,2,0:T(8,128)(2,1)S(1)} all-to-all(bf16[4,256,576]{1,2,0:T(8,128)(2,1)} %copy.92), channel_id=1, replica_groups=mesh['replica'=4,'shard'=8] {'replica'}, dimensions={0} | all-to-all | bytes 2359296 | tf_op jit(solution)/shard_map/all_to_all | solution.py:178
  720.6 3.7 convolution_convert_fusion.5
  725.0 5.4 convolution_convert_fusion.3
  730.7 6.5 convolution_convert_fusion.1
  749.3 3.3 fusion.97
  758.5 80.5 %reduce-scatter.11.cloned.1.call-done = bf16[96,2304]{1,0:T(8,128)(2,1)} async-done(((bf16[768,2304]{1,0:T(8,128)(2,1)}), bf16[96,2304]{1,0:T(8,128)(2,1)}) %reduce-scatter.11.cloned.1.call-update) | async-done | bytes 442384 | tf_op jit(solution)/shard_map/reduce_scatter | solution.py:219
  841.2 96.6 %reduce-scatter.23.cloned.1.call-done = bf16[384,768]{1,0:T(8,128)(2,1)} async-done(((bf16[3072,768]{1,0:T(8,128)(2,1)}), bf16[384,768]{1,0:T(8,128)(2,1)}) %reduce-scatter.23.cloned.1.call-update) | async-done | bytes 589840 | tf_op jit(solution)/shard_map/reduce_scatter | solution.py:219
  940.0 96.8 %reduce-scatter.19.cloned.1.call-done = bf16[96,3072]{1,0:T(8,128)(2,1)} async-done(((bf16[768,3072]{1,0:T(8,128)(2,1)}), bf16[96,3072]{1,0:T(8,128)(2,1)}) %reduce-scatter.19.cloned.1.call-update) | async-done | bytes 589840 | tf_op jit(solution)/shard_map/reduce_scatter | solution.py:219
  1038.9 80.4 %reduce-scatter.9.cloned.1.call-done = bf16[96,2304]{1,0:T(8,128)(2,1)} async-done(((bf16[768,2304]{1,0:T(8,128)(2,1)}), bf16[96,2304]{1,0:T(8,128)(2,1)}) %reduce-scatter.9.cloned.1.call-update) | async-done | bytes 442384 | tf_op jit(solution)/shard_map/reduce_scatter | solution.py:219
  1121.6 96.6 %reduce-scatter.17.cloned.1.call-done = bf16[96,3072]{1,0:T(8,128)(2,1)} async-done(((bf16[768,3072]{1,0:T(8,128)(2,1)}), bf16[96,3072]{1,0:T(8,128)(2,1)}) %reduce-scatter.17.cloned.1.call-update) | async-done | bytes 589840 | tf_op jit(solution)/shard_map/reduce_scatter | solution.py:219
  1220.4 96.6 %reduce-scatter.21.cloned.1.call-done = bf16[384,768]{1,0:T(8,128)(2,1)} async-done(((bf16[3072,768]{1,0:T(8,128)(2,1)}), bf16[384,768]{1,0:T(8,128)(2,1)}) %reduce-scatter.21.cloned.1.call-update) | async-done | bytes 589840 | tf_op jit(solution)/shard_map/reduce_scatter | solution.py:219
  1320.0 5.3 fusion.56
  1329.4 126.3 %all-reduce.4.cloned.1.call-done = f32[2,9216]{1,0:T(2,128)} async-done(((f32[2,9216]{1,0:T(2,128)}), f32[2,9216]{1,0:T(2,128)}) %all-reduce.4.cloned.1.call-update) | async-done | bytes 73744 | tf_op jit(solution)/shard_map/psum | solution.py:345
  1460.3 143.4 %all-reduce.6.cloned.1.call-done = (f32[1,96,4,3,192]{1,4,3,2,0:T(8,128)}, f32[1,96,4,3,192]{1,4,3,2,0:T(8,128)}, f32[1,96,768]{2,1,0:T(8,128)}, f32[1,96,768]{2...) async-done(((f32[1,96,4,3,192]{1,4,3,2,0:T(8,128)}, f32[1,96,4,3,192]{1,4,3,2,0:T(8,128)}, ...) | async-done | bytes 7077904 | tf_op jit(solution)/shard_map/psum | solution.py:218
  1608.1 3.8 reshape_reshape.2
  (402 shorter events, 121.8 us)
Async XLA Ops:
  7.2 88.3 %all-gather.17.cloned.1.call-start = ((), (), s32[]{:S(2)}) async-start(), calls=%async_computation.16 | async-start | bytes 3981312 | tf_op jit(solution)/shard_map/all_gather | solution.py:210
  12.3 125.3 %all-gather.21.cloned.1.call-start = ((), (), s32[]{:S(2)}) async-start(), calls=%async_computation.27 | async-start | bytes 1327104 | tf_op jit(solution)/shard_map/all_gather | solution.py:210
  14.1 204.0 %all-gather.23.cloned.1.call-start = ((), (), s32[]{:S(2)}) async-start(), calls=%async_computation.28 | async-start | bytes 5308416 | tf_op jit(solution)/shard_map/all_gather | solution.py:210
  15.4 283.0 %all-gather.25.cloned.1.call-start = ((), (), s32[]{:S(2)}) async-start(), calls=%async_computation.29 | async-start | bytes 5308416 | tf_op jit(solution)/shard_map/all_gather | solution.py:210
  16.6 346.9 %all-gather.19.cloned.1.call-start = ((), (), s32[]{:S(2)}) async-start(), calls=%async_computation.17 | async-start | bytes 3981312 | tf_op jit(solution)/shard_map/all_gather | solution.py:210
  17.7 395.2 %all-gather.27.cloned.1.call-start = ((), (), s32[]{:S(2)}) async-start(), calls=%async_computation.30 | async-start | bytes 1327104 | tf_op jit(solution)/shard_map/all_gather | solution.py:210
  18.3 474.9 %all-gather.29.cloned.1.call-start = ((), (), s32[]{:S(2)}) async-start(), calls=%async_computation.31 | async-start | bytes 5308416 | tf_op jit(solution)/shard_map/all_gather | solution.py:210
  19.0 554.6 %all-gather.31.cloned.1.call-start = ((), (), s32[]{:S(2)}) async-start(), calls=%async_computation.32 | async-start | bytes 5308416 | tf_op jit(solution)/shard_map/all_gather | solution.py:210
  19.1 57.5 %collective-permute-start.1 = (bf16[128,768]{1,0:T(8,128)(2,1)S(1)}, bf16[128,768]{1,0:T(8,128)(2,1)S(1)}, u32[]{:S(2)}, u32[]{:S(2)}) collective-permute-start(bf16[128,768]{1,0:T(8,128)(2,1)S(1)} %get-tuple-element.85), channel_id=1, source_target_pairs={{0,1},{1,0},{2,9},{3,8},{4,17},{5,16},{6,25},{7,24},{8,3},{9,2},{1... | collective-permute-start | bytes 589832 | tf_op jit(solution)/shard_map/ppermute | solution.py:145
  22.2 54.4 %collective-permute-start = (bf16[128,768]{1,0:T(8,128)(2,1)S(1)}, bf16[128,768]{1,0:T(8,128)(2,1)S(1)}, u32[]{:S(2)}, u32[]{:S(2)}) collective-permute-start(bf16[128,768]{1,0:T(8,128)(2,1)S(1)} %get-tuple-element.86), channel_id=1, source_target_pairs={{0,0},{1,1},{2,8},{3,9},{4,16},{5,17},{6,24},{7,25},{8,2},{9,3},{1... | collective-permute-start | bytes 589832 | tf_op jit(solution)/shard_map/ppermute | solution.py:145
  76.8 67.0 %copy-start.7 = (bf16[128,768]{1,0:T(8,128)(2,1)}, bf16[128,768]{1,0:T(8,128)(2,1)S(1)}, u32[]{:S(2)}) copy-start(bf16[128,768]{1,0:T(8,128)(2,1)S(1)} %get-tuple-element.83) | copy-start | bytes 589828
  76.8 67.0 %copy-start.9 = (bf16[128,768]{1,0:T(8,128)(2,1)}, bf16[128,768]{1,0:T(8,128)(2,1)S(1)}, u32[]{:S(2)}) copy-start(bf16[128,768]{1,0:T(8,128)(2,1)S(1)} %get-tuple-element.84) | copy-start | bytes 589828
  100.1 19.3 %all-to-all-start = ((bf16[256,4,576]{0,2,1:T(8,128)(2,1)}), bf16[256,4,576]{0,2,1:T(8,128)(2,1)S(1)}, u32[]{:S(2)}, u32[]{:S(2)}) async-start(bf16[256,4,576]{0,2,1:T(8,128)(2,1)} %bitcast.14), calls=%async_computation | async-start | bytes 2359296 | tf_op jit(solution)/shard_map/all_to_all | solution.py:175
  105.1 113.0 %copy-start.39 = (f32[768]{0:T(1024)}, f32[768]{0:T(1024)S(1)}, u32[]{:S(2)}) copy-start(f32[768]{0:T(1024)S(1)} %add.361) | copy-start | bytes 9220
  105.8 257.6 %copy-start.41 = (f32[768]{0:T(1024)}, f32[768]{0:T(1024)S(1)}, u32[]{:S(2)}) copy-start(f32[768]{0:T(1024)S(1)} %add.374) | copy-start | bytes 9220
  132.7 11.0 all-to-all-start.1
  143.7 79.8 %copy-start.22 = (bf16[4,256,192]{1,2,0:T(8,128)(2,1)}, bf16[4,256,192]{1,2,0:T(8,128)(2,1)S(1)}, u32[]{:S(2)}) copy-start(bf16[4,256,192]{1,2,0:T(8,128)(2,1)S(1)} %all-to-all-done.1) | copy-start | bytes 1179652
  145.7 506.5 %copy-start = (f32[256,768]{1,0:T(8,128)}, f32[256,768]{1,0:T(8,128)S(1)}, u32[]{:S(2)}) copy-start(f32[256,768]{1,0:T(8,128)S(1)} %get-tuple-element.110) | copy-start | bytes 2359300
  145.8 77.8 %copy-start.52 = (f32[256]{0:T(256)}, f32[256]{0:T(256)S(1)}, u32[]{:S(2)}) copy-start(f32[256]{0:T(256)S(1)} %broadcast_multiply_fusion.2) | copy-start | bytes 3076
  146.0 77.5 %copy-start.79 = (f32[256]{0:T(256)}, f32[256]{0:T(256)S(1)}, u32[]{:S(2)}) copy-start(f32[256]{0:T(256)S(1)} %multiply_reduce_fusion.8) | copy-start | bytes 3076
  146.0 77.5 %copy-start.67 = (f32[256]{0:T(256)}, f32[256]{0:T(256)S(1)}, u32[]{:S(2)}) copy-start(f32[256]{0:T(256)S(1)} %fusion.89) | copy-start | bytes 3076
  303.8 62.9 %copy-start.55 = (f32[256]{0:T(256)}, f32[256]{0:T(256)S(1)}, u32[]{:S(2)}) copy-start(f32[256]{0:T(256)S(1)} %broadcast_multiply_fusion.1) | copy-start | bytes 3076
  304.0 62.6 %copy-start.81 = (f32[256]{0:T(256)}, f32[256]{0:T(256)S(1)}, u32[]{:S(2)}) copy-start(f32[256]{0:T(256)S(1)} %multiply_reduce_fusion.7) | copy-start | bytes 3076
  368.1 22.3 %all-to-all-start.2 = ((bf16[256,4,576]{0,2,1:T(8,128)(2,1)}), bf16[256,4,576]{0,2,1:T(8,128)(2,1)S(1)}, u32[]{:S(2)}, u32[]{:S(2)}) async-start(bf16[256,4,576]{0,2,1:T(8,128)(2,1)} %bitcast.211), calls=%async_computation.2 | async-start | bytes 2359296 | tf_op jit(solution)/shard_map/all_to_all | solution.py:175
  372.4 36.7 %collective-permute-start.5 = (bf16[128,768]{1,0:T(8,128)(2,1)}, bf16[128,768]{1,0:T(8,128)(2,1)S(1)}, u32[]{:S(2)}, u32[]{:S(2)}) collective-permute-start(bf16[128,768]{1,0:T(8,128)(2,1)} %get-tuple-element.77), channel_id=1, source_target_pairs={{0,1},{1,0},{2,9},{3,8},{4,17},{5,16},{6,25},{7,24},{8,3},{9,2},{1... | collective-permute-start | bytes 589832 | tf_op jit(solution)/shard_map/ppermute | solution.py:145
  372.9 36.2 %collective-permute-start.4 = (bf16[128,768]{1,0:T(8,128)(2,1)S(1)}, bf16[128,768]{1,0:T(8,128)(2,1)S(1)}, u32[]{:S(2)}, u32[]{:S(2)}) collective-permute-start(bf16[128,768]{1,0:T(8,128)(2,1)S(1)} %get-tuple-element.78), channel_id=1, source_target_pairs={{0,0},{1,1},{2,8},{3,9},{4,16},{5,17},{6,24},{7,25},{8,2},{9,3},{1... | collective-permute-start | bytes 589832 | tf_op jit(solution)/shard_map/ppermute | solution.py:145
  403.6 11.5 all-to-all-start.3
  409.1 84.0 %copy-start.43 = (f32[768]{0:T(1024)S(1)}, f32[768]{0:T(1024)}, u32[]{:S(2)}) copy-start(f32[768]{0:T(1024)} %add.385) | copy-start | bytes 9220
  410.9 162.7 %copy-start.14 = (bf16[128,768]{1,0:T(8,128)(2,1)}, bf16[128,768]{1,0:T(8,128)(2,1)S(1)}, u32[]{:S(2)}) copy-start(bf16[128,768]{1,0:T(8,128)(2,1)S(1)} %get-tuple-element.75) | copy-start | bytes 589828
  410.9 162.7 %copy-start.18 = (bf16[128,768]{1,0:T(8,128)(2,1)}, bf16[128,768]{1,0:T(8,128)(2,1)S(1)}, u32[]{:S(2)}) copy-start(bf16[128,768]{1,0:T(8,128)(2,1)S(1)} %get-tuple-element.76) | copy-start | bytes 589828
  415.1 83.6 %copy-start.12 = (bf16[4,256,192]{1,2,0:T(8,128)(2,1)}, bf16[4,256,192]{1,2,0:T(8,128)(2,1)S(1)}, u32[]{:S(2)}) copy-start(bf16[4,256,192]{1,2,0:T(8,128)(2,1)S(1)} %all-to-all-done.3) | copy-start | bytes 1179652
  417.1 166.4 %copy-start.58 = (f32[256]{0:T(256)}, f32[256]{0:T(256)S(1)}, u32[]{:S(2)}) copy-start(f32[256]{0:T(256)S(1)} %broadcast_multiply_fusion) | copy-start | bytes 3076
  417.3 166.2 %copy-start.72 = (f32[256]{0:T(256)}, f32[256]{0:T(256)S(1)}, u32[]{:S(2)}) copy-start(f32[256]{0:T(256)S(1)} %fusion.91) | copy-start | bytes 3076
  618.3 19.3 %all-to-all-start.5 = ((bf16[4,256,576]{1,2,0:T(8,128)(2,1)}), bf16[4,256,576]{1,2,0:T(8,128)(2,1)S(1)}, u32[]{:S(2)}, u32[]{:S(2)}) async-start(bf16[4,256,576]{1,2,0:T(8,128)(2,1)} %copy.89), calls=%async_computation.5 | async-start | bytes 2359296 | tf_op jit(solution)/shard_map/all_to_all | solution.py:178
  621.8 132.2 %reduce-scatter.15.cloned.1.call-start = ((), (), s32[]{:S(2)}) async-start(), calls=%async_computation.22 | async-start | bytes 1327104 | tf_op jit(solution)/shard_map/reduce_scatter | solution.py:219
  624.8 132.0 %reduce-scatter.13.cloned.1.call-start = ((), (), s32[]{:S(2)}) async-start(), calls=%async_computation.21 | async-start | bytes 1327104 | tf_op jit(solution)/shard_map/reduce_scatter | solution.py:219
  655.1 183.9 %reduce-scatter.11.cloned.1.call-start = ((), (), s32[]{:S(2)}) async-start(), calls=%async_computation.20 | async-start | bytes 3981312 | tf_op jit(solution)/shard_map/reduce_scatter | solution.py:219
  658.3 279.5 %reduce-scatter.23.cloned.1.call-start = ((), (), s32[]{:S(2)}) async-start(), calls=%async_computation.26 | async-start | bytes 5308416 | tf_op jit(solution)/shard_map/reduce_scatter | solution.py:219
  665.6 371.1 %reduce-scatter.19.cloned.1.call-start = ((), (), s32[]{:S(2)}) async-start(), calls=%async_computation.24 | async-start | bytes 5308416 | tf_op jit(solution)/shard_map/reduce_scatter | solution.py:219
  671.5 447.8 %reduce-scatter.9.cloned.1.call-start = ((), (), s32[]{:S(2)}) async-start(), calls=%async_computation.19 | async-start | bytes 3981312 | tf_op jit(solution)/shard_map/reduce_scatter | solution.py:219
  724.3 493.8 %reduce-scatter.17.cloned.1.call-start = ((), (), s32[]{:S(2)}) async-start(), calls=%async_computation.23 | async-start | bytes 5308416 | tf_op jit(solution)/shard_map/reduce_scatter | solution.py:219
  730.4 586.6 %reduce-scatter.21.cloned.1.call-start = ((), (), s32[]{:S(2)}) async-start(), calls=%async_computation.25 | async-start | bytes 5308416 | tf_op jit(solution)/shard_map/reduce_scatter | solution.py:219
  737.2 718.4 %all-reduce.4.cloned.1.call-start = ((), (), s32[]{:S(2)}) async-start(), calls=%async_computation.18 | async-start | bytes 147456 | tf_op jit(solution)/shard_map/psum | solution.py:345
  753.9 849.8 %all-reduce.6.cloned.1.call-start = ((), (), s32[]{:S(2)}) async-start(), calls=%async_computation.33 | async-start | bytes 15335424 | tf_op jit(solution)/shard_map/psum | solution.py:218
  1325.4 132.9 %collective-permute-start.3 = (bf16[128,768]{1,0:T(8,128)(2,1)S(1)}, bf16[128,768]{1,0:T(8,128)(2,1)S(1)}, u32[]{:S(2)}, u32[]{:S(2)}) collective-permute-start(bf16[128,768]{1,0:T(8,128)(2,1)S(1)} %get-tuple-element.81), channel_id=1, source_target_pairs={{1,0},{0,1},{9,2},{8,3},{17,4},{16,5},{25,6},{24,7},{3,8},{2,9},{1... | collective-permute-start | bytes 589832 | tf_op jit(solution)/shard_map/ppermute | solution.py:165
  1326.9 131.3 %collective-permute-start.2 = (bf16[128,768]{1,0:T(8,128)(2,1)S(1)}, bf16[128,768]{1,0:T(8,128)(2,1)S(1)}, u32[]{:S(2)}, u32[]{:S(2)}) collective-permute-start(bf16[128,768]{1,0:T(8,128)(2,1)S(1)} %get-tuple-element.82), channel_id=1, source_target_pairs={{0,0},{1,1},{8,2},{9,3},{16,4},{17,5},{24,6},{25,7},{2,8},{3,9},{1... | collective-permute-start | bytes 589832 | tf_op jit(solution)/shard_map/ppermute | solution.py:165
  1328.1 130.2 %collective-permute-start.7 = (bf16[128,768]{1,0:T(8,128)(2,1)S(1)}, bf16[128,768]{1,0:T(8,128)(2,1)S(1)}, u32[]{:S(2)}, u32[]{:S(2)}) collective-permute-start(bf16[128,768]{1,0:T(8,128)(2,1)S(1)} %get-tuple-element.73), channel_id=1, source_target_pairs={{1,0},{0,1},{9,2},{8,3},{17,4},{16,5},{25,6},{24,7},{3,8},{2,9},{1... | collective-permute-start | bytes 589832 | tf_op jit(solution)/shard_map/ppermute | solution.py:165
  1328.7 129.6 %collective-permute-start.6 = (bf16[128,768]{1,0:T(8,128)(2,1)S(1)}, bf16[128,768]{1,0:T(8,128)(2,1)S(1)}, u32[]{:S(2)}, u32[]{:S(2)}) collective-permute-start(bf16[128,768]{1,0:T(8,128)(2,1)S(1)} %get-tuple-element.74), channel_id=1, source_target_pairs={{0,0},{1,1},{8,2},{9,3},{16,4},{17,5},{24,6},{25,7},{2,8},{3,9},{1... | collective-permute-start | bytes 589832 | tf_op jit(solution)/shard_map/ppermute | solution.py:165
  (83 other events, 691.0 us)
Sparse Core Ops, SparseCore 0:
  12.5 82.9 all-gather.16
  97.6 39.5 all-gather.20
  140.0 78.0 all-gather.22
  220.7 77.6 all-gather.24
  300.5 62.9 all-gather.18
  365.5 47.3 all-gather.26
  415.1 77.9 all-gather.28
  495.9 77.6 all-gather.30
  626.0 63.7 reduce-scatter.14
  693.0 63.7 reduce-scatter.12
  760.4 78.4 reduce-scatter.10
  842.5 95.2 reduce-scatter.22
  941.4 95.2 reduce-scatter.18
  1040.2 79.0 reduce-scatter.8
  1122.8 95.2 reduce-scatter.16
  1221.7 95.2 reduce-scatter.20
  1323.0 132.6 all-reduce.3
  1459.5 144.1 all-reduce.5

commit v2 on v1

--- a/solution.py
+++ b/solution.py
@@ -192,25 +192,206 @@
         return parts[..., :HEADS, :].reshape(lead + (-1,))
 
 
-def gather_vectors(place, vectors):
-    layers = vectors[0].shape[0]
-    packed = jnp.concatenate(vectors, -1)
-    whole = lax.all_gather(packed, "shard", axis=0)
+MESH = pl.DeviceIdType.MESH
+
+
+class Grid:
+    def __init__(self, replicas, shards):
+        self.cores = 2 if replicas % 2 == 0 else 1
+        self.xs = replicas // self.cores
+        self.zs = 4 if shards % 4 == 0 else 1
+        self.ys = shards // self.zs
+        r, s = lax.axis_index("replica"), lax.axis_index("shard")
+        self.x, self.core = r // self.cores, lax.rem(r, self.cores)
+        self.z, self.y = s // self.ys, lax.rem(s, self.ys)
+
+    def device(self, x=0, core=0, z=0, y=0):
+        to_x = lax.rem(self.x + x + self.xs, self.xs)
+        to_core = lax.rem(self.core + core, self.cores)
+        to_z = lax.rem(self.z + z + self.zs, self.zs)
+        to_y = lax.rem(self.y + y + self.ys, self.ys)
+        return {"replica": to_x * self.cores + to_core, "shard": to_z * self.ys + to_y}
+
+    def block(self, z_back, y_back):
+        from_z = lax.rem(self.z - z_back + self.zs, self.zs)
+        from_y = lax.rem(self.y - y_back + self.ys, self.ys)
+        return from_z * self.ys + from_y
+
+    def greet(self):
+        near = []
+        for axis, size in (("x", self.xs), ("core", self.cores), ("z", self.zs), ("y", self.ys)):
+            if size > 1:
+                near.append({axis: 1})
+            if size > 2:
+                near.append({axis: -1})
+        barrier = pltpu.get_barrier_semaphore()
+        for step in near:
+            pl.semaphore_signal(barrier, 1, device_id=self.device(**step), device_id_type=MESH)
+        pl.semaphore_wait(barrier, len(near))
+
+
+def window(ref, row, rows, col, cols):
+    row = row if isinstance(row, int) else pl.multiple_of(row, 16)
+    col = col if isinstance(col, int) else pl.multiple_of(col, 128)
+    return ref.at[pl.ds(row, rows), pl.ds(col, cols)]
+
+
+def part_of(grid, kind, ref, shape, block, x_at):
+    rows, cols = shape
+    row = block * rows
+    if kind == "whole":
+        return window(ref, row, rows, 0, cols)
+    half = cols // grid.cores
+    if kind == "half":
+        return window(ref, row, rows, grid.core * half, half)
+    if kind == "columns":
+        share = half // grid.xs
+        return window(ref, row, rows, grid.core * half + x_at * share, share)
+    share = rows // grid.xs
+    return window(ref, row + x_at * share, share, grid.core * half, half)
+
+
+def half_of(grid, ref, shape, block):
+    rows, cols = shape
+    half = cols // grid.cores
+    return window(ref, block * rows, rows, grid.core * half, half)
+
+
+def copies_of_gather(kind, grid):
+    blocks = grid.zs * grid.ys
+    count = blocks - 1
+    if kind in ("columns", "rows"):
+        count += (blocks - 1) * (grid.xs - 1)
+    if kind != "whole":
+        count += (blocks - 1) * (grid.cores - 1)
+    return count
+
+
+def gather_kernel(replicas, shards, kinds, *refs):
+    count = len(kinds)
+    sources, targets = refs[:count], refs[count : 2 * count]
+    send_sems, recv_sems, own_sems = refs[2 * count :]
+    grid = Grid(replicas, shards)
+    shapes = [source.shape for source in sources]
+    started = []
+
+    def send(source, target, device):
+        at = len(started)
+        copy = pltpu.make_async_remote_copy(
+            src_ref=source,
+            dst_ref=target,
+            send_sem=send_sems.at[at],
+            recv_sem=recv_sems.at[at],
+            device_id=device,
+            device_id_type=MESH,
+        )
+        copy.start()
+        started.append(copy)
+        return copy
+
+    def fetched(job, z_back, y_back, x_back=0):
+        kind, shape = kinds[job], shapes[job]
+        x_at = lax.rem(grid.x - x_back + grid.xs, grid.xs)
+        target = part_of(grid, kind, targets[job], shape, grid.block(z_back, y_back), x_at)
+        if z_back == 0 and y_back == 0:
+            return part_of(grid, kind, sources[job], shape, 0, x_at), target
+        return target, target
+
+    grid.greet()
+    own = []
+    for job in range(count):
+        rows = shapes[job][0]
+        place = targets[job].at[pl.ds(pl.multiple_of(grid.block(0, 0) * rows, 16), rows), :]
+        copy = pltpu.make_async_copy(sources[job], place, own_sems.at[job])
+        copy.start()
+        own.append(copy)
+
+    along_z, along_y, along_x, along_core = {}, {}, {}, {}
+    for step in range(grid.zs + 3):
+        for job, kind in enumerate(kinds):
+            z_back = step
+            if z_back < grid.zs:
+                if z_back > 0:
+                    along_z[job, z_back - 1].wait_recv()
+                if z_back < grid.zs - 1:
+                    along_z[job, z_back] = send(*fetched(job, z_back, 0), grid.device(z=1))
+                if grid.ys > 1:
+                    along_y[job, z_back, 0] = send(*fetched(job, z_back, 0), grid.device(y=1))
+            z_back = step - 1
+            if 0 <= z_back < grid.zs:
+                for y_back in range(1, grid.ys):
+                    along_y[job, z_back, y_back - 1].wait_recv()
+                    if y_back < grid.ys - 1:
+                        along_y[job, z_back, y_back] = send(
+                            *fetched(job, z_back, y_back), grid.device(y=1)
+                        )
+                if kind in ("columns", "rows") and grid.xs > 1:
+                    for y_back in range(0 if z_back else 1, grid.ys):
+                        along_x[job, z_back, y_back, 0] = send(
+                            *fetched(job, z_back, y_back), grid.device(x=1)
+                        )
+            z_back = step - 2
+            if 0 <= z_back < grid.zs and kind != "whole":
+                for y_back in range(0 if z_back else 1, grid.ys):
+                    if kind != "half":
+                        for x_back in range(1, grid.xs):
+                            along_x[job, z_back, y_back, x_back - 1].wait_recv()
+                            if x_back < grid.xs - 1:
+                                along_x[job, z_back, y_back, x_back] = send(
+                                    *fetched(job, z_back, y_back, x_back), grid.device(x=1)
+                                )
+                    if grid.cores > 1:
+                        half = half_of(grid, targets[job], shapes[job], grid.block(z_back, y_back))
+                        along_core[job, z_back, y_back] = send(half, half, grid.device(core=1))
+            z_back = step - 3
+            if 0 <= z_back < grid.zs and kind != "whole" and grid.cores > 1:
+                for y_back in range(0 if z_back else 1, grid.ys):
+                    along_core[job, z_back, y_back].wait_recv()
+    for copy in started:
+        copy.wait_send()
+    for copy in own:
+        copy.wait()
+
+
+def gather_shards(place, kinds, shards):
+    sizes = Grid(place.replicas, place.shards)
+    copies = sum(copies_of_gather(kind, sizes) for kind in kinds)
+    return pl.pallas_call(
+        functools.partial(gather_kernel, place.replicas, place.shards, kinds),
+        out_shape=[
+            jax.ShapeDtypeStruct((place.shards * a.shape[0], a.shape[1]), a.dtype) for a in shards
+        ],
+        in_specs=[pl.BlockSpec(memory_space=pltpu.VMEM)] * len(shards),
+        out_specs=[pl.BlockSpec(memory_space=pl.ANY)] * len(shards),
+        scratch_shapes=[
+            pltpu.SemaphoreType.DMA((copies,)),
+            pltpu.SemaphoreType.DMA((copies,)),
+            pltpu.SemaphoreType.DMA((len(shards),)),
+        ],
+        compiler_params=pltpu.CompilerParams(collective_id=0, has_side_effects=True),
+        name="gather_shards",
+    )(*shards)
+
+
+def gather_all(place, vectors, mix, out_w, up, down):
+    layers = mix.shape[0]
+    packed = jnp.concatenate(vectors, -1).reshape(-1)
+    size = packed.shape[0]
+    lanes = 128 * -(-size // (16 * 128))
+    packed = jnp.pad(packed, (0, 16 * lanes - size)).reshape(16, lanes)
+    first = jnp.concatenate([mix, out_w], -1)
+    kinds, shards = ["whole"], [packed]
+    for layer in range(layers):
+        kinds += ["half", "columns", "rows"]
+        shards += [first[layer], up[layer], down[layer]]
+    whole = gather_shards(place, tuple(kinds), shards)
+    flat = whole[0].reshape(place.shards, -1)[:, :size].reshape(place.shards, layers, -1)
     out, start = [], 0
     for vector in vectors:
-        size = vector.shape[1]
-        piece = whole[:, :, start : start + size]
+        piece = flat[:, :, start : start + vector.shape[1]]
         out.append(jnp.swapaxes(piece, 0, 1).reshape(layers, -1).astype(F32))
-        start += size
-    return out
-
-
-def gather_weights(place, mix, out_w, up, down):
-    full = [
-        [lax.all_gather(w[layer], "shard", axis=0, tiled=True) for w in (mix, out_w, up, down)]
-        for layer in range(mix.shape[0])
-    ]
-    return full
+        start += vector.shape[1]
+    return [whole[1 + 3 * n : 4 + 3 * n] for n in range(layers)], out
 
 
 def reduce_weights(place, grads):
@@ -223,7 +404,8 @@
 
 
 def forward_block(place, current, weights, vectors):
-    mix, out_w, up, down = weights
+    mix_out, up, down = weights
+    mix, out_w = jnp.split(mix_out, [mix_out.shape[1] - place.width], 1)
     gain_one, shift_one, mix_bias, out_bias, gain_two, shift_two, up_bias, down_bias = vectors
     normed = norm_rows(current, gain_one, shift_one).astype(BF16)
     mixed = (dot(normed, mix, ((1,), (0,))) + mix_bias).astype(BF16)
@@ -238,7 +420,8 @@
 
 
 def backward_block(place, grad_next, weights, vectors, saved):
-    mix, out_w, up, down = weights
+    mix_out, up, down = weights
+    mix, out_w = jnp.split(mix_out, [mix_out.shape[1] - place.width], 1)
     gain_one, shift_one, mix_bias, out_bias, gain_two, shift_two, up_bias, down_bias = vectors
     current, normed, mixed, attended, x_mid, moved, pre, act = saved
     d_ffn = grad_next.astype(BF16)
@@ -301,7 +484,7 @@
     place = Place(tokens)
     layers = gain_one.shape[0]
     mix_weight = place.mix_columns(query_key_value_weight)
-    vectors = gather_vectors(
+    weights, vectors = gather_all(
         place,
         (
             gain_one,
@@ -314,10 +497,13 @@
             up_bias,
             down_bias,
         ),
+        mix_weight,
+        output_weight,
+        up_weight,
+        down_weight,
     )
     g1, s1, bq, bv, bo, g2, s2, bu, bd = vectors
     mix_bias = place.mix_columns(jnp.concatenate([bq, jnp.zeros_like(bq), bv], -1))
-    weights = gather_weights(place, mix_weight, output_weight, up_weight, down_weight)
 
     def layer_vectors(n):
         return (g1[n], s1[n], mix_bias[n], bo[n], g2[n], s2[n], bu[n], bd[n])

time: 1630 us -> 1200 us (0.74)
  waiting for transfers between devices: 1250 us -> 756 us
  Pallas kernels: 48.4 us -> 176 us
  blocking collectives: 93.5 us -> 39.1 us
    all_gather x8 -> x0, waiting for transfers between devices: 377 us -> none  [gather_weights(): lax.all_gather(w[layer], 'shard', axis=0, tiled=True)]
    pallas_call x0 -> x1, Pallas kernels: none -> 128 us  [gather_shards(): pl.pallas_call(functools.partial(gather_kernel, place.replicas, place.sha...]
    psum x1, waiting for transfers between devices: 126 us -> 0.03 us  [per_device(): packed = lax.psum(packed, BOTH)]
    all_gather x1 -> x0, blocking collectives: 52.8 us -> none  [gather_vectors(): whole = lax.all_gather(packed, 'shard', axis=0)]
  transfers between devices with their start and end apart: 31 -> 23, of which waited for: 21 -> 15; matrix products, arithmetic and copies ran while one was open for 9% -> 10% of each run, Pallas kernels for 2% -> 13%
where the time goes in v2:
time: 1200 us; the launch traced here: 1190 us
  waiting for transfers between devices  756 us (63%)
  Pallas kernels  176 us (15%)
  matrix products  82.2 us (7%)
  local copies, waits for them, and re-layouts  66.3 us (6%)
  blocking collectives  39.1 us (3%)
  other arithmetic  28.5 us (2%)
  starting transfers between devices  27.1 us (2%)
  between operations  17.5 us (1%)
    reduce_scatter x8, waiting for transfers between devices, reduce_weights(): lax.psum_scatter(g, 'shard', scatter_dimension=0, tiled=True).astype(F32)  553 us
    psum x1, waiting for transfers between devices, reduce_weights(): lax.psum(lax.psum_scatter(g, 'shard', scatter_dimension=0, tiled=True).as...  140 us
    pallas_call x1, Pallas kernels, gather_shards(): pl.pallas_call(functools.partial(gather_kernel, place.replicas, place.sha...  128 us
    dot_general x24, matrix products, dot(): lax.dot_general(a, b, (contract, ((), ())), preferred_element_type=F32)  82.2 us
    all_to_all x2, waiting for transfers between devices, to_heads(): return lax.all_to_all(values, 'replica', 1, 0, tiled=True)  35.8 us
    pallas_call x2, Pallas kernels, attend_back(): pl.pallas_call(attend_back_kernel, out_shape=jax.ShapeDtypeStruct((length...  28.8 us
  transfers between devices with their start and end apart: 23, of which 15 were waited for; matrix products, arithmetic and copies ran while one was open for 10% of the time, Pallas kernels for 13%

profile of v2, /device:TPU:0, one launch (start us, length us, event | category | flops | bytes accessed | tf_op | source)
XLA Modules:
  0.0 1192.8 jit_solution(778810468393687209)
XLA Ops:
  9.1 3.1 collective-permute-start.1
  14.4 2.9 reshape.300
  21.3 2.4 slice_bitcast_fusion
  24.8 127.6 %gather_shards.1 = (bf16[128,256]{1,0:T(8,128)(2,1)}, bf16[768,3072]{1,0:T(8,128)(2,1)}, bf16[768,3072]{1,0:T(8,128)(2,1)}, bf16[3072,768]{1,0:T(8,128)(2,1)}, b...) custom-call(bf16[16,256]{1,0:T(8,128)(2,1)} %reshape.299.refs_0_, ...), custom_call_target="tpu_custom_call" | custom-call | tf_op jit(solution)/shard_map/gather_shards/pallas_call | solution.py:359
  154.6 3.2 fusion
  159.2 3.5 all-to-all-start
  164.6 14.4 %all-to-all-done = bf16[256,4,576]{0,2,1:T(8,128)(2,1)S(1)} async-done(((bf16[256,4,576]{0,2,1:T(8,128)(2,1)}), bf16[256,4,576]{0,2,1:T(8,128)(2,1)S(1)}, u32[]{:S(2)}, u32[]{:S(2)}) %all-to-all-start) | async-done | bytes 1179680 | tf_op jit(solution)/shard_map/all_to_all | solution.py:175
  180.4 9.8 attend.2
  192.2 3.7 all-to-all-start.1
  198.2 5.0 all-to-all-done.1
  205.6 4.2 convolution_add_fusion.3
  215.5 3.5 all-to-all-start.2
  219.9 21.4 %all-to-all-done.2 = bf16[256,4,576]{0,2,1:T(8,128)(2,1)S(1)} async-done(((bf16[256,4,576]{0,2,1:T(8,128)(2,1)}), bf16[256,4,576]{0,2,1:T(8,128)(2,1)S(1)}, u32[]{:S(2)}, u32[]{:S(2)}) %all-to-all-start.2) | async-done | bytes 1179680 | tf_op jit(solution)/shard_map/all_to_all | solution.py:175
  242.7 9.8 attend.3
  254.5 4.1 all-to-all-start.3
  261.1 4.9 all-to-all-done.3
  268.3 4.0 convolution_add_fusion.2
  272.3 4.8 convert_reduce_fusion
  283.5 9.8 all_to_all.152
  294.3 14.5 %attend_back.2 = bf16[1024,576]{1,0:T(8,128)(2,1)} custom-call(bf16[1024,576]{1,0:T(8,128)(2,1)} %bitcast.154, bf16[1024,192]{1,0:T(8,128)(2,1)} %bitcast.171), custom_call_target="tpu_custom_call" | custom-call | tf_op jit(solution)/shard_map/attend_back/pallas_call | solution.py:113
  308.7 2.4 copy.62
  311.1 3.5 all-to-all-start.5
  314.9 2.6 convolution_convert_fusion.6
  317.6 12.9 %all-to-all-done.5 = bf16[4,256,576]{1,2,0:T(8,128)(2,1)S(1)} async-done(((bf16[4,256,576]{1,2,0:T(8,128)(2,1)}), bf16[4,256,576]{1,2,0:T(8,128)(2,1)S(1)}, u32[]{:S(2)}, u32[]{:S(2)}) %all-to-all-start.5) | async-done | bytes 1179680 | tf_op jit(solution)/shard_map/all_to_all | solution.py:178
  330.5 4.1 multiply_reduce_fusion.1
  336.6 3.7 convert_reduce_fusion.1
  345.3 3.1 convolution_convert_fusion.4
  349.4 6.4 convolution_convert_fusion
  356.5 5.1 convolution_convert_fusion.2
  363.6 10.0 all_to_all.153
  374.6 14.4 %attend_back.3 = bf16[1024,576]{1,0:T(8,128)(2,1)} custom-call(bf16[1024,576]{1,0:T(8,128)(2,1)} %bitcast.152, bf16[1024,192]{1,0:T(8,128)(2,1)} %bitcast.172), custom_call_target="tpu_custom_call" | custom-call | tf_op jit(solution)/shard_map/attend_back/pallas_call | solution.py:113
  389.0 2.4 copy.65
  391.5 19.3 %all_to_all.154 = bf16[4,256,576]{1,2,0:T(8,128)(2,1)S(1)} all-to-all(bf16[4,256,576]{1,2,0:T(8,128)(2,1)} %copy.65), channel_id=1, replica_groups=mesh['replica'=4,'shard'=8] {'replica'}, dimensions={0} | all-to-all | bytes 2359296 | tf_op jit(solution)/shard_map/all_to_all | solution.py:178
  410.8 3.8 convolution_convert_fusion.5
  415.3 5.4 convolution_convert_fusion.3
  420.7 6.5 convolution_convert_fusion.1
  441.2 3.3 fusion.72
  445.9 5.6 reduce-scatter.13.cloned.1.call-done
  453.2 80.6 %reduce-scatter.11.cloned.1.call-done = bf16[96,2304]{1,0:T(8,128)(2,1)} async-done(((bf16[768,2304]{1,0:T(8,128)(2,1)}), bf16[96,2304]{1,0:T(8,128)(2,1)}) %reduce-scatter.11.cloned.1.call-update) | async-done | bytes 442384 | tf_op jit(solution)/shard_map/reduce_scatter | solution.py:400
  536.0 96.8 %reduce-scatter.23.cloned.1.call-done = bf16[384,768]{1,0:T(8,128)(2,1)} async-done(((bf16[3072,768]{1,0:T(8,128)(2,1)}), bf16[384,768]{1,0:T(8,128)(2,1)}) %reduce-scatter.23.cloned.1.call-update) | async-done | bytes 589840 | tf_op jit(solution)/shard_map/reduce_scatter | solution.py:400
  635.0 96.6 %reduce-scatter.19.cloned.1.call-done = bf16[96,3072]{1,0:T(8,128)(2,1)} async-done(((bf16[768,3072]{1,0:T(8,128)(2,1)}), bf16[96,3072]{1,0:T(8,128)(2,1)}) %reduce-scatter.19.cloned.1.call-update) | async-done | bytes 589840 | tf_op jit(solution)/shard_map/reduce_scatter | solution.py:400
  733.8 80.4 %reduce-scatter.9.cloned.1.call-done = bf16[96,2304]{1,0:T(8,128)(2,1)} async-done(((bf16[768,2304]{1,0:T(8,128)(2,1)}), bf16[96,2304]{1,0:T(8,128)(2,1)}) %reduce-scatter.9.cloned.1.call-update) | async-done | bytes 442384 | tf_op jit(solution)/shard_map/reduce_scatter | solution.py:400
  816.5 96.6 %reduce-scatter.17.cloned.1.call-done = bf16[96,3072]{1,0:T(8,128)(2,1)} async-done(((bf16[768,3072]{1,0:T(8,128)(2,1)}), bf16[96,3072]{1,0:T(8,128)(2,1)}) %reduce-scatter.17.cloned.1.call-update) | async-done | bytes 589840 | tf_op jit(solution)/shard_map/reduce_scatter | solution.py:400
  915.3 96.8 %reduce-scatter.21.cloned.1.call-done = bf16[384,768]{1,0:T(8,128)(2,1)} async-done(((bf16[3072,768]{1,0:T(8,128)(2,1)}), bf16[384,768]{1,0:T(8,128)(2,1)}) %reduce-scatter.21.cloned.1.call-update) | async-done | bytes 589840 | tf_op jit(solution)/shard_map/reduce_scatter | solution.py:400
  1015.0 5.3 fusion.26
  1032.4 140.4 %all-reduce.7.cloned.1.call-done = (f32[1,96,4,3,192]{1,4,3,2,0:T(8,128)}, f32[1,96,4,3,192]{1,4,3,2,0:T(8,128)}, f32[1,96,768]{2,1,0:T(8,128)}, f32[1,96,768]{2...) async-done(((f32[1,96,4,3,192]{1,4,3,2,0:T(8,128)}, f32[1,96,4,3,192]{1,4,3,2,0:T(8,128)}, ...) | async-done | bytes 7077904 | tf_op jit(solution)/shard_map/psum | solution.py:399
  1174.6 2.5 copy.68
  1177.1 3.8 reshape_reshape.2
  (374 shorter events, 104.5 us)
Async XLA Ops:
  9.1 144.9 %collective-permute-start.1 = (bf16[128,768]{1,0:T(8,128)(2,1)S(1)}, bf16[128,768]{1,0:T(8,128)(2,1)S(1)}, u32[]{:S(2)}, u32[]{:S(2)}) collective-permute-start(bf16[128,768]{1,0:T(8,128)(2,1)S(1)} %get-tuple-element.87), channel_id=1, source_target_pairs={{0,1},{1,0},{2,9},{3,8},{4,17},{5,16},{6,25},{7,24},{8,3},{9,2},{1... | collective-permute-start | bytes 589832 | tf_op jit(solution)/shard_map/ppermute | solution.py:145
  12.2 141.8 %collective-permute-start = (bf16[128,768]{1,0:T(8,128)(2,1)S(1)}, bf16[128,768]{1,0:T(8,128)(2,1)S(1)}, u32[]{:S(2)}, u32[]{:S(2)}) collective-permute-start(bf16[128,768]{1,0:T(8,128)(2,1)S(1)} %get-tuple-element.88), channel_id=1, source_target_pairs={{0,0},{1,1},{2,8},{3,9},{4,16},{5,17},{6,24},{7,25},{8,2},{9,3},{1... | collective-permute-start | bytes 589832 | tf_op jit(solution)/shard_map/ppermute | solution.py:145
  154.1 49.2 %copy-start.7 = (bf16[128,768]{1,0:T(8,128)(2,1)}, bf16[128,768]{1,0:T(8,128)(2,1)S(1)}, u32[]{:S(2)}) copy-start(bf16[128,768]{1,0:T(8,128)(2,1)S(1)} %get-tuple-element.85) | copy-start | bytes 589828
  154.1 49.1 %copy-start.9 = (bf16[128,768]{1,0:T(8,128)(2,1)}, bf16[128,768]{1,0:T(8,128)(2,1)S(1)}, u32[]{:S(2)}) copy-start(bf16[128,768]{1,0:T(8,128)(2,1)S(1)} %get-tuple-element.86) | copy-start | bytes 589828
  159.2 19.8 %all-to-all-start = ((bf16[256,4,576]{0,2,1:T(8,128)(2,1)}), bf16[256,4,576]{0,2,1:T(8,128)(2,1)S(1)}, u32[]{:S(2)}, u32[]{:S(2)}) async-start(bf16[256,4,576]{0,2,1:T(8,128)(2,1)} %bitcast.20), calls=%async_computation | async-start | bytes 2359296 | tf_op jit(solution)/shard_map/all_to_all | solution.py:175
  192.2 11.0 all-to-all-start.1
  196.7 13.1 %copy-start.33 = (f32[768]{0:T(1024)}, f32[768]{0:T(1024)S(1)}, u32[]{:S(2)}) copy-start(f32[768]{0:T(1024)S(1)} %add.363) | copy-start | bytes 9220
  197.5 14.8 %copy-start.35 = (f32[768]{0:T(1024)}, f32[768]{0:T(1024)S(1)}, u32[]{:S(2)}) copy-start(f32[768]{0:T(1024)S(1)} %add.376) | copy-start | bytes 9220
  203.3 6.6 copy-start.18
  205.3 137.2 %copy-start = (f32[256,768]{1,0:T(8,128)}, f32[256,768]{1,0:T(8,128)S(1)}, u32[]{:S(2)}) copy-start(f32[256,768]{1,0:T(8,128)S(1)} %get-tuple-element.122) | copy-start | bytes 2359300
  205.6 7.3 slice-start
  215.5 25.8 %all-to-all-start.2 = ((bf16[256,4,576]{0,2,1:T(8,128)(2,1)}), bf16[256,4,576]{0,2,1:T(8,128)(2,1)S(1)}, u32[]{:S(2)}, u32[]{:S(2)}) async-start(bf16[256,4,576]{0,2,1:T(8,128)(2,1)} %bitcast.163), calls=%async_computation.2 | async-start | bytes 2359296 | tf_op jit(solution)/shard_map/all_to_all | solution.py:175
  219.1 41.8 %collective-permute-start.5 = (bf16[128,768]{1,0:T(8,128)(2,1)S(1)}, bf16[128,768]{1,0:T(8,128)(2,1)S(1)}, u32[]{:S(2)}, u32[]{:S(2)}) collective-permute-start(bf16[128,768]{1,0:T(8,128)(2,1)S(1)} %get-tuple-element.79), channel_id=1, source_target_pairs={{0,1},{1,0},{2,9},{3,8},{4,17},{5,16},{6,25},{7,24},{8,3},{9,2},{1... | collective-permute-start | bytes 589832 | tf_op jit(solution)/shard_map/ppermute | solution.py:145
  219.2 41.7 %collective-permute-start.4 = (bf16[128,768]{1,0:T(8,128)(2,1)S(1)}, bf16[128,768]{1,0:T(8,128)(2,1)S(1)}, u32[]{:S(2)}, u32[]{:S(2)}) collective-permute-start(bf16[128,768]{1,0:T(8,128)(2,1)S(1)} %get-tuple-element.80), channel_id=1, source_target_pairs={{0,0},{1,1},{2,8},{3,9},{4,16},{5,17},{6,24},{7,25},{8,2},{9,3},{1... | collective-permute-start | bytes 589832 | tf_op jit(solution)/shard_map/ppermute | solution.py:145
  242.7 15.9 %copy-start.39 = (f32[1,8,384]{2,1,0:T(8,128)S(1)}, f32[1,8,384]{2,1,0:T(8,128)}, u32[]{:S(2)}) copy-start(f32[1,8,384]{2,1,0:T(8,128)} %get-tuple-element.107) | copy-start | bytes 36868
  254.5 11.5 all-to-all-start.3
  260.1 12.2 %copy-start.37 = (f32[768]{0:T(1024)}, f32[768]{0:T(1024)S(1)}, u32[]{:S(2)}) copy-start(f32[768]{0:T(1024)S(1)} %add.387) | copy-start | bytes 9220
  261.1 18.7 %copy-start.12 = (bf16[128,768]{1,0:T(8,128)(2,1)}, bf16[128,768]{1,0:T(8,128)(2,1)S(1)}, u32[]{:S(2)}) copy-start(bf16[128,768]{1,0:T(8,128)(2,1)S(1)} %get-tuple-element.77) | copy-start | bytes 589828
  261.1 18.7 %copy-start.15 = (bf16[128,768]{1,0:T(8,128)(2,1)}, bf16[128,768]{1,0:T(8,128)(2,1)S(1)}, u32[]{:S(2)}) copy-start(bf16[128,768]{1,0:T(8,128)(2,1)S(1)} %get-tuple-element.78) | copy-start | bytes 589828
  266.0 6.3 copy-start.11
  266.0 6.3 slice-start.2
  268.0 11.3 copy-start.53
  268.3 11.1 copy-start.64
  268.3 8.8 slice-start.10
  281.4 27.4 %copy-start.20 = (bf16[256,768]{1,0:T(8,128)(2,1)}, bf16[256,768]{1,0:T(8,128)(2,1)S(1)}, u32[]{:S(2)}) copy-start(bf16[256,768]{1,0:T(8,128)(2,1)S(1)} %get-tuple-element.59) | copy-start | bytes 1179652
  311.1 19.3 %all-to-all-start.5 = ((bf16[4,256,576]{1,2,0:T(8,128)(2,1)}), bf16[4,256,576]{1,2,0:T(8,128)(2,1)S(1)}, u32[]{:S(2)}, u32[]{:S(2)}) async-start(bf16[4,256,576]{1,2,0:T(8,128)(2,1)} %copy.62), calls=%async_computation.5 | async-start | bytes 2359296 | tf_op jit(solution)/shard_map/all_to_all | solution.py:178
  314.7 124.1 %reduce-scatter.15.cloned.1.call-start = ((), (), s32[]{:S(2)}) async-start(), calls=%async_computation.20 | async-start | bytes 1327104 | tf_op jit(solution)/shard_map/reduce_scatter | solution.py:400
  317.5 134.0 %reduce-scatter.13.cloned.1.call-start = ((), (), s32[]{:S(2)}) async-start(), calls=%async_computation.19 | async-start | bytes 1327104 | tf_op jit(solution)/shard_map/reduce_scatter | solution.py:400
  335.9 6.9 copy-start.1
  345.2 188.5 %reduce-scatter.11.cloned.1.call-start = ((), (), s32[]{:S(2)}) async-start(), calls=%async_computation.18 | async-start | bytes 3981312 | tf_op jit(solution)/shard_map/reduce_scatter | solution.py:400
  348.4 284.4 %reduce-scatter.23.cloned.1.call-start = ((), (), s32[]{:S(2)}) async-start(), calls=%async_computation.24 | async-start | bytes 5308416 | tf_op jit(solution)/shard_map/reduce_scatter | solution.py:400
  355.8 375.8 %reduce-scatter.19.cloned.1.call-start = ((), (), s32[]{:S(2)}) async-start(), calls=%async_computation.22 | async-start | bytes 5308416 | tf_op jit(solution)/shard_map/reduce_scatter | solution.py:400
  361.6 452.6 %reduce-scatter.9.cloned.1.call-start = ((), (), s32[]{:S(2)}) async-start(), calls=%async_computation.17 | async-start | bytes 3981312 | tf_op jit(solution)/shard_map/reduce_scatter | solution.py:400
  389.0 21.8 %copy-start.8 = (bf16[128,768]{1,0:T(8,128)(2,1)S(1)}, bf16[128,768]{1,0:T(8,128)(2,1)}, u32[]{:S(2)}) copy-start(bf16[128,768]{1,0:T(8,128)(2,1)} %copy-done.7) | copy-start | bytes 589828
  389.0 21.8 %copy-start.10 = (bf16[128,768]{1,0:T(8,128)(2,1)S(1)}, bf16[128,768]{1,0:T(8,128)(2,1)}, u32[]{:S(2)}) copy-start(bf16[128,768]{1,0:T(8,128)(2,1)} %copy-done.9) | copy-start | bytes 589828
  389.0 21.8 %copy-start.32 = (f32[768]{0:T(1024)S(1)}, f32[768]{0:T(1024)}, u32[]{:S(2)}) copy-start(f32[768]{0:T(1024)} %copy-done.31) | copy-start | bytes 9220
  389.0 21.8 %copy-start.41 = (f32[256]{0:T(256)S(1)}, f32[256]{0:T(256)}, u32[]{:S(2)}) copy-start(f32[256]{0:T(256)} %copy-done.40) | copy-start | bytes 3076
  414.6 498.5 %reduce-scatter.17.cloned.1.call-start = ((), (), s32[]{:S(2)}) async-start(), calls=%async_computation.21 | async-start | bytes 5308416 | tf_op jit(solution)/shard_map/reduce_scatter | solution.py:400
  420.7 591.4 %reduce-scatter.21.cloned.1.call-start = ((), (), s32[]{:S(2)}) async-start(), calls=%async_computation.23 | async-start | bytes 5308416 | tf_op jit(solution)/shard_map/reduce_scatter | solution.py:400
  427.2 597.1 %all-reduce.5.cloned.1.call-start = ((), (), s32[]{:S(2)}) async-start(), calls=%async_computation.16 | async-start | bytes 147456 | tf_op jit(solution)/shard_map/psum | solution.py:531
  445.8 726.9 %all-reduce.7.cloned.1.call-start = ((), (), s32[]{:S(2)}) async-start(), calls=%async_computation.25 | async-start | bytes 15335424 | tf_op jit(solution)/shard_map/psum | solution.py:399
  1015.0 7.6 copy-start.2
  1015.0 7.6 copy-start.4
  1015.0 7.7 copy-start.69
  1020.4 7.8 collective-permute-start.3
  1021.9 6.3 collective-permute-start.2
  1023.1 7.3 collective-permute-start.7
  1023.7 6.7 collective-permute-start.6
  (70 other events, 222.9 us)
Sparse Core Ops, SparseCore 0:
  318.9 65.3 reduce-scatter.14
  387.7 63.7 reduce-scatter.12
  455.1 78.5 reduce-scatter.10
  537.2 95.5 reduce-scatter.22
  636.3 95.2 reduce-scatter.18
  735.1 79.0 reduce-scatter.8
  817.9 95.2 reduce-scatter.16
  916.8 95.2 reduce-scatter.20
Sparse Core Ops, SparseCore 1:
  445.9 146.2 all-reduce.4
  1014.4 158.3 all-reduce.6

commit v3 on v2

--- a/solution.py
+++ b/solution.py
@@ -394,13 +394,330 @@
     return [whole[1 + 3 * n : 4 + 3 * n] for n in range(layers)], out
 
 
-def reduce_weights(place, grads):
-    return [
-        lax.psum(
-            lax.psum_scatter(g, "shard", scatter_dimension=0, tiled=True).astype(F32), "replica"
+class Copies:
+    def __init__(self, send_sems, recv_sems):
+        self.send_sems, self.recv_sems, self.started = send_sems, recv_sems, []
+
+    def send(self, source, target, device):
+        at = len(self.started)
+        copy = pltpu.make_async_remote_copy(
+            src_ref=source,
+            dst_ref=target,
+            send_sem=self.send_sems.at[at],
+            recv_sem=self.recv_sems.at[at],
+            device_id=device,
+            device_id_type=MESH,
         )
-        for g in grads
+        copy.start()
+        self.started.append(copy)
+        return copy
+
+    def finish(self):
+        for copy in self.started:
+            copy.wait_send()
+
+
+def by_rows(rows, body):
+    @pl.loop(0, rows // 16)
+    def _(at):
+        body(pl.ds(pl.multiple_of(at * 16, 16), 16))
+
+
+def share_of(kind, grid, rows, cols):
+    if kind == "columns":
+        return rows, cols // grid.xs
+    if kind == "rows":
+        return rows // grid.xs, cols
+    return rows, cols
+
+
+def x_window(kind, ref, shape, x_at):
+    rows, cols = shape
+    lead = (slice(None),) * (len(ref.shape) - 2)
+    if kind == "columns":
+        return ref.at[lead + (slice(None), pl.ds(pl.multiple_of(x_at * cols, 128), cols))]
+    return ref.at[lead + (pl.ds(pl.multiple_of(x_at * rows, 16), rows), slice(None))]
+
+
+def reduce_kernel(replicas, shards, jobs, *refs):
+    kinds = [kind for kind, _, _ in jobs]
+    count = len(jobs)
+    outputs = 1 + max(out for _, out, _ in jobs)
+    grid = Grid(replicas, shards)
+    zs, ys, xs = grid.zs, grid.ys, grid.xs
+    refs = list(refs)
+
+    def take(number):
+        taken = refs[:number]
+        del refs[:number]
+        return taken
+
+    grads, (vec_ref,), outs, (vec_out,) = take(count), take(1), take(outputs), take(1)
+    own, got, x_got, y_got, z_got, x_sum, done = (take(count) for _ in range(7))
+    vec_got, vec_sum, send_sems, recv_sems, own_sems = refs
+    copies = Copies(send_sems, recv_sems)
+    r, s = lax.axis_index("replica"), lax.axis_index("shard")
+    halves = [(g.shape[1], g.shape[2] // grid.cores) for g in grads]
+    shares = [share_of(kind, grid, *half) for kind, half in zip(kinds, halves)]
+
+    barrier = pltpu.get_barrier_semaphore()
+    for step in range(1, shards):
+        peer = {"replica": r, "shard": lax.rem(s + step, shards)}
+        pl.semaphore_signal(barrier, 1, device_id=peer, device_id_type=MESH)
+    for step in range(1, replicas):
+        peer = {"replica": lax.rem(r + step, replicas), "shard": s}
+        pl.semaphore_signal(barrier, 1, device_id=peer, device_id_type=MESH)
+    pl.semaphore_wait(barrier, shards + replicas - 2)
+
+    def target_z(t):
+        return lax.rem(grid.z + 2 * zs - 1 - t, zs)
+
+    def load(job, t):
+        half = halves[job][1]
+        copy = pltpu.make_async_copy(
+            grads[job].at[
+                pl.ds(target_z(t) * ys, ys),
+                :,
+                pl.ds(pl.multiple_of(grid.core * half, 128), half),
+            ],
+            own[job].at[t % 2],
+            own_sems.at[job, t % 2],
+        )
+        copy.start()
+        return copy
+
+    loads, by_core = {}, {}
+    for t in range(zs):
+        for job in range(count):
+            half = halves[job][1]
+            other = lax.rem(grid.core + 1, grid.cores)
+            by_core[job, t] = copies.send(
+                grads[job].at[
+                    pl.ds(target_z(t) * ys, ys), :, pl.ds(pl.multiple_of(other * half, 128), half)
+                ],
+                got[job].at[t],
+                grid.device(core=1),
+            )
+            if t < 2:
+                loads[job, t] = load(job, t)
+    vec_copies = []
+    for step in range(1, shards):
+        to = lax.rem(s + step, shards)
+        vec_copies.append(
+            copies.send(vec_ref.at[to], vec_got.at[step - 1], {"replica": r, "shard": to})
+        )
+
+    by_x, by_y, by_z = {}, {}, {}
+
+    def base(job, t):
+        return got[job].at[t] if kinds[job] == "half" else x_got[job].at[t, 0]
+
+    def send_y(job, t):
+        for step in range(1, ys):
+            by_y[job, t, step] = copies.send(
+                base(job, t).at[lax.rem(grid.y + step, ys)],
+                y_got[job].at[t, step - 1],
+                grid.device(y=step),
+            )
+
+    for step in range(zs + 4):
+        for job, kind in enumerate(kinds):
+            rows, cols = shares[job]
+            t = step
+            if t < zs:
+                loads[job, t].wait()
+                by_core[job, t].wait_recv()
+                for y in range(ys):
+                    mine, sums = own[job].at[t % 2, y], got[job].at[t, y]
+
+                    def both(at, mine=mine, sums=sums):
+                        sums[at] = (mine[at].astype(F32) + sums[at].astype(F32)).astype(BF16)
+
+                    by_rows(halves[job][0], both)
+                if t + 2 < zs:
+                    loads[job, t + 2] = load(job, t + 2)
+                if kind == "half":
+                    send_y(job, t)
+                else:
+                    for turn in range(1, xs):
+                        by_x[job, t, turn] = copies.send(
+                            x_window(kind, got[job].at[t], shares[job], lax.rem(grid.x + turn, xs)),
+                            x_got[job].at[t, turn - 1],
+                            grid.device(x=turn),
+                        )
+            t = step - 1
+            if 0 <= t < zs and kind != "half":
+                for turn in range(1, xs):
+                    by_x[job, t, turn].wait_recv()
+                for y in range(ys):
+                    mine = x_window(kind, got[job].at[t, y], shares[job], grid.x)
+                    parts = [x_got[job].at[t, turn, y] for turn in range(xs - 1)]
+
+                    def all_x(at, mine=mine, parts=parts):
+                        total = mine[at].astype(F32)
+                        for part in parts:
+                            total += part[at].astype(F32)
+                        parts[0][at] = total.astype(BF16)
+
+                    by_rows(rows, all_x)
+                send_y(job, t)
+            t = step - 2
+            if 0 <= t < zs:
+                for turn in range(1, ys):
+                    by_y[job, t, turn].wait_recv()
+                parts = [y_got[job].at[t, turn] for turn in range(ys - 1)]
+                target = parts[0]
+                if t > 0:
+                    by_z[job, t - 1].wait_recv()
+                    parts.append(z_got[job].at[t - 1])
+                if t == zs - 1:
+                    target = (
+                        x_sum[job].at[grid.x]
+                        if kind == "half"
+                        else x_window(kind, done[job].at[0], shares[job], grid.x)
+                    )
+                mine = base(job, t).at[grid.y]
+
+                def all_y(at, mine=mine, parts=parts, target=target):
+                    total = mine[at].astype(F32)
+                    for part in parts:
+                        total += part[at].astype(F32)
+                    target[at] = total.astype(BF16)
+
+                by_rows(rows, all_y)
+                if t < zs - 1:
+                    by_z[job, t] = copies.send(target, z_got[job].at[t], grid.device(z=1))
+                else:
+                    for turn in range(1, xs):
+                        by_x[job, "done", turn] = copies.send(target, target, grid.device(x=turn))
+            if step == zs + 2:
+                for turn in range(1, xs):
+                    by_x[job, "done", turn].wait_recv()
+                if kind == "half":
+                    sums, target = x_sum[job], done[job].at[0]
+
+                    def across(at, sums=sums, target=target):
+                        total = sums[0, at].astype(F32)
+                        for x_at in range(1, xs):
+                            total += sums[x_at, at].astype(F32)
+                        target[at] = total.astype(BF16)
+
+                    by_rows(rows, across)
+                by_core[job, "done"] = copies.send(
+                    done[job].at[0], done[job].at[1], grid.device(core=1)
+                )
+            if step == zs + 3:
+                by_core[job, "done"].wait_recv()
+                half_rows, half = halves[job]
+                _, out, layer = jobs[job]
+                for side in range(2):
+                    column = lax.rem(grid.core + side, 2) * half
+                    place = outs[out].at[layer, :, pl.ds(pl.multiple_of(column, 128), half)]
+
+                    def write(at, place=place, source=done[job].at[side]):
+                        place[at] = source[at].astype(F32)
+
+                    by_rows(half_rows, write)
+
+        if step == zs + 1:
+            total = vec_ref[s]
+            for copy in vec_copies:
+                copy.wait_recv()
+            for at in range(shards - 1):
+                total += vec_got[at]
+            vec_sum[r] = total
+            vec_copies = [
+                copies.send(
+                    vec_sum.at[r],
+                    vec_sum.at[r],
+                    {"replica": lax.rem(r + turn, replicas), "shard": s},
+                )
+                for turn in range(1, replicas)
+            ]
+        if step == zs + 3:
+            for copy in vec_copies:
+                copy.wait_recv()
+            total = vec_sum[0]
+            for at in range(1, replicas):
+                total += vec_sum[at]
+            vec_out[...] = total
+    copies.finish()
+
+
+def reduce_all(place, grads, vectors):
+    grid = Grid(place.replicas, place.shards)
+    zs, ys, xs = grid.zs, grid.ys, grid.xs
+    layers, members = len(grads), len(grads[0])
+    jobs, arrays = [], []
+    for layer in reversed(range(layers)):
+        for out, (kind, value) in enumerate(grads[layer]):
+            jobs.append((kind, out, layer))
+            arrays.append(value.reshape(place.shards, -1, value.shape[1]))
+    own, got, x_got, y_got, z_got, x_sum, done = ([] for _ in range(7))
+    copies = (place.shards - 1) + (place.replicas - 1)
+    for (kind, _, _), value in zip(jobs, arrays):
+        rows, half = value.shape[1], value.shape[2] // grid.cores
+        share = share_of(kind, grid, rows, half)
+        split = kind != "half"
+        tiny = (16, 128)
+        own.append(pltpu.VMEM((2, ys, rows, half), BF16))
+        got.append(pltpu.VMEM((zs, ys, rows, half), BF16))
+        x_got.append(pltpu.VMEM((zs, xs - 1, ys) + share if split else tiny, BF16))
+        y_got.append(pltpu.VMEM((zs, ys - 1) + share, BF16))
+        z_got.append(pltpu.VMEM((zs - 1,) + share, BF16))
+        x_sum.append(pltpu.VMEM(tiny if split else (xs,) + share, BF16))
+        done.append(pltpu.VMEM((2, rows, half), BF16))
+        copies += zs + (zs * (xs - 1) if split else 0) + zs * (ys - 1) + (zs - 1) + (xs - 1) + 1
+    shapes = [
+        jax.ShapeDtypeStruct((layers, arrays[m].shape[1], arrays[m].shape[2]), F32)
+        for m in range(members)
     ]
+    vec = vectors.shape[1:]
+    return pl.pallas_call(
+        functools.partial(reduce_kernel, place.replicas, place.shards, tuple(jobs)),
+        out_shape=shapes + [jax.ShapeDtypeStruct(vec, F32)],
+        in_specs=[pl.BlockSpec(memory_space=pl.ANY)] * len(arrays)
+        + [pl.BlockSpec(memory_space=pltpu.VMEM)],
+        out_specs=[pl.BlockSpec(memory_space=pltpu.VMEM)] * (members + 1),
+        scratch_shapes=own
+        + got
+        + x_got
+        + y_got
+        + z_got
+        + x_sum
+        + done
+        + [
+            pltpu.VMEM((place.shards - 1,) + vec, F32),
+            pltpu.VMEM((place.replicas,) + vec, F32),
+            pltpu.SemaphoreType.DMA((copies,)),
+            pltpu.SemaphoreType.DMA((copies,)),
+            pltpu.SemaphoreType.DMA((len(jobs), 2)),
+        ],
+        compiler_params=pltpu.CompilerParams(
+            collective_id=1, has_side_effects=True, vmem_limit_bytes=60 * 1024 * 1024
+        ),
+        name="reduce_all",
+    )(*arrays, vectors)
+
+
+def pack_vectors(place, by_layer):
+    sizes = [vector.shape[0] // place.shards for vector in by_layer[0]]
+    packed = jnp.concatenate(
+        [vector.reshape(place.shards, -1) for vectors in by_layer for vector in vectors], 1
+    )
+    size = packed.shape[1]
+    lanes = 128 * -(-size // (16 * 128))
+    packed = jnp.pad(packed, ((0, 0), (0, 16 * lanes - size)))
+    return packed.reshape(place.shards, 16, lanes), sizes
+
+
+def unpack_vectors(summed, layers, sizes):
+    flat = summed.reshape(-1)[: layers * sum(sizes)].reshape(layers, -1)
+    out, start = [], 0
+    for size in sizes:
+        out.append(flat[:, start : start + size])
+        start += size
+    return out
 
 
 def forward_block(place, current, weights, vectors):
@@ -520,20 +837,12 @@
         grad_now, local, vector_grads[n] = backward_block(
             place, grad_now, weights[n], layer_vectors(n), saved[n]
         )
-        weight_grads[n] = reduce_weights(place, local)
+        weight_grads[n] = list(zip(("half", "half", "columns", "rows"), local))
     grad_tokens = place.from_sequences(grad_now.astype(BF16)).astype(F32)
-    grad_mix, grad_out, grad_up, grad_down = (
-        jnp.stack([weight_grads[n][m] for n in range(layers)]) for m in range(4)
-    )
+    packed, sizes = pack_vectors(place, vector_grads)
+    grad_mix, grad_out, grad_up, grad_down, summed = reduce_all(place, weight_grads, packed)
     grad_mix = place.unmix_columns(grad_mix)
-    sizes = [v.shape[0] for v in vector_grads[0]]
-    packed = jnp.stack([jnp.concatenate(v) for v in vector_grads])
-    packed = lax.psum(packed, BOTH)
-    own, start = [], 0
-    for size in sizes:
-        part = size // place.shards
-        own.append(lax.dynamic_slice_in_dim(packed, start + place.s * part, part, 1))
-        start += size
+    own = unpack_vectors(summed, layers, sizes)
     (
         grad_gain_one,
         grad_shift_one,

time: 1200 us -> 606 us (0.51)
  waiting for transfers between devices: 756 us -> 53.4 us
  Pallas kernels: 176 us -> 327 us
  blocking collectives: 39.1 us -> 0 us
  starting transfers between devices: 27.1 us -> 45.6 us
  between operations: 17.5 us -> 2.33 us
  other arithmetic: 28.5 us -> 15.6 us
    reduce_scatter x8 -> x0, waiting for transfers between devices: 553 us -> none  [reduce_weights(): lax.psum_scatter(g, 'shard', scatter_dimension=0, tiled=True).astype(F32)]
    pallas_call x0 -> x1, Pallas kernels: none -> 153 us  [reduce_all(): pl.pallas_call(functools.partial(reduce_kernel, place.replicas, place.sha...]
    psum x2 -> x0, waiting for transfers between devices: 140 us -> none  [the longest x1 140 us: reduce_weights(): lax.psum(lax.psum_scatter(g, 'shard', scatter_dimension=0, tiled=True).as...]
    all_to_all x3 -> x0, blocking collectives: 39.1 us -> none  [the longest x2 19.8 us: to_heads(): return lax.all_to_all(values, 'replica', 1, 0, tiled=True)]
    another operation x10 -> x0, other arithmetic: 16.8 us -> none  [the longest x9 16.1 us: per_device(): jnp.stack([weight_grads[n][m] for n in range(layers)])]
    reshape x0 -> x19, local copies, waits for them, and re-layouts: none -> 14.1 us  [the longest x18 13.4 us: pack_vectors(): vector.reshape(place.shards, -1)]
    all_to_all x2 -> x4, waiting for transfers between devices: 35.8 us -> 34.2 us  [to_heads(): return lax.all_to_all(values, 'replica', 1, 0, tiled=True)]
  transfers between devices with their start and end apart: 23 -> 16, of which waited for: 15 -> 6; matrix products, arithmetic and copies ran while one was open for 10% -> 19% of each run, Pallas kernels for 13% -> 53%
where the time goes in v3:
time: 606 us; the launch traced here: 596 us
  Pallas kernels  327 us (54%)
  local copies, waits for them, and re-layouts  76.7 us (13%)
  matrix products  75.8 us (13%)
  waiting for transfers between devices  53.4 us (9%)
  starting transfers between devices  45.6 us (8%)
  other arithmetic  15.6 us (3%)
    pallas_call x1, Pallas kernels, reduce_all(): pl.pallas_call(functools.partial(reduce_kernel, place.replicas, place.sha...  153 us
    pallas_call x1, Pallas kernels, gather_shards(): pl.pallas_call(functools.partial(gather_kernel, place.replicas, place.sha...  125 us
    dot_general x24, matrix products, dot(): lax.dot_general(a, b, (contract, ((), ())), preferred_element_type=F32)  75.8 us
    all_to_all x4, waiting for transfers between devices, to_heads(): return lax.all_to_all(values, 'replica', 1, 0, tiled=True)  34.2 us
    pallas_call x2, Pallas kernels, attend_back(): pl.pallas_call(attend_back_kernel, out_shape=jax.ShapeDtypeStruct((length...  28.7 us
    pallas_call x2, Pallas kernels, attend(): pl.pallas_call(attend_kernel, out_shape=jax.ShapeDtypeStruct((length, hea...  19.6 us
    all_to_all x4, waiting for transfers between devices, to_rows(): return lax.all_to_all(values, 'replica', 0, 1, tiled=True)  19.2 us
    all_to_all x4, starting transfers between devices, to_rows(): return lax.all_to_all(values, 'replica', 0, 1, tiled=True)  17.2 us
  transfers between devices with their start and end apart: 16, of which 6 were waited for; matrix products, arithmetic and copies ran while one was open for 19% of the time, Pallas kernels for 53%

profile of v3, /device:TPU:0, one launch (start us, length us, event | category | flops | bytes accessed | tf_op | source)
XLA Modules:
  0.0 595.9 jit_solution(567790647072570150)
XLA Ops:
  2.5 3.0 collective-permute-start.1
  5.5 3.0 collective-permute-start
  10.0 3.0 reshape.397
  18.6 125.3 %gather_shards.1 = (bf16[128,256]{1,0:T(8,128)(2,1)}, bf16[768,3072]{1,0:T(8,128)(2,1)}, bf16[768,3072]{1,0:T(8,128)(2,1)}, bf16[3072,768]{1,0:T(8,128)(2,1)}, b...) custom-call(bf16[16,256]{1,0:T(8,128)(2,1)} %reshape.396.refs_0_, ...), custom_call_target="tpu_custom_call" | custom-call | tf_op jit(solution)/shard_map/gather_shards/pallas_call | solution.py:359
  147.1 3.2 fusion
  151.8 3.5 all-to-all-start
  157.2 14.4 %all-to-all-done = bf16[256,4,576]{0,2,1:T(8,128)(2,1)S(1)} async-done(((bf16[256,4,576]{0,2,1:T(8,128)(2,1)}), bf16[256,4,576]{0,2,1:T(8,128)(2,1)S(1)}, u32[]{:S(2)}, u32[]{:S(2)}) %all-to-all-start) | async-done | bytes 1179680 | tf_op jit(solution)/shard_map/all_to_all | solution.py:175
  173.0 9.8 %attend.2 = bf16[1024,192]{1,0:T(8,128)(2,1)} custom-call(bf16[1024,576]{1,0:T(8,128)(2,1)} %bitcast.147), custom_call_target="tpu_custom_call" | custom-call | tf_op jit(solution)/shard_map/attend/pallas_call | solution.py:70
  184.8 3.7 all-to-all-start.1
  190.2 5.6 all-to-all-done.1
  195.8 2.0 fusion.87
  198.2 4.0 convolution_add_fusion.3
  202.2 2.1 fusion.88
  207.8 3.5 all-to-all-start.2
  213.7 19.8 %all-to-all-done.2 = bf16[256,4,576]{0,2,1:T(8,128)(2,1)S(1)} async-done(((bf16[256,4,576]{0,2,1:T(8,128)(2,1)}), bf16[256,4,576]{0,2,1:T(8,128)(2,1)S(1)}, u32[]{:S(2)}, u32[]{:S(2)}) %all-to-all-start.2) | async-done | bytes 1179680 | tf_op jit(solution)/shard_map/all_to_all | solution.py:175
  235.0 9.8 %attend.3 = bf16[1024,192]{1,0:T(8,128)(2,1)} custom-call(bf16[1024,576]{1,0:T(8,128)(2,1)} %bitcast.149), custom_call_target="tpu_custom_call" | custom-call | tf_op jit(solution)/shard_map/attend/pallas_call | solution.py:70
  246.8 4.1 all-to-all-start.3
  258.2 2.0 fusion.89
  260.5 3.9 convolution_add_fusion.2
  264.5 2.7 fusion.26
  267.2 4.6 convert_reduce_fusion
  271.8 2.1 multiply_reduce_fusion
  275.9 2.5 convolution_convert_fusion.9
  280.3 4.1 all-to-all-start.4
  290.3 3.0 collective-permute-start.2
  294.7 2.5 convolution_convert_fusion.7
  299.1 14.4 %attend_back.2 = bf16[1024,576]{1,0:T(8,128)(2,1)} custom-call(bf16[1024,576]{1,0:T(8,128)(2,1)} %bitcast.150, bf16[1024,192]{1,0:T(8,128)(2,1)} %bitcast.170), custom_call_target="tpu_custom_call" | custom-call | tf_op jit(solution)/shard_map/attend_back/pallas_call | solution.py:113
  313.5 2.4 copy.61
  315.9 5.9 all-to-all-start.5
  321.9 5.3 convolution_convert_fusion.4
  327.2 4.4 convolution_convert_fusion.3
  331.6 6.6 %all-to-all-done.5 = bf16[4,256,576]{1,2,0:T(8,128)(2,1)S(1)} async-done(((bf16[4,256,576]{1,2,0:T(8,128)(2,1)}), bf16[4,256,576]{1,2,0:T(8,128)(2,1)S(1)}, u32[]{:S(2)}, u32[]{:S(2)}) %all-to-all-start.5) | async-done | bytes 1179680 | tf_op jit(solution)/shard_map/all_to_all | solution.py:178
  338.2 4.1 multiply_reduce_fusion.1
  342.3 3.1 convolution_convert_fusion.5
  347.3 3.7 convert_reduce_fusion.1
  351.1 2.3 multiply_reduce_fusion.2
  359.8 3.7 all-to-all-start.6
  372.6 14.4 %attend_back.3 = bf16[1024,576]{1,0:T(8,128)(2,1)} custom-call(bf16[1024,576]{1,0:T(8,128)(2,1)} %bitcast.148, bf16[1024,192]{1,0:T(8,128)(2,1)} %bitcast.171), custom_call_target="tpu_custom_call" | custom-call | tf_op jit(solution)/shard_map/attend_back/pallas_call | solution.py:113
  386.9 2.4 copy.64
  389.3 3.5 all-to-all-start.7
  392.9 5.3 convolution_convert_fusion.1
  398.3 4.5 convolution_convert_fusion
  402.8 5.9 all-to-all-done.7
  408.7 4.0 fusion.72
  412.8 3.1 convolution_convert_fusion.2
  425.6 152.9 %reduce_all.1 = (f32[2,96,2304]{2,1,0:T(8,128)}, f32[2,96,768]{2,1,0:T(8,128)}, f32[2,96,3072]{2,1,0:T(8,128)}, f32[2,384,768]{2,1,0:T(8,128)}, f32[16,256]{1,0:T(8,128)}) custom-call(bf16[8,96,2304]{2,1,0:T(8,128)(2,1)} %bitcast.146, bf16[8,96,768]{2,1,0:T(8,128)(2,1)} %bitcast.158, bf16[8,96,3072]{2,1,0:T(8,128)(2,1)} %bitcast.143, ...), custom_call_target="tpu_custom_call" | custom-call | tf_op jit(solution)/shard_map/reduce_all/pallas_call | solution.py:676
  581.8 2.5 copy.66
  584.4 3.7 reshape_reshape.2
  (324 shorter events, 88.4 us)
Async XLA Ops:
  2.5 143.0 %collective-permute-start.1 = (bf16[128,768]{1,0:T(8,128)(2,1)}, bf16[128,768]{1,0:T(8,128)(2,1)}, u32[]{:S(2)}, u32[]{:S(2)}) collective-permute-start(bf16[128,768]{1,0:T(8,128)(2,1)} %get-tuple-element.89), channel_id=1, source_target_pairs={{0,1},{1,0},{2,9},{3,8},{4,17},{5,16},{6,25},{7,24},{8,3},{9,2},{1... | collective-permute-start | bytes 589832 | tf_op jit(solution)/shard_map/ppermute | solution.py:145
  5.5 140.0 %collective-permute-start = (bf16[128,768]{1,0:T(8,128)(2,1)}, bf16[128,768]{1,0:T(8,128)(2,1)}, u32[]{:S(2)}, u32[]{:S(2)}) collective-permute-start(bf16[128,768]{1,0:T(8,128)(2,1)} %get-tuple-element.90), channel_id=1, source_target_pairs={{0,0},{1,1},{2,8},{3,9},{4,16},{5,17},{6,24},{7,25},{8,2},{9,3},{1... | collective-permute-start | bytes 589832 | tf_op jit(solution)/shard_map/ppermute | solution.py:145
  146.7 49.2 %copy-start.6 = (bf16[128,768]{1,0:T(8,128)(2,1)}, bf16[128,768]{1,0:T(8,128)(2,1)S(1)}, u32[]{:S(2)}) copy-start(bf16[128,768]{1,0:T(8,128)(2,1)S(1)} %get-tuple-element.87) | copy-start | bytes 589828
  146.7 49.2 %copy-start.8 = (bf16[128,768]{1,0:T(8,128)(2,1)}, bf16[128,768]{1,0:T(8,128)(2,1)S(1)}, u32[]{:S(2)}) copy-start(bf16[128,768]{1,0:T(8,128)(2,1)S(1)} %get-tuple-element.88) | copy-start | bytes 589828
  151.8 19.8 %all-to-all-start = ((bf16[256,4,576]{0,2,1:T(8,128)(2,1)}), bf16[256,4,576]{0,2,1:T(8,128)(2,1)S(1)}, u32[]{:S(2)}, u32[]{:S(2)}) async-start(bf16[256,4,576]{0,2,1:T(8,128)(2,1)} %bitcast.20), calls=%async_computation | async-start | bytes 2359296 | tf_op jit(solution)/shard_map/all_to_all | solution.py:175
  184.8 11.0 %all-to-all-start.1 = ((bf16[4,256,192]{1,2,0:T(8,128)(2,1)}), bf16[4,256,192]{1,2,0:T(8,128)(2,1)S(1)}, u32[]{:S(2)}, u32[]{:S(2)}) async-start(bf16[4,256,192]{1,2,0:T(8,128)(2,1)} %copy.55), calls=%async_computation.1 | async-start | bytes 786432 | tf_op jit(solution)/shard_map/all_to_all | solution.py:178
  189.3 12.8 %copy-start.32 = (f32[768]{0:T(1024)}, f32[768]{0:T(1024)S(1)}, u32[]{:S(2)}) copy-start(f32[768]{0:T(1024)S(1)} %add.288) | copy-start | bytes 9220
  190.0 14.5 %copy-start.34 = (f32[768]{0:T(1024)}, f32[768]{0:T(1024)S(1)}, u32[]{:S(2)}) copy-start(f32[768]{0:T(1024)S(1)} %add.301) | copy-start | bytes 9220
  195.8 6.3 %copy-start.20 = (bf16[4,256,192]{1,2,0:T(8,128)(2,1)}, bf16[4,256,192]{1,2,0:T(8,128)(2,1)S(1)}, u32[]{:S(2)}) copy-start(bf16[4,256,192]{1,2,0:T(8,128)(2,1)S(1)} %all-to-all-done.1) | copy-start | bytes 1179652
  198.1 7.0 %slice-start = ((s8[4718592]{0:T(1024)(128)(4,1)}), s8[4194304]{0:T(1024)(128)(4,1)S(1)}, s32[]{:S(2)}) async-start(s8[4718592]{0:T(1024)(128)(4,1)} %bitcast.180), calls=%async_computation.8 | async-start | bytes 8388608
  207.8 25.8 %all-to-all-start.2 = ((bf16[256,4,576]{0,2,1:T(8,128)(2,1)}), bf16[256,4,576]{0,2,1:T(8,128)(2,1)S(1)}, u32[]{:S(2)}, u32[]{:S(2)}) async-start(bf16[256,4,576]{0,2,1:T(8,128)(2,1)} %bitcast.164), calls=%async_computation.2 | async-start | bytes 2359296 | tf_op jit(solution)/shard_map/all_to_all | solution.py:175
  212.1 44.9 %collective-permute-start.5 = (bf16[128,768]{1,0:T(8,128)(2,1)}, bf16[128,768]{1,0:T(8,128)(2,1)S(1)}, u32[]{:S(2)}, u32[]{:S(2)}) collective-permute-start(bf16[128,768]{1,0:T(8,128)(2,1)} %get-tuple-element.81), channel_id=1, source_target_pairs={{0,1},{1,0},{2,9},{3,8},{4,17},{5,16},{6,25},{7,24},{8,3},{9,2},{1... | collective-permute-start | bytes 589832 | tf_op jit(solution)/shard_map/ppermute | solution.py:145
  212.2 44.8 %collective-permute-start.4 = (bf16[128,768]{1,0:T(8,128)(2,1)}, bf16[128,768]{1,0:T(8,128)(2,1)S(1)}, u32[]{:S(2)}, u32[]{:S(2)}) collective-permute-start(bf16[128,768]{1,0:T(8,128)(2,1)} %get-tuple-element.82), channel_id=1, source_target_pairs={{0,0},{1,1},{2,8},{3,9},{4,16},{5,17},{6,24},{7,25},{8,2},{9,3},{1... | collective-permute-start | bytes 589832 | tf_op jit(solution)/shard_map/ppermute | solution.py:145
  246.8 11.4 %all-to-all-start.3 = ((bf16[4,256,192]{1,2,0:T(8,128)(2,1)}), bf16[4,256,192]{1,2,0:T(8,128)(2,1)S(1)}, u32[]{:S(2)}, u32[]{:S(2)}) async-start(bf16[4,256,192]{1,2,0:T(8,128)(2,1)} %copy.58), calls=%async_computation.3 | async-start | bytes 786432 | tf_op jit(solution)/shard_map/all_to_all | solution.py:178
  257.1 10.0 %copy-start.12 = (bf16[128,768]{1,0:T(8,128)(2,1)}, bf16[128,768]{1,0:T(8,128)(2,1)S(1)}, u32[]{:S(2)}) copy-start(bf16[128,768]{1,0:T(8,128)(2,1)S(1)} %get-tuple-element.79) | copy-start | bytes 589828
  257.1 10.0 %copy-start.16 = (bf16[128,768]{1,0:T(8,128)(2,1)}, bf16[128,768]{1,0:T(8,128)(2,1)S(1)}, u32[]{:S(2)}) copy-start(bf16[128,768]{1,0:T(8,128)(2,1)S(1)} %get-tuple-element.80) | copy-start | bytes 589828
  258.2 6.2 %slice-start.10 = ((s8[4718592]{0:T(1024)(128)(4,1)}), s8[4194304]{0:T(1024)(128)(4,1)S(1)}, s32[]{:S(2)}) async-start(s8[4718592]{0:T(1024)(128)(4,1)} %bitcast.199), calls=%async_computation.18 | async-start | bytes 8388608
  260.2 13.7 %copy-start.46 = (f32[256]{0:T(256)}, f32[256]{0:T(256)S(1)}, u32[]{:S(2)}) copy-start(f32[256]{0:T(256)S(1)} %broadcast_multiply_fusion) | copy-start | bytes 3076
  260.5 13.5 %copy-start.54 = (f32[256]{0:T(256)}, f32[256]{0:T(256)S(1)}, u32[]{:S(2)}) copy-start(f32[256]{0:T(256)S(1)} %fusion.62) | copy-start | bytes 3076
  264.4 7.3 %slice-start.8 = ((s8[4718592]{0:T(1024)(128)(4,1)}), s8[4194304]{0:T(1024)(128)(4,1)S(1)}, s32[]{:S(2)}) async-start(s8[4718592]{0:T(1024)(128)(4,1)} %bitcast.197), calls=%async_computation.16 | async-start | bytes 8388608
  274.3 12.0 %copy-start.4 = (f32[256,768]{1,0:T(8,128)}, f32[256,768]{1,0:T(8,128)S(1)}, u32[]{:S(2)}) copy-start(f32[256,768]{1,0:T(8,128)S(1)} %get-tuple-element.67) | copy-start | bytes 2359300
  280.3 16.8 %all-to-all-start.4 = ((bf16[256,4,192]{0,2,1:T(8,128)(2,1)}), bf16[256,4,192]{0,2,1:T(8,128)(2,1)}, u32[]{:S(2)}, u32[]{:S(2)}) async-start(bf16[256,4,192]{0,2,1:T(8,128)(2,1)} %bitcast.173), calls=%async_computation.4 | async-start | bytes 786432 | tf_op jit(solution)/shard_map/all_to_all | solution.py:175
  290.3 298.5 %collective-permute-start.3 = (bf16[128,768]{1,0:T(8,128)(2,1)}, bf16[128,768]{1,0:T(8,128)(2,1)}, u32[]{:S(2)}, u32[]{:S(2)}) collective-permute-start(bf16[128,768]{1,0:T(8,128)(2,1)} %get-tuple-element.85), channel_id=1, source_target_pairs={{1,0},{0,1},{9,2},{8,3},{17,4},{16,5},{25,6},{24,7},{3,8},{2,9},{1... | collective-permute-start | bytes 589832 | tf_op jit(solution)/shard_map/ppermute | solution.py:165
  290.3 298.4 %collective-permute-start.2 = (bf16[128,768]{1,0:T(8,128)(2,1)}, bf16[128,768]{1,0:T(8,128)(2,1)}, u32[]{:S(2)}, u32[]{:S(2)}) collective-permute-start(bf16[128,768]{1,0:T(8,128)(2,1)} %get-tuple-element.86), channel_id=1, source_target_pairs={{0,0},{1,1},{8,2},{9,3},{16,4},{17,5},{24,6},{25,7},{2,8},{3,9},{1... | collective-permute-start | bytes 589832 | tf_op jit(solution)/shard_map/ppermute | solution.py:165
  315.9 22.3 %all-to-all-start.5 = ((bf16[4,256,576]{1,2,0:T(8,128)(2,1)}), bf16[4,256,576]{1,2,0:T(8,128)(2,1)S(1)}, u32[]{:S(2)}, u32[]{:S(2)}) async-start(bf16[4,256,576]{1,2,0:T(8,128)(2,1)} %copy.61), calls=%async_computation.5 | async-start | bytes 2359296 | tf_op jit(solution)/shard_map/all_to_all | solution.py:178
  327.2 11.0 %copy-start.45 = (f32[256]{0:T(256)S(1)}, f32[256]{0:T(256)}, u32[]{:S(2)}) copy-start(f32[256]{0:T(256)} %copy-done.44) | copy-start | bytes 3076
  327.2 11.0 %copy-start.52 = (f32[256]{0:T(256)S(1)}, f32[256]{0:T(256)}, u32[]{:S(2)}) copy-start(f32[256]{0:T(256)} %copy-done.51) | copy-start | bytes 3076
  338.2 8.5 %slice-start.6 = ((s8[4718592]{0:T(1024)(128)(4,1)}), s8[4194304]{0:T(1024)(128)(4,1)S(1)}, s32[]{:S(2)}) async-start(s8[4718592]{0:T(1024)(128)(4,1)} %bitcast.195), calls=%async_computation.14 | async-start | bytes 8388608
  346.7 9.6 %copy-start = (f32[256,768]{1,0:T(8,128)}, f32[256,768]{1,0:T(8,128)S(1)}, u32[]{:S(2)}) copy-start(f32[256,768]{1,0:T(8,128)S(1)} %get-tuple-element.59) | copy-start | bytes 2359300
  353.7 6.1 %copy-start.2 = (f32[256,768]{1,0:T(8,128)}, f32[256,768]{1,0:T(8,128)S(1)}, u32[]{:S(2)}) copy-start(f32[256,768]{1,0:T(8,128)S(1)} %get-tuple-element.63) | copy-start | bytes 2359300
  355.3 8.1 %copy-start.67 = (f32[768]{0:T(1024)S(1)}, f32[768]{0:T(1024)}, u32[]{:S(2)}) copy-start(f32[768]{0:T(1024)} %get-tuple-element.41) | copy-start | bytes 9220
  355.4 8.8 %copy-start.56 = (f32[3072]{0:T(1024)S(1)}, f32[3072]{0:T(1024)}, u32[]{:S(2)}) copy-start(f32[3072]{0:T(1024)} %get-tuple-element.133) | copy-start | bytes 36868
  355.4 9.4 %copy-start.70 = (f32[768]{0:T(1024)S(1)}, f32[768]{0:T(1024)}, u32[]{:S(2)}) copy-start(f32[768]{0:T(1024)} %get-tuple-element.43) | copy-start | bytes 9220
  355.4 10.1 %copy-start.47 = (f32[768]{0:T(1024)S(1)}, f32[768]{0:T(1024)}, u32[]{:S(2)}) copy-start(f32[768]{0:T(1024)} %get-tuple-element.58) | copy-start | bytes 9220
  355.4 11.4 %copy-start.69 = (f32[768]{0:T(1024)S(1)}, f32[768]{0:T(1024)}, u32[]{:S(2)}) copy-start(f32[768]{0:T(1024)} %get-tuple-element.49) | copy-start | bytes 9220
  355.4 12.1 %copy-start.66 = (f32[768]{0:T(1024)S(1)}, f32[768]{0:T(1024)}, u32[]{:S(2)}) copy-start(f32[768]{0:T(1024)} %get-tuple-element.48) | copy-start | bytes 9220
  355.4 14.7 %copy-start.21 = (bf16[4,256,192]{1,2,0:T(8,128)(2,1)S(1)}, bf16[4,256,192]{1,2,0:T(8,128)(2,1)}, u32[]{:S(2)}) copy-start(bf16[4,256,192]{1,2,0:T(8,128)(2,1)} %copy-done.20) | copy-start | bytes 1179652
  359.8 11.8 %all-to-all-start.6 = ((bf16[256,4,192]{0,2,1:T(8,128)(2,1)}), bf16[256,4,192]{0,2,1:T(8,128)(2,1)S(1)}, u32[]{:S(2)}, u32[]{:S(2)}) async-start(bf16[256,4,192]{0,2,1:T(8,128)(2,1)} %bitcast.54), calls=%async_computation.6 | async-start | bytes 786432 | tf_op jit(solution)/shard_map/all_to_all | solution.py:175
  386.9 6.0 copy-start.33
  386.9 6.0 copy-start.50
  389.3 19.3 %all-to-all-start.7 = ((bf16[4,256,576]{1,2,0:T(8,128)(2,1)}), bf16[4,256,576]{1,2,0:T(8,128)(2,1)S(1)}, u32[]{:S(2)}, u32[]{:S(2)}) async-start(bf16[4,256,576]{1,2,0:T(8,128)(2,1)} %copy.64), calls=%async_computation.7 | async-start | bytes 2359296 | tf_op jit(solution)/shard_map/all_to_all | solution.py:178
  398.2 10.4 %copy-start.7 = (bf16[128,768]{1,0:T(8,128)(2,1)S(1)}, bf16[128,768]{1,0:T(8,128)(2,1)}, u32[]{:S(2)}) copy-start(bf16[128,768]{1,0:T(8,128)(2,1)} %copy-done.6) | copy-start | bytes 589828
  398.2 10.4 %copy-start.9 = (bf16[128,768]{1,0:T(8,128)(2,1)S(1)}, bf16[128,768]{1,0:T(8,128)(2,1)}, u32[]{:S(2)}) copy-start(bf16[128,768]{1,0:T(8,128)(2,1)} %copy-done.8) | copy-start | bytes 589828
  398.3 10.4 %copy-start.39 = (f32[256]{0:T(256)S(1)}, f32[256]{0:T(256)}, u32[]{:S(2)}) copy-start(f32[256]{0:T(256)} %copy-done.38) | copy-start | bytes 3076
  412.8 6.0 %copy-start.3 = (f32[256,768]{1,0:T(8,128)S(1)}, f32[256,768]{1,0:T(8,128)}, u32[]{:S(2)}) copy-start(f32[256,768]{1,0:T(8,128)} %copy-done.2) | copy-start | bytes 2359300
  422.7 166.1 %collective-permute-start.7 = (bf16[128,768]{1,0:T(8,128)(2,1)S(1)}, bf16[128,768]{1,0:T(8,128)(2,1)S(1)}, u32[]{:S(2)}, u32[]{:S(2)}) collective-permute-start(bf16[128,768]{1,0:T(8,128)(2,1)S(1)} %get-tuple-element.77), channel_id=1, source_target_pairs={{1,0},{0,1},{9,2},{8,3},{17,4},{16,5},{25,6},{24,7},{3,8},{2,9},{1... | collective-permute-start | bytes 589832 | tf_op jit(solution)/shard_map/ppermute | solution.py:165
  424.7 164.1 %collective-permute-start.6 = (bf16[128,768]{1,0:T(8,128)(2,1)S(1)}, bf16[128,768]{1,0:T(8,128)(2,1)S(1)}, u32[]{:S(2)}, u32[]{:S(2)}) collective-permute-start(bf16[128,768]{1,0:T(8,128)(2,1)S(1)} %get-tuple-element.78), channel_id=1, source_target_pairs={{0,0},{1,1},{8,2},{9,3},{16,4},{17,5},{24,6},{25,7},{2,8},{3,9},{1... | collective-permute-start | bytes 589832 | tf_op jit(solution)/shard_map/ppermute | solution.py:165
  584.4 7.5 %copy-start.27 = (f32[2,96,768]{2,1,0:T(8,128)S(1)}, f32[2,96,768]{2,1,0:T(8,128)}, u32[]{:S(2)}) copy-start(f32[2,96,768]{2,1,0:T(8,128)} %get-tuple-element.161) | copy-start | bytes 1769476
  (56 other events, 193.0 us)

commit v4 on v1

v4 whole, which is shorter than its diff:
```python
import functools

import jax
import jax.numpy as jnp
from jax import lax
from jax.experimental import pallas as pl
from jax.experimental.pallas import tpu as pltpu
from jax.sharding import PartitionSpec as P

HEADS = 12
HEAD_DIM = 64
EPSILON = 1e-05
MASKED = -1e30
F32 = jnp.float32
BF16 = jnp.bfloat16
BOTH = ("replica", "shard")
MESH = pl.DeviceIdType.MESH
VMEM_BLOCK = pl.BlockSpec(memory_space=pltpu.VMEM)
ANY_BLOCK = pl.BlockSpec(memory_space=pl.ANY)


def dot(a, b, contract):
    return lax.dot_general(a, b, (contract, ((), ())), preferred_element_type=F32)


def norm_rows(values, gain, shift):
    centre = values - jnp.mean(values, -1, keepdims=True)
    spread = jnp.mean(centre * centre, -1, keepdims=True)
    return centre * lax.rsqrt(spread + EPSILON) * gain + shift


class Place:
    def __init__(self, replicas, shards):
        self.replicas, self.shards = replicas, shards
        self.cores = 2
        self.xs = replicas // self.cores
        self.zs = 4
        self.ys = shards // self.zs
        assert self.xs * self.cores == replicas and self.zs * self.ys == shards
        self.heads = -(-HEADS // replicas)
        self.padded = self.heads * replicas
        self.span = 3 * self.heads * HEAD_DIM
        self.columns = 128 * -(-self.span // 128)

    def locate(self):
        self.r, self.s = lax.axis_index("replica"), lax.axis_index("shard")
        self.x, self.core = self.r // self.cores, lax.rem(self.r, self.cores)
        self.z, self.y = self.s // self.ys, lax.rem(self.s, self.ys)
        return self

    def device(self, x=0, core=0, z=0, y=0):
        to_x = lax.rem(self.x + x + self.xs, self.xs)
        to_core = lax.rem(self.core + core, self.cores)
        to_z = lax.rem(self.z + z + self.zs, self.zs)
        to_y = lax.rem(self.y + y + self.ys, self.ys)
        return {"replica": to_x * self.cores + to_core, "shard": to_z * self.ys + to_y}

    def block(self, z_back, y_back):
        from_z = lax.rem(self.z - z_back + self.zs, self.zs)
        from_y = lax.rem(self.y - y_back + self.ys, self.ys)
        return from_z * self.ys + from_y

    def turn_pairs(self, turn, held):
        pairs = []
        for r in range(self.replicas):
            for s in range(self.shards):
                target = (s // held) * self.shards + held * r + (s + turn) % held
                pairs.append((r * self.shards + s, target))
        return pairs

    def to_sequences(self, blocks):
        held = blocks.shape[0]
        assert held * self.replicas == self.shards
        got = []
        for turn in range(held):
            block = lax.dynamic_index_in_dim(blocks, (self.s + turn) % held, 0, keepdims=False)
            got.append(lax.ppermute(block, BOTH, self.turn_pairs(turn, held)))
        stacked = jnp.stack(got)
        ordered = [
            lax.dynamic_index_in_dim(stacked, (self.s - u) % held, 0, keepdims=False)
            for u in range(held)
        ]
        return jnp.concatenate(ordered, 0)

    def from_sequences(self, values, held):
        blocks = values.reshape(held, -1, values.shape[-1])
        got = []
        for turn in range(held):
            pairs = [(b, a) for a, b in self.turn_pairs(turn, held)]
            block = lax.dynamic_index_in_dim(blocks, (self.s - turn) % held, 0, keepdims=False)
            got.append(lax.ppermute(block, BOTH, pairs))
        stacked = jnp.stack(got)
        return jnp.stack(
            [
                lax.dynamic_index_in_dim(stacked, (i - self.s) % held, 0, keepdims=False)
                for i in range(held)
            ]
        )

    def mix_columns(self, weight):
        lead = weight.shape[:-1]
        parts = weight.reshape(lead + (3, HEADS, HEAD_DIM))
        extra = [(0, 0)] * len(lead) + [(0, 0), (0, self.padded - HEADS), (0, 0)]
        parts = jnp.pad(parts, extra)
        parts = parts.reshape(lead + (3, self.replicas, self.heads * HEAD_DIM))
        parts = jnp.swapaxes(parts, -3, -2).reshape(lead + (self.replicas, self.span))
        parts = jnp.pad(parts, [(0, 0)] * (len(lead) + 1) + [(0, self.columns - self.span)])
        return parts.reshape(lead + (-1,))

    def unmix_columns(self, values):
        lead = values.shape[:-1]
        parts = values.reshape(lead + (self.replicas, self.columns))[..., : self.span]
        parts = parts.reshape(lead + (self.replicas, 3, self.heads * HEAD_DIM))
        parts = jnp.swapaxes(parts, -3, -2).reshape(lead + (3, self.padded, HEAD_DIM))
        return parts[..., :HEADS, :].reshape(lead + (-1,))


class Copies:
    def __init__(self, send_sems, recv_sems):
        self.send_sems, self.recv_sems, self.started = send_sems, recv_sems, []

    def send(self, source, target, device):
        at = len(self.started)
        copy = pltpu.make_async_remote_copy(
            src_ref=source,
            dst_ref=target,
            send_sem=self.send_sems.at[at],
            recv_sem=self.recv_sems.at[at],
            device_id=device,
            device_id_type=MESH,
        )
        copy.start()
        self.started.append(copy)
        return copy

    def finish(self):
        for copy in self.started:
            copy.wait_send()


class Task:
    def __init__(self, run, inputs, outputs, scratch, copies):
        self.run, self.inputs, self.outputs = run, inputs, outputs
        self.scratch, self.copies = scratch, copies


def fuse(place, name, collective_id, tasks, order):
    sizes = (place.replicas, place.shards)
    count = sum(task.copies for task in tasks)

    def kernel(*refs):
        here = Place(*sizes).locate()
        refs = list(refs)

        def take(number):
            taken = refs[:number]
            del refs[:number]
            return taken

        ins = [take(len(task.inputs)) for task in tasks]
        outs = [take(len(task.outputs)) for task in tasks]
        own = [take(len(task.scratch)) for task in tasks]
        copies = Copies(*refs)
        barrier = pltpu.get_barrier_semaphore()
        for step in range(1, here.shards):
            peer = {"replica": here.r, "shard": lax.rem(here.s + step, here.shards)}
            pl.semaphore_signal(barrier, 1, device_id=peer, device_id_type=MESH)
        for step in range(1, here.replicas):
            peer = {"replica": lax.rem(here.r + step, here.replicas), "shard": here.s}
            pl.semaphore_signal(barrier, 1, device_id=peer, device_id_type=MESH)
        pl.semaphore_wait(barrier, here.shards + here.replicas - 2)
        streams = [
            task.run(here, copies, *group) for task, *group in zip(tasks, ins, outs, own)
        ]
        for at in order:
            next(streams[at], None)
        for stream in streams:
            for _ in stream:
                pass
        copies.finish()

    results = pl.pallas_call(
        kernel,
        out_shape=[shape for task in tasks for shape, _ in task.outputs],
        in_specs=[spec for task in tasks for _, spec in task.inputs],
        out_specs=[spec for task in tasks for _, spec in task.outputs],
        scratch_shapes=[shape for task in tasks for shape in task.scratch]
        + [pltpu.SemaphoreType.DMA((count,)), pltpu.SemaphoreType.DMA((count,))],
        compiler_params=pltpu.CompilerParams(
            collective_id=collective_id,
            has_side_effects=True,
            vmem_limit_bytes=60 * 1024 * 1024,
        ),
        name=name,
    )(*[value for task in tasks for value, _ in task.inputs])
    split, start = [], 0
    for task in tasks:
        split.append(list(results[start : start + len(task.outputs)]))
        start += len(task.outputs)
    return split


def by_rows(rows, body):
    @pl.loop(0, rows // 16)
    def _(at):
        body(pl.ds(pl.multiple_of(at * 16, 16), 16))


def block_probs(q_ref, k_ref, head, first, rows):
    count = first + rows
    query = q_ref[head, first:count, :]
    keys = k_ref[head, 0:count, :]
    scores = dot(query, keys, ((1,), (1,))) * (HEAD_DIM**-0.5)
    row = lax.broadcasted_iota(jnp.int32, (rows, count), 0) + first
    col = lax.broadcasted_iota(jnp.int32, (rows, count), 1)
    scores = jnp.where(row >= col, scores, MASKED)
    expo = jnp.exp(scores - jnp.max(scores, -1, keepdims=True))
    return expo / jnp.sum(expo, -1, keepdims=True), query, keys


def split_heads(source, targets):
    for place, target in enumerate(targets):
        heads = target.shape[0]
        for head in range(heads):
            start = (place * heads + head) * HEAD_DIM
            target[head] = source[:, start : start + HEAD_DIM]


class Blocks:
    def __init__(self, here, ready, land, send_sems, recv_sems):
        self.here, self.ready, self.land = here, ready, land
        self.send_sems, self.recv_sems = send_sems, recv_sems

    def copy(self, at, source):
        here = self.here
        return pltpu.make_async_remote_copy(
            src_ref=self.ready.at[at],
            dst_ref=self.land(source),
            send_sem=self.send_sems.at[at],
            recv_sem=self.recv_sems.at[source],
            device_id={"replica": at, "shard": here.s},
            device_id_type=MESH,
        )

    def send(self, at):
        here = self.here

        @pl.when(here.r != at)
        def _():
            self.copy(at, here.r).start()

        @pl.when(here.r == at)
        def _():
            self.land(at)[...] = self.ready[at]

    def finish(self):
        for at in range(self.here.replicas):

            @pl.when(self.here.r != at)
            def _(at=at):
                self.copy(at, at).wait_recv()
                self.copy(at, at).wait_send()


def attend_task(place, mixed):
    rows, replicas, heads, columns = mixed.shape[0], place.replicas, place.heads, place.columns
    length, wide = rows * replicas, heads * HEAD_DIM

    def run(here, copies, ins, outs, scratch):
        (mixed_ref,), (seq_ref, out_ref) = ins, outs
        q_ref, k_ref, v_ref, o_ref, ready, landed, send_sems, recv_sems = scratch
        mine = pl.ds(pl.multiple_of(here.r * rows, 16), rows)
        arriving = []
        for step in range(1, replicas):
            to = lax.rem(here.r + step, replicas)
            source = mixed_ref.at[:, pl.ds(pl.multiple_of(to * columns, 128), columns)]
            device = {"replica": to, "shard": here.s}
            arriving.append(copies.send(source, seq_ref.at[mine, :], device))
        seq_ref[mine, :] = mixed_ref[:, pl.ds(pl.multiple_of(here.r * columns, 128), columns)]
        yield
        for copy in arriving:
            copy.wait_recv()
        split_heads(seq_ref, (q_ref, k_ref, v_ref))
        blocks = Blocks(here, ready, lambda at: landed.at[at], send_sems, recv_sems)
        yield
        for at in range(replicas):
            first = at * rows

            @pl.loop(0, heads)
            def _(head, first=first):
                probs, _, _ = block_probs(q_ref, k_ref, head, first, rows)
                keys = v_ref[head, 0 : first + rows, :]
                o_ref[head] = dot(probs.astype(BF16), keys, ((1,), (0,))).astype(BF16)

            for head in range(heads):
                ready[at, :, head * HEAD_DIM : (head + 1) * HEAD_DIM] = o_ref[head]
            blocks.send(at)
            yield
        blocks.finish()
        width = out_ref.shape[1]
        for at in range(replicas):
            start = at * wide
            size = min(wide, width - start)
            if size > 0:
                out_ref[:, start : start + size] = landed[at, :, :size]

    part = pltpu.VMEM((heads, length, HEAD_DIM), BF16)
    return Task(
        run,
        [(mixed, VMEM_BLOCK)],
        [
            (jax.ShapeDtypeStruct((length, columns), BF16), VMEM_BLOCK),
            (jax.ShapeDtypeStruct((rows, HEADS * HEAD_DIM), BF16), VMEM_BLOCK),
        ],
        [part] * 3
        + [pltpu.VMEM((heads, rows, HEAD_DIM), BF16)]
        + [pltpu.VMEM((replicas, rows, wide), BF16)] * 2
        + [pltpu.SemaphoreType.DMA((replicas,))] * 2,
        replicas - 1,
    )


def attend_back_task(place, seq, d_attended):
    rows, width = d_attended.shape
    replicas, heads, columns = place.replicas, place.heads, place.columns
    length, wide = rows * replicas, heads * HEAD_DIM

    def run(here, copies, ins, outs, scratch):
        (seq_ref, d_ref), (out_ref,) = ins, outs
        q_ref, k_ref, v_ref, do_ref, dq_ref, dk_ref, dv_ref = scratch[:7]
        d_ready, d_landed, ready, send_sems, recv_sems = scratch[7:]
        for at in range(replicas):
            start = at * wide
            size = max(0, min(wide, width - start))
            if size > 0:
                d_ready[at, :, :size] = d_ref[:, start : start + size]
            if size < wide:
                d_ready[at, :, size:] = jnp.zeros((rows, wide - size), BF16)
        arriving = []
        for step in range(1, replicas):
            to = lax.rem(here.r + step, replicas)
            device = {"replica": to, "shard": here.s}
            arriving.append(copies.send(d_ready.at[to], d_landed.at[here.r], device))
        d_landed[here.r] = d_ready[here.r]
        yield
        split_heads(seq_ref, (q_ref, k_ref, v_ref))
        dk_ref[...] = jnp.zeros((heads, length, HEAD_DIM), F32)
        dv_ref[...] = jnp.zeros((heads, length, HEAD_DIM), F32)
        for copy in arriving:
            copy.wait_recv()
        for at in range(replicas):
            for head in range(heads):
                do_ref[head, at * rows : (at + 1) * rows, :] = d_landed[
                    at, :, head * HEAD_DIM : (head + 1) * HEAD_DIM
                ]

        def land(source):
            return out_ref.at[:, pl.ds(pl.multiple_of(source * columns, 128), columns)]

        blocks = Blocks(here, ready, land, send_sems, recv_sems)
        yield
        for at in reversed(range(replicas)):
            first = at * rows
            count = first + rows

            @pl.loop(0, heads)
            def _(head, first=first, count=count):
                probs, query, keys = block_probs(q_ref, k_ref, head, first, rows)
                d_out = do_ref[head, first:count, :]
                d_probs = dot(d_out, v_ref[head, 0:count, :], ((1,), (1,)))
                row_dot = jnp.sum(d_probs * probs, -1, keepdims=True)
                d_scores = (probs * (d_probs - row_dot) * (HEAD_DIM**-0.5)).astype(BF16)
                dq_ref[head] = dot(d_scores, keys, ((1,), (0,))).astype(BF16)
                dk_ref[head, 0:count, :] += dot(d_scores, query, ((0,), (0,)))
                dv_ref[head, 0:count, :] += dot(probs.astype(BF16), d_out, ((0,), (0,)))

            for head in range(heads):
                pieces = (
                    dq_ref[head],
                    dk_ref[head, first:count, :].astype(BF16),
                    dv_ref[head, first:count, :].astype(BF16),
                )
                for part, piece in enumerate(pieces):
                    start = (part * heads + head) * HEAD_DIM
                    ready[at, :, start : start + HEAD_DIM] = piece
            if place.span < columns:
                ready[at, :, place.span :] = jnp.zeros((rows, columns - place.span), BF16)
            blocks.send(at)
            yield
        blocks.finish()

    part = pltpu.VMEM((heads, length, HEAD_DIM), BF16)
    sums = pltpu.VMEM((heads, length, HEAD_DIM), F32)
    return Task(
        run,
        [(seq, VMEM_BLOCK), (d_attended, VMEM_BLOCK)],
        [(jax.ShapeDtypeStruct((rows, replicas * columns), BF16), VMEM_BLOCK)],
        [part] * 4
        + [pltpu.VMEM((heads, rows, HEAD_DIM), BF16), sums, sums]
        + [pltpu.VMEM((replicas, rows, wide), BF16)] * 2
        + [pltpu.VMEM((replicas, rows, columns), BF16)]
        + [pltpu.SemaphoreType.DMA((replicas,))] * 2,
        replicas - 1,
    )


def fits(place, kind, shape):
    rows, half = shape[0], shape[1] // place.cores
    if kind == "columns" and half % (128 * place.xs):
        return "half"
    if kind == "rows" and rows % (16 * place.xs):
        return "half"
    return kind


def window(ref, row, rows, col, cols):
    row = row if isinstance(row, int) else pl.multiple_of(row, 16)
    col = col if isinstance(col, int) else pl.multiple_of(col, 128)
    return ref.at[pl.ds(row, rows), pl.ds(col, cols)]


def part_of(here, kind, ref, shape, block, x_at):
    rows, cols = shape
    row = block * rows
    if kind == "whole":
        return window(ref, row, rows, 0, cols)
    half = cols // here.cores
    if kind == "half":
        return window(ref, row, rows, here.core * half, half)
    if kind == "columns":
        share = half // here.xs
        return window(ref, row, rows, here.core * half + x_at * share, share)
    share = rows // here.xs
    return window(ref, row + x_at * share, share, here.core * half, half)


def half_of(here, ref, shape, block):
    rows, cols = shape
    half = cols // here.cores
    return window(ref, block * rows, rows, here.core * half, half)


def gather_task(place, jobs):
    kinds = [fits(place, kind, value.shape) for kind, value in jobs]
    arrays = [value for _, value in jobs]
    shapes = [value.shape for value in arrays]
    others = place.shards - 1
    copies = sum(
        others
        + (others * (place.xs - 1) if kind in ("columns", "rows") else 0)
        + (others * (place.cores - 1) if kind != "whole" else 0)
        for kind in kinds
    )

    def run(here, copies, sources, targets, scratch):
        (own_sems,) = scratch

        def fetched(job, z_back, y_back, x_back=0):
            kind, shape = kinds[job], shapes[job]
            x_at = lax.rem(here.x - x_back + here.xs, here.xs)
            target = part_of(here, kind, targets[job], shape, here.block(z_back, y_back), x_at)
            if z_back == 0 and y_back == 0:
                return part_of(here, kind, sources[job], shape, 0, x_at), target
            return target, target

        own = []
        along_z, along_y, along_x, along_core = {}, {}, {}, {}
        for step in range(here.zs + 3):
            for job, kind in enumerate(kinds):
                z_back = step
                if z_back < here.zs:
                    if z_back > 0:
                        along_z[job, z_back - 1].wait_recv()
                    if z_back < here.zs - 1:
                        along_z[job, z_back] = copies.send(
                            *fetched(job, z_back, 0), here.device(z=1)
                        )
                    if here.ys > 1:
                        along_y[job, z_back, 0] = copies.send(
                            *fetched(job, z_back, 0), here.device(y=1)
                        )
                if step == 0:
                    rows = shapes[job][0]
                    row = pl.multiple_of(here.block(0, 0) * rows, 16)
                    copy = pltpu.make_async_copy(
                        sources[job], targets[job].at[pl.ds(row, rows), :], own_sems.at[job]
                    )
                    copy.start()
                    own.append(copy)
                z_back = step - 1
                if 0 <= z_back < here.zs:
                    for y_back in range(1, here.ys):
                        along_y[job, z_back, y_back - 1].wait_recv()
                        if y_back < here.ys - 1:
                            along_y[job, z_back, y_back] = copies.send(
                                *fetched(job, z_back, y_back), here.device(y=1)
                            )
                    if kind in ("columns", "rows") and here.xs > 1:
                        for y_back in range(0 if z_back else 1, here.ys):
                            along_x[job, z_back, y_back, 0] = copies.send(
                                *fetched(job, z_back, y_back), here.device(x=1)
                            )
                z_back = step - 2
                if 0 <= z_back < here.zs and kind != "whole":
                    for y_back in range(0 if z_back else 1, here.ys):
                        if kind != "half":
                            for x_back in range(1, here.xs):
                                along_x[job, z_back, y_back, x_back - 1].wait_recv()
                                if x_back < here.xs - 1:
                                    along_x[job, z_back, y_back, x_back] = copies.send(
                                        *fetched(job, z_back, y_back, x_back), here.device(x=1)
                                    )
                        half = half_of(here, targets[job], shapes[job], here.block(z_back, y_back))
                        along_core[job, z_back, y_back] = copies.send(
                            half, half, here.device(core=1)
                        )
                z_back = step - 3
                if 0 <= z_back < here.zs and kind != "whole":
                    for y_back in range(0 if z_back else 1, here.ys):
                        along_core[job, z_back, y_back].wait_recv()
            yield
        for copy in own:
            copy.wait()

    return Task(
        run,
        [(value, VMEM_BLOCK) for value in arrays],
        [
            (jax.ShapeDtypeStruct((place.shards * a.shape[0], a.shape[1]), a.dtype), ANY_BLOCK)
            for a in arrays
        ],
        [pltpu.SemaphoreType.DMA((len(jobs),))],
        copies,
    )


def share_of(place, kind, rows, cols):
    if kind == "columns":
        return rows, cols // place.xs
    if kind == "rows":
        return rows // place.xs, cols
    return rows, cols


def x_window(kind, ref, shape, x_at):
    rows, cols = shape
    lead = (slice(None),) * (len(ref.shape) - 2)
    if kind == "columns":
        return ref.at[lead + (slice(None), pl.ds(pl.multiple_of(x_at * cols, 128), cols))]
    return ref.at[lead + (pl.ds(pl.multiple_of(x_at * rows, 16), rows), slice(None))]


def reduce_task(place, jobs):
    zs, ys, xs = place.zs, place.ys, place.xs
    arrays = [value.reshape(place.shards, -1, value.shape[1]) for _, _, value in jobs]
    kinds = [fits(place, kind, value.shape[1:]) for (kind, _, _), value in zip(jobs, arrays)]
    behind = [late for _, late, _ in jobs]
    halves = [(value.shape[1], value.shape[2] // place.cores) for value in arrays]
    shares = [share_of(place, kind, *half) for kind, half in zip(kinds, halves)]
    count = len(jobs)
    own, got, x_got, y_got, z_got, x_sum, done = ([] for _ in range(7))
    copies = 0
    for kind, half, share in zip(kinds, halves, shares):
        split = kind != "half"
        tiny = (16, 128)
        own.append(pltpu.VMEM((2, ys) + half, BF16))
        got.append(pltpu.VMEM((zs, ys) + half, BF16))
        x_got.append(pltpu.VMEM((zs, xs - 1, ys) + share if split else tiny, BF16))
        y_got.append(pltpu.VMEM((zs, ys - 1) + share, BF16))
        z_got.append(pltpu.VMEM((zs - 1,) + share, BF16))
        x_sum.append(pltpu.VMEM(tiny if split else (xs,) + share, BF16))
        done.append(pltpu.VMEM((2,) + half, BF16))
        copies += zs + (zs * (xs - 1) if split else 0) + zs * (ys - 1) + (zs - 1) + (xs - 1) + 1

    def run(here, copies, grads, outs, scratch):
        own, got, x_got, y_got, z_got, x_sum, done = (
            scratch[at * count : (at + 1) * count] for at in range(7)
        )
        own_sems = scratch[-1]

        def target_z(t):
            return lax.rem(here.z + 2 * zs - 1 - t, zs)

        def half_at(job, t, core):
            half = halves[job][1]
            return grads[job].at[
                pl.ds(target_z(t) * ys, ys), :, pl.ds(pl.multiple_of(core * half, 128), half)
            ]

        def load(job, t):
            copy = pltpu.make_async_copy(
                half_at(job, t, here.core), own[job].at[t % 2], own_sems.at[job, t % 2]
            )
            copy.start()
            return copy

        loads, by_core = {}, {}
        for wave in range(zs + max(behind)):
            for job in range(count):
                t = wave - behind[job]
                if 0 <= t < zs:
                    by_core[job, t] = copies.send(
                        half_at(job, t, lax.rem(here.core + 1, here.cores)),
                        got[job].at[t],
                        here.device(core=1),
                    )
                    if t < 2:
                        loads[job, t] = load(job, t)
        yield
        by_x, by_y, by_z = {}, {}, {}

        def base(job, t):
            return got[job].at[t] if kinds[job] == "half" else x_got[job].at[t, 0]

        def send_y(job, t):
            for turn in range(1, ys):
                by_y[job, t, turn] = copies.send(
                    base(job, t).at[lax.rem(here.y + turn, ys)],
                    y_got[job].at[t, turn - 1],
                    here.device(y=turn),
                )

        for step in range(zs + 4 + max(behind)):
            for job, kind in enumerate(kinds):
                rows, cols = shares[job]
                local = step - behind[job]
                t = local
                if 0 <= t < zs:
                    loads[job, t].wait()
                    by_core[job, t].wait_recv()
                    for y in range(ys):
                        mine, sums = own[job].at[t % 2, y], got[job].at[t, y]

                        def both(at, mine=mine, sums=sums):
                            sums[at] = (mine[at].astype(F32) + sums[at].astype(F32)).astype(BF16)

                        by_rows(halves[job][0], both)
                    if t + 2 < zs:
                        loads[job, t + 2] = load(job, t + 2)
                    if kind == "half":
                        send_y(job, t)
                    else:
                        for turn in range(1, xs):
                            x_at = lax.rem(here.x + turn, xs)
                            by_x[job, t, turn] = copies.send(
                                x_window(kind, got[job].at[t], shares[job], x_at),
                                x_got[job].at[t, turn - 1],
                                here.device(x=turn),
                            )
                t = local - 1
                if 0 <= t < zs and kind != "half":
                    for turn in range(1, xs):
                        by_x[job, t, turn].wait_recv()
                    for y in range(ys):
                        mine = x_window(kind, got[job].at[t, y], shares[job], here.x)
                        parts = [x_got[job].at[t, turn, y] for turn in range(xs - 1)]

                        def all_x(at, mine=mine, parts=parts):
                            total = mine[at].astype(F32)
                            for part in parts:
                                total += part[at].astype(F32)
                            parts[0][at] = total.astype(BF16)

                        by_rows(rows, all_x)
                    send_y(job, t)
                t = local - 2
                if 0 <= t < zs:
                    for turn in range(1, ys):
                        by_y[job, t, turn].wait_recv()
                    parts = [y_got[job].at[t, turn] for turn in range(ys - 1)]
                    target = parts[0]
                    if t > 0:
                        by_z[job, t - 1].wait_recv()
                        parts.append(z_got[job].at[t - 1])
                    if t == zs - 1:
                        target = (
                            x_sum[job].at[here.x]
                            if kind == "half"
                            else x_window(kind, done[job].at[0], shares[job], here.x)
                        )
                    mine = base(job, t).at[here.y]

                    def all_y(at, mine=mine, parts=parts, target=target):
                        total = mine[at].astype(F32)
                        for part in parts:
                            total += part[at].astype(F32)
                        target[at] = total.astype(BF16)

                    by_rows(rows, all_y)
                    if t < zs - 1:
                        by_z[job, t] = copies.send(target, z_got[job].at[t], here.device(z=1))
                    else:
                        for turn in range(1, xs):
                            by_x[job, "done", turn] = copies.send(
                                target, target, here.device(x=turn)
                            )
                if local == zs + 2:
                    for turn in range(1, xs):
                        by_x[job, "done", turn].wait_recv()
                    if kind == "half":
                        sums, target = x_sum[job], done[job].at[0]

                        def across(at, sums=sums, target=target):
                            total = sums[0, at].astype(F32)
                            for x_at in range(1, xs):
                                total += sums[x_at, at].astype(F32)
                            target[at] = total.astype(BF16)

                        by_rows(rows, across)
                    by_core[job, "done"] = copies.send(
                        done[job].at[0], done[job].at[1], here.device(core=1)
                    )
                if local == zs + 3:
                    by_core[job, "done"].wait_recv()
                    half_rows, half = halves[job]
                    for side in range(2):
                        column = lax.rem(here.core + side, 2) * half
                        place_at = outs[job].at[:, pl.ds(pl.multiple_of(column, 128), half)]

                        def write(at, place_at=place_at, source=done[job].at[side]):
                            place_at[at] = source[at].astype(F32)

                        by_rows(half_rows, write)
            yield

    return Task(
        run,
        [(value, ANY_BLOCK) for value in arrays],
        [(jax.ShapeDtypeStruct(value.shape[1:], F32), VMEM_BLOCK) for value in arrays],
        own
        + got
        + x_got
        + y_got
        + z_got
        + x_sum
        + done
        + [pltpu.SemaphoreType.DMA((count, 2))],
        copies,
    )


def reduce_vectors_task(place, vectors):
    shape = vectors.shape[1:]

    def run(here, copies, ins, outs, scratch):
        (vec_ref,), (out_ref,), (got, sums) = ins, outs, scratch
        arriving = []
        for step in range(1, here.shards):
            to = lax.rem(here.s + step, here.shards)
            device = {"replica": here.r, "shard": to}
            arriving.append(copies.send(vec_ref.at[to], got.at[step - 1], device))
        yield
        yield
        yield
        for copy in arriving:
            copy.wait_recv()
        total = vec_ref[here.s]
        for at in range(here.shards - 1):
            total += got[at]
        sums[here.r] = total
        arriving = []
        for step in range(1, here.replicas):
            device = {"replica": lax.rem(here.r + step, here.replicas), "shard": here.s}
            arriving.append(copies.send(sums.at[here.r], sums.at[here.r], device))
        yield
        yield
        for copy in arriving:
            copy.wait_recv()
        total = sums[0]
        for at in range(1, here.replicas):
            total += sums[at]
        out_ref[...] = total

    return Task(
        run,
        [(vectors, VMEM_BLOCK)],
        [(jax.ShapeDtypeStruct(shape, F32), VMEM_BLOCK)],
        [
            pltpu.VMEM((place.shards - 1,) + shape, F32),
            pltpu.VMEM((place.replicas,) + shape, F32),
        ],
        place.shards + place.replicas - 2,
    )


def pack_lanes(values, lead):
    size = values.shape[-1]
    lanes = 128 * -(-size // (16 * 128))
    values = jnp.pad(values, [(0, 0)] * len(lead) + [(0, 16 * lanes - size)])
    return values.reshape(lead + (16, lanes))


def unpack_vectors(flat, layers, sizes):
    flat = flat[..., : layers * sum(sizes)]
    flat = flat.reshape(flat.shape[:-1] + (layers, -1))
    out, start = [], 0
    for size in sizes:
        out.append(flat[..., start : start + size])
        start += size
    return out


def per_device(
    tokens,
    gain_one,
    shift_one,
    query_key_value_weight,
    b_query,
    b_value,
    output_weight,
    output_proj_bias,
    gain_two,
    shift_two,
    up_weight,
    up_bias,
    down_weight,
    down_bias,
    cotangent,
):
    place = Place(lax.axis_size("replica"), lax.axis_size("shard")).locate()
    held, _, width = tokens.shape
    layers = gain_one.shape[0]
    last = layers - 1
    mix = place.mix_columns(query_key_value_weight)
    vectors = (
        gain_one,
        shift_one,
        b_query,
        b_value,
        output_proj_bias,
        gain_two,
        shift_two,
        up_bias,
        down_bias,
    )
    sizes = [vector.shape[1] for vector in vectors]
    packed = pack_lanes(jnp.concatenate(vectors, -1).reshape(-1), ())
    current = place.to_sequences(tokens).astype(F32)

    ((whole_vectors, first_mix),) = fuse(
        place, "gather_first", 0, [gather_task(place, [("whole", packed), ("half", mix[0])])], ()
    )
    flat = whole_vectors.reshape(place.shards, -1)
    g1, s1, bq, bv, bo, g2, s2, bu, bd = (
        jnp.swapaxes(piece, 0, 1).reshape(layers, -1).astype(F32)
        for piece in unpack_vectors(flat, layers, sizes)
    )
    mix_bias = place.mix_columns(jnp.concatenate([bq, jnp.zeros_like(bq), bv], -1))
    mixes, outs = [first_mix], []
    ups, downs = [], []

    saved = []
    for n in range(layers):
        normed = norm_rows(current, g1[n], s1[n]).astype(BF16)
        mixed = (dot(normed, mixes[n], ((1,), (0,))) + mix_bias[n]).astype(BF16)
        jobs = [("columns", up_weight[n]), ("rows" if n < last else "half", down_weight[n])]
        if n == 0:
            jobs.append(("half", output_weight[0]))
        if n < last:
            jobs += [("half", mix[n + 1]), ("half", output_weight[n + 1])]
        (seq, attended), gathered = fuse(
            place,
            f"attend_{n}",
            1 + n,
            [attend_task(place, mixed), gather_task(place, jobs)],
            (0, 1, 1, 0) + (0, 1) * place.replicas,
        )
        ups.append(gathered.pop(0))
        downs.append(gathered.pop(0))
        if n == 0:
            outs.append(gathered.pop(0))
        if n < last:
            mixes.append(gathered.pop(0))
            outs.append(gathered.pop(0))
        x_mid = current + (dot(attended, outs[n], ((1,), (0,))) + bo[n])
        moved = norm_rows(x_mid, g2[n], s2[n]).astype(BF16)
        pre = dot(moved, ups[n], ((1,), (0,))) + bu[n]
        act = jax.nn.gelu(pre, approximate=True).astype(BF16)
        saved.append((current, normed, seq, attended, x_mid, moved, pre, act))
        current = x_mid + dot(act, downs[n], ((1,), (0,))) + bd[n]
    output = place.from_sequences(current.astype(BF16), held)

    grad_now = place.to_sequences(cotangent).astype(F32)
    summed = [{} for _ in range(layers)]
    vector_grads = [None] * layers
    waiting = []
    for n in reversed(range(layers)):
        current, normed, seq, attended, x_mid, moved, pre, act = saved[n]
        d_ffn = grad_now.astype(BF16)
        grad_down = dot(act, d_ffn, ((0,), (0,))).astype(BF16)
        grad_b_down = jnp.sum(d_ffn.astype(F32), 0)
        d_act = dot(d_ffn, downs[n], ((1,), (1,)))
        gelu_back = jax.vjp(lambda inner: jax.nn.gelu(inner, approximate=True), pre)[1]
        d_pre = gelu_back(d_act)[0].astype(BF16)
        grad_up = dot(moved, d_pre, ((0,), (0,))).astype(BF16)
        grad_b_up = jnp.sum(d_pre.astype(F32), 0)
        d_moved = dot(d_pre, ups[n], ((1,), (1,)))
        norm_back = jax.vjp(norm_rows, x_mid, g2[n], s2[n])[1]
        d_from_norm, grad_gain_two, grad_shift_two = norm_back(d_moved)
        grad_mid = grad_now + d_from_norm
        d_branch = grad_mid.astype(BF16)
        grad_out = dot(attended, d_branch, ((0,), (0,))).astype(BF16)
        grad_b_out = jnp.sum(d_branch.astype(F32), 0)
        d_att = dot(d_branch, outs[n], ((1,), (1,))).astype(BF16)
        waiting += [("up", n, "columns", 0, grad_up), ("down", n, "half", 1, grad_down)]
        (d_mixed,), sums = fuse(
            place,
            f"attend_back_{n}",
            1 + layers + n,
            [
                attend_back_task(place, seq, d_att),
                reduce_task(place, [job[2:] for job in waiting]),
            ],
            (0, 1, 1, 0) + (0, 1) * place.replicas,
        )
        for job, value in zip(waiting, sums):
            summed[job[1]][job[0]] = value
        grad_mix = dot(normed, d_mixed, ((0,), (0,))).astype(BF16)
        waiting = [("mix", n, "half", 0, grad_mix), ("out", n, "half", 0, grad_out)]
        grad_b_mix = place.unmix_columns(jnp.sum(d_mixed.astype(F32), 0))
        d_normed = dot(d_mixed, mixes[n], ((1,), (1,)))
        first_back = jax.vjp(norm_rows, current, g1[n], s1[n])[1]
        d_from_first, grad_gain_one, grad_shift_one = first_back(d_normed)
        grad_now = grad_mid + d_from_first
        vector_grads[n] = (
            grad_gain_one,
            grad_shift_one,
            grad_b_mix[:width],
            grad_b_mix[2 * width :],
            grad_b_out,
            grad_gain_two,
            grad_shift_two,
            grad_b_up,
            grad_b_down,
        )
    grad_tokens = place.from_sequences(grad_now.astype(BF16), held).astype(F32)
    rows = [v.reshape(place.shards, -1) for vectors in vector_grads for v in vectors]
    packed = pack_lanes(jnp.concatenate(rows, 1), (place.shards,))
    sums, (vector_sums,) = fuse(
        place,
        "reduce_last",
        1 + 2 * layers,
        [
            reduce_task(place, [job[2:] for job in waiting]),
            reduce_vectors_task(place, packed),
        ],
        (0, 1) * 8,
    )
    for job, value in zip(waiting, sums):
        summed[job[1]][job[0]] = value
    weight_grads = {
        name: jnp.stack([summed[n][name] for n in range(layers)])
        for name in ("mix", "out", "up", "down")
    }
    own = unpack_vectors(vector_sums.reshape(-1), layers, sizes)
    (
        grad_gain_one,
        grad_shift_one,
        grad_b_query,
        grad_b_value,
        grad_b_out,
        grad_gain_two,
        grad_shift_two,
        grad_b_up,
        grad_b_down,
    ) = own
    return (
        output,
        grad_tokens,
        grad_gain_one,
        grad_shift_one,
        place.unmix_columns(weight_grads["mix"]),
        grad_b_query,
        grad_b_value,
        weight_grads["out"],
        grad_b_out,
        grad_gain_two,
        grad_shift_two,
        weight_grads["up"],
        grad_b_up,
        weight_grads["down"],
        grad_b_down,
    )


def solution(mesh):
    vector, matrix = P(None, "shard"), P(None, "shard", None)
    rows = P("replica", "shard", None)
    in_specs = (
        rows,
        vector,
        vector,
        matrix,
        vector,
        vector,
        matrix,
        vector,
        vector,
        vector,
        matrix,
        vector,
        matrix,
        vector,
        rows,
    )
    out_specs = (
        rows,
        rows,
        vector,
        vector,
        matrix,
        vector,
        vector,
        matrix,
        vector,
        vector,
        vector,
        matrix,
        vector,
        matrix,
        vector,
    )
    return jax.shard_map(
        per_device, mesh=mesh, in_specs=in_specs, out_specs=out_specs, check_vma=False
    )
```

time: 1630 us -> 596 us (0.37)
  waiting for transfers between devices: 1250 us -> 0.02 us
  Pallas kernels: 48.4 us -> 417 us
  blocking collectives: 93.5 us -> 0 us
  matrix products: 95.2 us -> 74.6 us
  starting transfers between devices: 28.1 us -> 11 us
    reduce_scatter x8 -> x0, waiting for transfers between devices: 549 us -> none  [reduce_weights(): lax.psum_scatter(g, 'shard', scatter_dimension=0, tiled=True).astype(F32)]
    all_gather x8 -> x0, waiting for transfers between devices: 377 us -> none  [gather_weights(): lax.all_gather(w[layer], 'shard', axis=0, tiled=True)]
    pallas_call x4 -> x6, Pallas kernels: 48.4 us -> 417 us  [fuse(): pl.pallas_call(kernel, out_shape=[shape for task in tasks for shape, _ in...]
    psum x2 -> x0, waiting for transfers between devices: 270 us -> none  [the longest x1 143 us: reduce_weights(): lax.psum(lax.psum_scatter(g, 'shard', scatter_dimension=0, tiled=True).as...]
    all_gather x1 -> x0, blocking collectives: 52.8 us -> none  [gather_vectors(): whole = lax.all_gather(packed, 'shard', axis=0)]
    all_to_all x5 -> x0, waiting for transfers between devices: 51.3 us -> none  [the longest x2 30.2 us: to_heads(): return lax.all_to_all(values, 'replica', 1, 0, tiled=True)]
    all_to_all x3 -> x0, blocking collectives: 40.7 us -> none  [the longest x2 21.4 us: to_heads(): return lax.all_to_all(values, 'replica', 1, 0, tiled=True)]
    reshape x2 -> x27, local copies, waits for them, and re-layouts: 0.17 us -> 26 us  [the longest x18 21.5 us: per_device(): v.reshape(place.shards, -1)]
  transfers between devices with their start and end apart: 31 -> 8, of which waited for: 21 -> 0; matrix products, arithmetic and copies ran while one was open for 9% -> 14% of each run, Pallas kernels for 2% -> 41%
where the time goes in v4:
time: 596 us; the launch traced here: 587 us
  Pallas kernels  417 us (70%)
  matrix products  74.6 us (13%)
  local copies, waits for them, and re-layouts  63 us (11%)
  other arithmetic  19.8 us (3%)
  starting transfers between devices  11 us (2%)
    pallas_call x6, Pallas kernels, fuse(): pl.pallas_call(kernel, out_shape=[shape for task in tasks for shape, _ in...  417 us
    dot_general x24, matrix products, dot(): lax.dot_general(a, b, (contract, ((), ())), preferred_element_type=F32)  74.6 us
    reshape x18, local copies, waits for them, and re-layouts, per_device(): v.reshape(place.shards, -1)  21.5 us
  transfers between devices with their start and end apart: 8, of which 0 were waited for; matrix products, arithmetic and copies ran while one was open for 14% of the time, Pallas kernels for 41%

profile of v4, /device:TPU:0, one launch (start us, length us, event | category | flops | bytes accessed | tf_op | source)
XLA Modules:
  0.0 587.3 jit_solution(13931941043994507293)
XLA Ops:
  1.7 3.1 collective-permute-start.1
  5.5 1.8 dynamic-slice_bitcast_fusion.2
  7.3 3.0 collective-permute-start.4
  11.8 2.9 reshape.388
  17.0 41.8 %gather_first.1 = (bf16[128,256]{1,0:T(8,128)(2,1)}, bf16[768,2560]{1,0:T(8,128)(2,1)}) custom-call(bf16[16,256]{1,0:T(8,128)(2,1)} %reshape.387.refs_0_, bf16[96,2560]{1,0:T(8,128)(2,1)} %copy.43.refs_1_), custom_call_target="tpu_custom_call" | custom-call | tf_op jit(solution)/shard_map/gather_first/pallas_call | solution.py:182
  60.9 2.3 slice_bitcast_fusion.1
  67.6 4.4 fusion.refs_0_
  72.1 90.5 %attend_0.1 = (bf16[1024,640]{1,0:T(8,128)(2,1)}, bf16[256,768]{1,0:T(8,128)(2,1)}, bf16[768,3072]{1,0:T(8,128)(2,1)}, bf16[3072,768]{1,0:T(8,128)(2,1)}, bf16[7...) custom-call(bf16[256,2560]{1,0:T(8,128)(2,1)} %fusion.refs_0_, ...), custom_call_target="tpu_custom_call" | custom-call | tf_op jit(solution)/shard_map/attend_0/pallas_call | solution.py:182
  162.6 2.0 fusion.73
  164.9 4.0 convolution_add_fusion.3
  168.9 2.1 fusion.74
  172.1 2.3 fusion.1.refs_0_
  174.4 52.3 %attend_1.1 = (bf16[1024,640]{1,0:T(8,128)(2,1)}, bf16[256,768]{1,0:T(8,128)(2,1)}, bf16[768,3072]{1,0:T(8,128)(2,1)}, bf16[3072,768]{1,0:T(8,128)(2,1)}) custom-call(bf16[256,2560]{1,0:T(8,128)(2,1)} %fusion.1.refs_0_, bf16[96,3072]{1,0:T(8,128)(2,1)} %get-tuple-element.94.refs_1_, bf16[384,768]{1,0:T(8,128)(2,1)} %get-tuple-element.92.refs_2_), custom_call_target="tpu_custom_call" | custom-call | tf_op jit(solution)/shard_map/attend_1/pallas_call | solution.py:182
  226.7 2.1 fusion.75
  230.4 1.5 convolution_add_fusion.2
  232.0 5.2 convert_reduce_fusion
  237.2 2.2 multiply_reduce_fusion
  242.7 1.5 convolution_convert_fusion.7
  244.2 4.4 convolution_convert_fusion.4
  248.6 3.7 convolution_convert_fusion.5
  252.3 83.1 %attend_back_1.1 = (bf16[256,2560]{1,0:T(8,128)(2,1)}, f32[96,3072]{1,0:T(8,128)}, f32[384,768]{1,0:T(8,128)}) custom-call(bf16[1024,640]{1,0:T(8,128)(2,1)} %get-tuple-element.50.refs_0_, bf16[256,768]{1,0:T(8,128)(2,1)} %convolution_convert_fusion.9.refs_1_, bf16[8,96,3072]{2,1,0:T(8,128)(2,1)} %bitcast.135, bf16[8,384,768]{2,1,0:T(8,128)(2,1)} %bitcast.143), custom_call_target="tpu_custom_call" | custom-call | tf_op jit(solution)/shard_map/attend_back_1/pallas_call | solution.py:182
  335.5 4.6 multiply_reduce_fusion.1
  342.2 6.1 %convert_reduce_fusion.1 = (f32[3072]{0:T(1024)}, bf16[256,3072]{1,0:T(8,128)(2,1)S(1)}) fusion(f32[256,3072]{1,0:T(8,128)S(1)} %copy-done.38, bf16[3072,768]{1,0:T(8,128)(2,1)} %get-tuple-element.44, f32[256,768]{1,0:T(8,128)S(1)} %get-tuple-element.83), kind=kOutput, calls=%fused_computation.31 | convolution fusion | flops 1225454592 | bytes 10235904 | tf_op jit(solution)/shard_map/dot_general | solution.py:23
  348.3 2.2 multiply_reduce_fusion.2
  353.7 1.5 convolution_convert_fusion.6
  355.2 4.4 convolution_convert_fusion.1
  359.7 3.3 convolution_convert_fusion.3
  362.9 4.1 convolution_convert_fusion.2
  367.0 95.9 %attend_back_0.1 = (bf16[256,2560]{1,0:T(8,128)(2,1)}, f32[96,2560]{1,0:T(8,128)}, f32[96,768]{1,0:T(8,128)}, f32[96,3072]{1,0:T(8,128)}, f32[384,768]{1,0:T(8,128)}) custom-call(bf16[1024,640]{1,0:T(8,128)(2,1)} %get-tuple-element.52.refs_0_, bf16[256,768]{1,0:T(8,128)(2,1)} %convolution_convert_fusion.8.refs_1_, bf16[8,96,2560]{2,1,0:T(8,128)(2,1)} %bitcast.133, ...), custom_call_target="tpu_custom_call" | custom-call | tf_op jit(solution)/shard_map/attend_back_0/pallas_call | solution.py:182
  462.9 4.6 fusion.59
  468.3 3.3 convolution_convert_fusion
  471.6 2.7 fusion.20
  479.3 1.6 collective-permute-start.3
  493.1 1.4 reshape.417
  494.5 1.4 slice_reduce_fusion
  495.9 1.3 reshape.419
  497.3 1.3 reshape.418
  498.6 1.3 reshape.409
  501.2 1.3 reshape.404
  502.6 1.7 fusion.29
  504.3 1.4 reshape.403
  511.2 2.7 copy.46
  513.9 53.7 %reduce_last.1 = (f32[96,2560]{1,0:T(8,128)}, f32[96,768]{1,0:T(8,128)}, f32[16,256]{1,0:T(8,128)}) custom-call(bf16[8,96,2560]{2,1,0:T(8,128)(2,1)} %bitcast.136, bf16[8,96,768]{2,1,0:T(8,128)(2,1)} %bitcast.140, f32[8,16,256]{2,1,0:T(8,128)} %bitcast.152), custom_call_target="tpu_custom_call" | custom-call | tf_op jit(solution)/shard_map/reduce_last/pallas_call | solution.py:182
  568.9 2.7 copy.45
  571.6 1.6 pad_maximum_fusion.1
  575.9 2.5 copy.42
  578.4 3.8 reshape_reshape.2
  582.3 1.6 pad_maximum_fusion.2
  (223 shorter events, 55.6 us)
Async XLA Ops:
  1.7 65.3 %collective-permute-start.1 = (bf16[128,768]{1,0:T(8,128)(2,1)S(1)}, bf16[128,768]{1,0:T(8,128)(2,1)S(1)}, u32[]{:S(2)}, u32[]{:S(2)}) collective-permute-start(bf16[128,768]{1,0:T(8,128)(2,1)S(1)} %get-tuple-element.113), channel_id=1, source_target_pairs={{0,1},{1,0},{2,9},{3,8},{4,17},{5,16},{6,25},{7,24},{8,3},{9,2},{1... | collective-permute-start | bytes 589832 | tf_op jit(solution)/shard_map/ppermute | solution.py:77
  4.8 62.3 %collective-permute-start = (bf16[128,768]{1,0:T(8,128)(2,1)S(1)}, bf16[128,768]{1,0:T(8,128)(2,1)S(1)}, u32[]{:S(2)}, u32[]{:S(2)}) collective-permute-start(bf16[128,768]{1,0:T(8,128)(2,1)S(1)} %get-tuple-element.114), channel_id=1, source_target_pairs={{0,0},{1,1},{2,8},{3,9},{4,16},{5,17},{6,24},{7,25},{8,2},{9,3},{1... | collective-permute-start | bytes 589832 | tf_op jit(solution)/shard_map/ppermute | solution.py:77
  7.3 221.8 %collective-permute-start.5 = (bf16[128,768]{1,0:T(8,128)(2,1)}, bf16[128,768]{1,0:T(8,128)(2,1)}, u32[]{:S(2)}, u32[]{:S(2)}) collective-permute-start(bf16[128,768]{1,0:T(8,128)(2,1)} %get-tuple-element.105), channel_id=1, source_target_pairs={{0,1},{1,0},{2,9},{3,8},{4,17},{5,16},{6,25},{7,24},{8,3},{9,2},{1... | collective-permute-start | bytes 589832 | tf_op jit(solution)/shard_map/ppermute | solution.py:77
  7.3 221.8 %collective-permute-start.4 = (bf16[128,768]{1,0:T(8,128)(2,1)}, bf16[128,768]{1,0:T(8,128)(2,1)}, u32[]{:S(2)}, u32[]{:S(2)}) collective-permute-start(bf16[128,768]{1,0:T(8,128)(2,1)} %get-tuple-element.106), channel_id=1, source_target_pairs={{0,0},{1,1},{2,8},{3,9},{4,16},{5,17},{6,24},{7,25},{8,2},{9,3},{1... | collective-permute-start | bytes 589832 | tf_op jit(solution)/shard_map/ppermute | solution.py:77
  16.0 47.2 %copy-start.10 = (bf16[2,384,768]{2,1,0:T(8,128)(2,1)S(1)}, bf16[2,384,768]{2,1,0:T(8,128)(2,1)}, u32[]{:S(2)}) copy-start(bf16[2,384,768]{2,1,0:T(8,128)(2,1)} %param.27) | copy-start | bytes 3538948
  59.9 6.4 %copy-start.17 = (bf16[2,96,768]{2,1,0:T(8,128)(2,1)S(1)}, bf16[2,96,768]{2,1,0:T(8,128)(2,1)}, u32[]{:S(2)}) copy-start(bf16[2,96,768]{2,1,0:T(8,128)(2,1)} %param.21) | copy-start | bytes 884740
  65.5 164.9 %copy-start.26 = (f32[768]{0:T(1024)}, f32[768]{0:T(1024)S(1)}, u32[]{:S(2)}) copy-start(f32[768]{0:T(1024)S(1)} %add.316) | copy-start | bytes 9220
  65.5 99.3 %copy-start.22 = (f32[768]{0:T(1024)}, f32[768]{0:T(1024)S(1)}, u32[]{:S(2)}) copy-start(f32[768]{0:T(1024)S(1)} %add.292) | copy-start | bytes 9220
  65.8 105.4 %copy-start.24 = (f32[768]{0:T(1024)}, f32[768]{0:T(1024)S(1)}, u32[]{:S(2)}) copy-start(f32[768]{0:T(1024)S(1)} %add.305) | copy-start | bytes 9220
  65.9 6.2 %copy-start.20 = (f32[768]{0:T(1024)}, f32[768]{0:T(1024)S(1)}, u32[]{:S(2)}) copy-start(f32[768]{0:T(1024)S(1)} %add.281) | copy-start | bytes 9220
  67.4 400.9 %copy-start.30 = (f32[256]{0:T(256)}, f32[256]{0:T(256)S(1)}, u32[]{:S(2)}) copy-start(f32[256]{0:T(256)S(1)} %broadcast_multiply_fusion.3) | copy-start | bytes 3076
  67.6 4.5 copy-start.33
  67.6 400.6 %copy-start.31 = (f32[256]{0:T(256)}, f32[256]{0:T(256)S(1)}, u32[]{:S(2)}) copy-start(f32[256]{0:T(256)S(1)} %fusion.46) | copy-start | bytes 3076
  164.6 4.2 slice-start.6
  164.9 4.0 slice-start.7
  168.8 2.1 copy-start.37
  168.9 3.2 copy-start.36
  226.7 3.7 copy-start.35
  229.1 2.9 slice-start
  231.9 12.3 %copy-start.39 = (f32[256,3072]{1,0:T(8,128)}, f32[256,3072]{1,0:T(8,128)S(1)}, u32[]{:S(2)}) copy-start(f32[256,3072]{1,0:T(8,128)S(1)} %convolution_add_fusion.2) | copy-start | bytes 9437188
  239.4 3.3 copy-start.9
  244.2 4.4 copy-start.27
  335.5 4.6 copy-start.7
  340.0 2.1 copy-start.38
  341.2 7.0 %slice-start.4 = ((s8[4718592]{0:T(1024)(128)(4,1)}), s8[4194304]{0:T(1024)(128)(4,1)S(1)}, s32[]{:S(2)}) async-start(s8[4718592]{0:T(1024)(128)(4,1)} %bitcast.172), calls=%async_computation.4 | async-start | bytes 8388608
  342.2 6.1 %slice-start.5 = ((s8[4718592]{0:T(1024)(128)(4,1)}), s8[524288]{0:T(1024)(128)(4,1)S(1)}, s32[]{:S(2)}) async-start(s8[4718592]{0:T(1024)(128)(4,1)} %bitcast.172), calls=%async_computation.5 | async-start | bytes 1048576
  350.4 3.2 copy-start.16
  350.8 8.8 %copy-start.32 = (f32[256]{0:T(256)}, f32[256]{0:T(256)S(1)}, u32[]{:S(2)}) copy-start(f32[256]{0:T(256)S(1)} %negate_multiply_fusion.1) | copy-start | bytes 3076
  355.2 4.4 copy-start.25
  359.7 3.3 copy-start.23
  462.8 4.6 copy-start.5
  462.9 5.4 copy-start.21
  462.9 8.7 %slice-start.2 = ((s8[4718592]{0:T(1024)(128)(4,1)}), s8[4194304]{0:T(1024)(128)(4,1)S(1)}, s32[]{:S(2)}) async-start(s8[4718592]{0:T(1024)(128)(4,1)} %bitcast.170), calls=%async_computation.2 | async-start | bytes 8388608
  467.4 4.1 slice-start.3
  468.3 3.3 copy-start.34
  468.3 3.3 copy-start.40
  471.6 20.9 %copy-start.28 = (f32[2560]{0:T(1024)S(1)}, f32[2560]{0:T(1024)}, u32[]{:S(2)}) copy-start(f32[2560]{0:T(1024)} %convert_reduce_fusion.2) | copy-start | bytes 30724
  471.6 34.7 %copy-start.1 = (f32[256,768]{1,0:T(8,128)S(1)}, f32[256,768]{1,0:T(8,128)}, u32[]{:S(2)}) copy-start(f32[256,768]{1,0:T(8,128)} %copy-done) | copy-start | bytes 2359300
  479.3 104.5 %collective-permute-start.3 = (bf16[128,768]{1,0:T(8,128)(2,1)S(1)}, bf16[128,768]{1,0:T(8,128)(2,1)S(1)}, u32[]{:S(2)}, u32[]{:S(2)}) collective-permute-start(bf16[128,768]{1,0:T(8,128)(2,1)S(1)} %get-tuple-element.109), channel_id=1, source_target_pairs={{1,0},{0,1},{9,2},{8,3},{17,4},{16,5},{25,6},{24,7},{3,8},{2,9},{1... | collective-permute-start | bytes 589832 | tf_op jit(solution)/shard_map/ppermute | solution.py:91
  480.9 102.9 %collective-permute-start.2 = (bf16[128,768]{1,0:T(8,128)(2,1)S(1)}, bf16[128,768]{1,0:T(8,128)(2,1)S(1)}, u32[]{:S(2)}, u32[]{:S(2)}) collective-permute-start(bf16[128,768]{1,0:T(8,128)(2,1)S(1)} %get-tuple-element.110), channel_id=1, source_target_pairs={{0,0},{1,1},{8,2},{9,3},{16,4},{17,5},{24,6},{25,7},{2,8},{3,9},{1... | collective-permute-start | bytes 589832 | tf_op jit(solution)/shard_map/ppermute | solution.py:91
  493.1 14.4 %copy-start.29 = (f32[2560]{0:T(1024)S(1)}, f32[2560]{0:T(1024)}, u32[]{:S(2)}) copy-start(f32[2560]{0:T(1024)} %convert_reduce_fusion.3) | copy-start | bytes 30724
  509.4 74.5 %collective-permute-start.7 = (bf16[128,768]{1,0:T(8,128)(2,1)S(1)}, bf16[128,768]{1,0:T(8,128)(2,1)}, u32[]{:S(2)}, u32[]{:S(2)}) collective-permute-start(bf16[128,768]{1,0:T(8,128)(2,1)S(1)} %get-tuple-element.101), channel_id=1, source_target_pairs={{1,0},{0,1},{9,2},{8,3},{17,4},{16,5},{25,6},{24,7},{3,8},{2,9},{1... | collective-permute-start | bytes 589832 | tf_op jit(solution)/shard_map/ppermute | solution.py:91
  509.9 74.0 %collective-permute-start.6 = (bf16[128,768]{1,0:T(8,128)(2,1)S(1)}, bf16[128,768]{1,0:T(8,128)(2,1)}, u32[]{:S(2)}, u32[]{:S(2)}) collective-permute-start(bf16[128,768]{1,0:T(8,128)(2,1)S(1)} %get-tuple-element.102), channel_id=1, source_target_pairs={{0,0},{1,1},{8,2},{9,3},{16,4},{17,5},{24,6},{25,7},{2,8},{3,9},{1... | collective-permute-start | bytes 589832 | tf_op jit(solution)/shard_map/ppermute | solution.py:91
  513.9 57.7 %copy-start.13 = (f32[96,3072]{1,0:T(8,128)S(1)}, f32[96,3072]{1,0:T(8,128)}, u32[]{:S(2)}) copy-start(f32[96,3072]{1,0:T(8,128)} %get-tuple-element.60) | copy-start | bytes 3538948
  513.9 57.7 %copy-start.15 = (f32[96,3072]{1,0:T(8,128)S(1)}, f32[96,3072]{1,0:T(8,128)}, u32[]{:S(2)}) copy-start(f32[96,3072]{1,0:T(8,128)} %get-tuple-element.59) | copy-start | bytes 3538948
  571.6 2.6 copy-start.6
  578.4 3.8 copy-start.12
  578.4 3.8 copy-start.14
  (9 other events, 12.7 us)

commit v5 on v4

--- a/solution.py
+++ b/solution.py
@@ -27,6 +27,16 @@
     centre = values - jnp.mean(values, -1, keepdims=True)
     spread = jnp.mean(centre * centre, -1, keepdims=True)
     return centre * lax.rsqrt(spread + EPSILON) * gain + shift
+
+
+def norm_rows_back(values, gain, grad):
+    centre = values - jnp.mean(values, -1, keepdims=True)
+    scale = lax.rsqrt(jnp.mean(centre * centre, -1, keepdims=True) + EPSILON)
+    normal = centre * scale
+    inner = grad * gain
+    along = jnp.mean(inner * normal, -1, keepdims=True)
+    d_values = scale * (inner - jnp.mean(inner, -1, keepdims=True) - normal * along)
+    return d_values, jnp.sum(grad * normal, 0, keepdims=True), jnp.sum(grad, 0, keepdims=True)
 
 
 class Place:
@@ -106,13 +116,6 @@
         parts = jnp.swapaxes(parts, -3, -2).reshape(lead + (self.replicas, self.span))
         parts = jnp.pad(parts, [(0, 0)] * (len(lead) + 1) + [(0, self.columns - self.span)])
         return parts.reshape(lead + (-1,))
-
-    def unmix_columns(self, values):
-        lead = values.shape[:-1]
-        parts = values.reshape(lead + (self.replicas, self.columns))[..., : self.span]
-        parts = parts.reshape(lead + (self.replicas, 3, self.heads * HEAD_DIM))
-        parts = jnp.swapaxes(parts, -3, -2).reshape(lead + (3, self.padded, HEAD_DIM))
-        return parts[..., :HEADS, :].reshape(lead + (-1,))
 
 
 class Copies:
@@ -550,11 +553,30 @@
     return ref.at[lead + (pl.ds(pl.multiple_of(x_at * rows, 16), rows), slice(None))]
 
 
+def unmix(here, halves, out, core, shape):
+    rows, half = shape
+    part = here.heads * HEAD_DIM
+    width = out.shape[1] // 3
+
+    def write(at):
+        for r in range(here.replicas):
+            side, start = divmod(r * here.columns, half)
+            size = min(part, width - r * part)
+            if size > 0:
+                values = halves[(side + core) % 2, at, start : start + here.span].astype(F32)
+                for place_at in range(3):
+                    to = place_at * width + r * part
+                    out[at, to : to + size] = values[:, place_at * part : place_at * part + size]
+
+    by_rows(rows, write)
+
+
 def reduce_task(place, jobs):
     zs, ys, xs = place.zs, place.ys, place.xs
     arrays = [value.reshape(place.shards, -1, value.shape[1]) for _, _, value in jobs]
     kinds = [fits(place, kind, value.shape[1:]) for (kind, _, _), value in zip(jobs, arrays)]
-    behind = [late for _, late, _ in jobs]
+    behind = [0] * len(jobs)
+    mixed = [natural for _, natural, _ in jobs]
     halves = [(value.shape[1], value.shape[2] // place.cores) for value in arrays]
     shares = [share_of(place, kind, *half) for kind, half in zip(kinds, halves)]
     count = len(jobs)
@@ -713,20 +735,36 @@
                 if local == zs + 3:
                     by_core[job, "done"].wait_recv()
                     half_rows, half = halves[job]
-                    for side in range(2):
-                        column = lax.rem(here.core + side, 2) * half
-                        place_at = outs[job].at[:, pl.ds(pl.multiple_of(column, 128), half)]
-
-                        def write(at, place_at=place_at, source=done[job].at[side]):
-                            place_at[at] = source[at].astype(F32)
-
-                        by_rows(half_rows, write)
+                    if mixed[job]:
+                        for core in range(2):
+
+                            @pl.when(here.core == core)
+                            def _(job=job, core=core):
+                                unmix(here, done[job], outs[job], core, halves[job])
+
+                    else:
+                        for side in range(2):
+                            column = lax.rem(here.core + side, 2) * half
+                            place_at = outs[job].at[:, pl.ds(pl.multiple_of(column, 128), half)]
+
+                            def write(at, place_at=place_at, source=done[job].at[side]):
+                                place_at[at] = source[at].astype(F32)
+
+                            by_rows(half_rows, write)
             yield
 
     return Task(
         run,
         [(value, ANY_BLOCK) for value in arrays],
-        [(jax.ShapeDtypeStruct(value.shape[1:], F32), VMEM_BLOCK) for value in arrays],
+        [
+            (
+                jax.ShapeDtypeStruct(
+                    (value.shape[1], 3 * HEADS * HEAD_DIM if flag else value.shape[2]), F32
+                ),
+                VMEM_BLOCK,
+            )
+            for flag, value in zip(mixed, arrays)
+        ],
         own
         + got
         + x_got
@@ -739,22 +777,123 @@
     )
 
 
-def reduce_vectors_task(place, vectors):
-    shape = vectors.shape[1:]
+def lanes_of(size):
+    return 128 * -(-size // 128)
+
+
+def gather_vectors_task(place, narrow, wide):
+    layers, small = narrow[0].shape
+    large = wide.shape[1]
+    count = len(narrow)
+    at_large = lanes_of(small)
+    lanes = at_large + lanes_of(large)
+    height = 16 * -(-count * layers // 16)
+    shape = (height, lanes)
+    part = place.heads * HEAD_DIM
+    width = small * place.shards
 
     def run(here, copies, ins, outs, scratch):
-        (vec_ref,), (out_ref,), (got, sums) = ins, outs, scratch
+        rows_ref, wide_ref, bias_ref = outs
+        stage, packed, landed = scratch
+        stage[...] = jnp.zeros(shape, F32)
+        for at, ref in enumerate(ins[:count]):
+            stage[at * layers : (at + 1) * layers, :small] = ref[...].astype(F32)
+        stage[0:layers, at_large : at_large + large] = ins[count][...].astype(F32)
+        packed[...] = stage[...].astype(BF16)
         arriving = []
         for step in range(1, here.shards):
             to = lax.rem(here.s + step, here.shards)
             device = {"replica": here.r, "shard": to}
-            arriving.append(copies.send(vec_ref.at[to], got.at[step - 1], device))
+            arriving.append(copies.send(packed, landed.at[here.s], device))
+        landed[here.s] = packed[...]
         yield
         yield
         yield
         for copy in arriving:
             copy.wait_recv()
-        total = vec_ref[here.s]
+        for s in range(here.shards):
+            block = landed[s].astype(F32)
+            rows_ref[:, s * small : (s + 1) * small] = block[: count * layers, :small]
+            wide_ref[:, s * large : (s + 1) * large] = block[
+                :layers, at_large : at_large + large
+            ]
+        bias_ref[...] = jnp.zeros(bias_ref.shape, F32)
+        for r in range(here.replicas):
+            size = min(part, width - r * part)
+            if size > 0:
+                for vector, place_at in ((2, 0), (3, 2)):
+                    start = r * here.columns + place_at * part
+                    bias_ref[:, start : start + size] = rows_ref[
+                        vector * layers : (vector + 1) * layers, r * part : r * part + size
+                    ]
+
+    return Task(
+        run,
+        [(value, VMEM_BLOCK) for value in (*narrow, wide)],
+        [
+            (jax.ShapeDtypeStruct((count * layers, width), F32), VMEM_BLOCK),
+            (jax.ShapeDtypeStruct((layers, large * place.shards), F32), VMEM_BLOCK),
+            (jax.ShapeDtypeStruct((layers, place.replicas * place.columns), F32), VMEM_BLOCK),
+        ],
+        [
+            pltpu.VMEM(shape, F32),
+            pltpu.VMEM(shape, BF16),
+            pltpu.VMEM((place.shards,) + shape, BF16),
+        ],
+        place.shards - 1,
+    )
+
+
+def reduce_vectors_task(place, by_layer):
+    layers = len(by_layer)
+    rows, wide, mixed = by_layer[0]
+    count = len(rows)
+    width, inner = rows[0].shape[1], wide.shape[1]
+    small, large = width // place.shards, inner // place.shards
+    at_large = lanes_of(small)
+    height = 8 * -(-count * layers // 8)
+    shape = (height, at_large + lanes_of(large))
+    part = place.heads * HEAD_DIM
+    given = [at for at, row in enumerate(rows) if row is not None]
+    values = []
+    for layer_rows, layer_wide, layer_mixed in by_layer:
+        values += [layer_rows[at] for at in given] + [layer_wide, layer_mixed]
+
+    def run(here, copies, ins, outs, scratch):
+        (out_ref,), (lines, wides, packed, got, sums) = outs, scratch
+        per = len(given) + 2
+        lines[...] = jnp.zeros(lines.shape, F32)
+        for layer in range(layers):
+            own = ins[layer * per : (layer + 1) * per]
+            for ref, at in zip(own, given):
+                lines[at * layers + layer : at * layers + layer + 1, :] = ref[...]
+            wides[layer : layer + 1, :] = own[-2][...]
+            for r in range(here.replicas):
+                size = min(part, width - r * part)
+                if size > 0:
+                    for vector, place_at in ((2, 0), (3, 2)):
+                        row = vector * layers + layer
+                        start = r * here.columns + place_at * part
+                        lines[row : row + 1, r * part : r * part + size] = own[-1][
+                            :, start : start + size
+                        ]
+        packed[...] = jnp.zeros(packed.shape, F32)
+        for s in range(here.shards):
+            packed[s, :, :small] = lines[:, s * small : (s + 1) * small]
+            packed[s, 0:layers, at_large : at_large + large] = wides[
+                :, s * large : (s + 1) * large
+            ]
+        arriving = []
+        for step in range(1, here.shards):
+            to = lax.rem(here.s + step, here.shards)
+            device = {"replica": here.r, "shard": to}
+            arriving.append(copies.send(packed.at[to], got.at[step - 1], device))
+        yield
+        yield
+        yield
+        for copy in arriving:
+            copy.wait_recv()
+        total = packed[here.s]
         for at in range(here.shards - 1):
             total += got[at]
         sums[here.r] = total
@@ -773,31 +912,17 @@
 
     return Task(
         run,
-        [(vectors, VMEM_BLOCK)],
+        [(value, VMEM_BLOCK) for value in values],
         [(jax.ShapeDtypeStruct(shape, F32), VMEM_BLOCK)],
         [
+            pltpu.VMEM((height, width), F32),
+            pltpu.VMEM((layers, inner), F32),
+            pltpu.VMEM((place.shards,) + shape, F32),
             pltpu.VMEM((place.shards - 1,) + shape, F32),
             pltpu.VMEM((place.replicas,) + shape, F32),
         ],
         place.shards + place.replicas - 2,
     )
-
-
-def pack_lanes(values, lead):
-    size = values.shape[-1]
-    lanes = 128 * -(-size // (16 * 128))
-    values = jnp.pad(values, [(0, 0)] * len(lead) + [(0, 16 * lanes - size)])
-    return values.reshape(lead + (16, lanes))
-
-
-def unpack_vectors(flat, layers, sizes):
-    flat = flat[..., : layers * sum(sizes)]
-    flat = flat.reshape(flat.shape[:-1] + (layers, -1))
-    out, start = [], 0
-    for size in sizes:
-        out.append(flat[..., start : start + size])
-        start += size
-    return out
 
 
 def per_device(
@@ -822,7 +947,7 @@
     layers = gain_one.shape[0]
     last = layers - 1
     mix = place.mix_columns(query_key_value_weight)
-    vectors = (
+    narrow = (
         gain_one,
         shift_one,
         b_query,
@@ -830,22 +955,21 @@
         output_proj_bias,
         gain_two,
         shift_two,
-        up_bias,
         down_bias,
     )
-    sizes = [vector.shape[1] for vector in vectors]
-    packed = pack_lanes(jnp.concatenate(vectors, -1).reshape(-1), ())
     current = place.to_sequences(tokens).astype(F32)
-
-    ((whole_vectors, first_mix),) = fuse(
-        place, "gather_first", 0, [gather_task(place, [("whole", packed), ("half", mix[0])])], ()
-    )
-    flat = whole_vectors.reshape(place.shards, -1)
-    g1, s1, bq, bv, bo, g2, s2, bu, bd = (
-        jnp.swapaxes(piece, 0, 1).reshape(layers, -1).astype(F32)
-        for piece in unpack_vectors(flat, layers, sizes)
-    )
-    mix_bias = place.mix_columns(jnp.concatenate([bq, jnp.zeros_like(bq), bv], -1))
+    (first_mix,), (lines, up_lines, mix_lines) = fuse(
+        place,
+        "gather_first",
+        0,
+        [gather_task(place, [("half", mix[0])]), gather_vectors_task(place, narrow, up_bias)],
+        (1, 0) * 7,
+    )
+    g1, s1, _, _, bo, g2, s2, bd = (
+        [lines[at * layers + n : at * layers + n + 1] for n in range(layers)] for at in range(8)
+    )
+    mix_bias = [mix_lines[n : n + 1] for n in range(layers)]
+    bu = [up_lines[n : n + 1] for n in range(layers)]
     mixes, outs = [first_mix], []
     ups, downs = [], []
 
@@ -888,21 +1012,20 @@
         current, normed, seq, attended, x_mid, moved, pre, act = saved[n]
         d_ffn = grad_now.astype(BF16)
         grad_down = dot(act, d_ffn, ((0,), (0,))).astype(BF16)
-        grad_b_down = jnp.sum(d_ffn.astype(F32), 0)
+        grad_b_down = jnp.sum(d_ffn.astype(F32), 0, keepdims=True)
         d_act = dot(d_ffn, downs[n], ((1,), (1,)))
         gelu_back = jax.vjp(lambda inner: jax.nn.gelu(inner, approximate=True), pre)[1]
         d_pre = gelu_back(d_act)[0].astype(BF16)
         grad_up = dot(moved, d_pre, ((0,), (0,))).astype(BF16)
-        grad_b_up = jnp.sum(d_pre.astype(F32), 0)
+        grad_b_up = jnp.sum(d_pre.astype(F32), 0, keepdims=True)
         d_moved = dot(d_pre, ups[n], ((1,), (1,)))
-        norm_back = jax.vjp(norm_rows, x_mid, g2[n], s2[n])[1]
-        d_from_norm, grad_gain_two, grad_shift_two = norm_back(d_moved)
+        d_from_norm, grad_gain_two, grad_shift_two = norm_rows_back(x_mid, g2[n], d_moved)
         grad_mid = grad_now + d_from_norm
         d_branch = grad_mid.astype(BF16)
         grad_out = dot(attended, d_branch, ((0,), (0,))).astype(BF16)
-        grad_b_out = jnp.sum(d_branch.astype(F32), 0)
+        grad_b_out = jnp.sum(d_branch.astype(F32), 0, keepdims=True)
         d_att = dot(d_branch, outs[n], ((1,), (1,))).astype(BF16)
-        waiting += [("up", n, "columns", 0, grad_up), ("down", n, "half", 1, grad_down)]
+        waiting += [("up", n, "columns", False, grad_up), ("down", n, "half", False, grad_down)]
         (d_mixed,), sums = fuse(
             place,
             f"attend_back_{n}",
@@ -916,35 +1039,35 @@
         for job, value in zip(waiting, sums):
             summed[job[1]][job[0]] = value
         grad_mix = dot(normed, d_mixed, ((0,), (0,))).astype(BF16)
-        waiting = [("mix", n, "half", 0, grad_mix), ("out", n, "half", 0, grad_out)]
-        grad_b_mix = place.unmix_columns(jnp.sum(d_mixed.astype(F32), 0))
+        waiting = [("mix", n, "half", True, grad_mix), ("out", n, "half", False, grad_out)]
+        grad_b_mix = jnp.sum(d_mixed.astype(F32), 0, keepdims=True)
         d_normed = dot(d_mixed, mixes[n], ((1,), (1,)))
-        first_back = jax.vjp(norm_rows, current, g1[n], s1[n])[1]
-        d_from_first, grad_gain_one, grad_shift_one = first_back(d_normed)
+        d_from_first, grad_gain_one, grad_shift_one = norm_rows_back(current, g1[n], d_normed)
         grad_now = grad_mid + d_from_first
         vector_grads[n] = (
-            grad_gain_one,
-            grad_shift_one,
-            grad_b_mix[:width],
-            grad_b_mix[2 * width :],
-            grad_b_out,
-            grad_gain_two,
-            grad_shift_two,
+            (
+                grad_gain_one,
+                grad_shift_one,
+                None,
+                None,
+                grad_b_out,
+                grad_gain_two,
+                grad_shift_two,
+                grad_b_down,
+            ),
             grad_b_up,
-            grad_b_down,
+            grad_b_mix,
         )
     grad_tokens = place.from_sequences(grad_now.astype(BF16), held).astype(F32)
-    rows = [v.reshape(place.shards, -1) for vectors in vector_grads for v in vectors]
-    packed = pack_lanes(jnp.concatenate(rows, 1), (place.shards,))
     sums, (vector_sums,) = fuse(
         place,
         "reduce_last",
         1 + 2 * layers,
         [
             reduce_task(place, [job[2:] for job in waiting]),
-            reduce_vectors_task(place, packed),
+            reduce_vectors_task(place, vector_grads),
         ],
-        (0, 1) * 8,
+        (1, 0) * 8,
     )
     for job, value in zip(waiting, sums):
         summed[job[1]][job[0]] = value
@@ -952,7 +1075,7 @@
         name: jnp.stack([summed[n][name] for n in range(layers)])
         for name in ("mix", "out", "up", "down")
     }
-    own = unpack_vectors(vector_sums.reshape(-1), layers, sizes)
+    small = gain_one.shape[1]
     (
         grad_gain_one,
         grad_shift_one,
@@ -961,15 +1084,16 @@
         grad_b_out,
         grad_gain_two,
         grad_shift_two,
-        grad_b_up,
         grad_b_down,
-    ) = own
+    ) = (vector_sums[at * layers : (at + 1) * layers, :small] for at in range(8))
+    start = lanes_of(small)
+    grad_b_up = vector_sums[:layers, start : start + up_bias.shape[1]]
     return (
         output,
         grad_tokens,
         grad_gain_one,
         grad_shift_one,
-        place.unmix_columns(weight_grads["mix"]),
+        weight_grads["mix"],
         grad_b_query,
         grad_b_value,
         weight_grads["out"],

time: 596 us -> 566 us (0.950)
  local copies, waits for them, and re-layouts: 63 us -> 31.2 us
  Pallas kernels: 417 us -> 424 us
    reshape x27 -> x0, local copies, waits for them, and re-layouts: 26 us -> none  [the longest x18 21.5 us: per_device(): v.reshape(place.shards, -1)]
    another operation x3 -> x0, local copies, waits for them, and re-layouts: 9.16 us -> none  [the longest x2 5.33 us: per_device(): jnp.stack([summed[n][name] for n in range(layers)])]
    broadcast_in_dim x0 -> x14, local copies, waits for them, and re-layouts: none -> 8.27 us  [the longest x4 2.35 us: norm_rows_back(): jnp.sum(grad, 0, keepdims=True)]
    pallas_call x6, Pallas kernels: 417 us -> 424 us  [fuse(): pl.pallas_call(kernel, out_shape=[shape for task in tasks for shape, _ in...]
  transfers between devices with their start and end apart: 8 -> 8, of which waited for: 0 -> 0; matrix products, arithmetic and copies ran while one was open for 14% -> 9% of each run, Pallas kernels for 41% -> 47%
where the time goes in v5:
time: 566 us; the launch traced here: 557 us
  Pallas kernels  424 us (75%)
  matrix products  74.3 us (13%)
  local copies, waits for them, and re-layouts  31.2 us (6%)
  other arithmetic  14.4 us (3%)
  starting transfers between devices  11 us (2%)
    pallas_call x6, Pallas kernels, fuse(): pl.pallas_call(kernel, out_shape=[shape for task in tasks for shape, _ in...  424 us
    dot_general x24, matrix products, dot(): lax.dot_general(a, b, (contract, ((), ())), preferred_element_type=F32)  74.3 us
  transfers between devices with their start and end apart: 8, of which 0 were waited for; matrix products, arithmetic and copies ran while one was open for 9% of the time, Pallas kernels for 47%

profile of v5, /device:TPU:0, one launch (start us, length us, event | category | flops | bytes accessed | tf_op | source)
XLA Modules:
  0.0 556.9 jit_solution(1994225214646449359)
XLA Ops:
  1.7 3.1 collective-permute-start.1
  5.5 1.8 dynamic-slice_bitcast_fusion.2
  7.3 3.0 collective-permute-start.4
  10.3 2.9 reshape.153
  13.1 1.1 copy.31
  16.5 2.3 slice_bitcast_fusion.1
  18.8 1.1 slice_bitcast_fusion
  19.9 51.8 %gather_first.1 = (bf16[768,2560]{1,0:T(8,128)(2,1)}, f32[16,768]{1,0:T(8,128)}, f32[2,3072]{1,0:T(2,128)}, f32[2,2560]{1,0:T(2,128)}) custom-call(bf16[96,2560]{1,0:T(8,128)(2,1)} %copy.34.refs_0_, bf16[2,96]{1,0:T(2,128)(2,1)} %refs_1_.1, bf16[2,96]{1,0:T(2,128)(2,1)} %refs_2_.1, bf16[2,96]{1,0:T(2,128)(2,1)} %refs_3_.1, bf16[2,96]{1,0:T(2,128)(2,1)} %refs_4_.1, ...), custom_call_target="tpu_custom_call" | custom-call | tf_op jit(solution)/shard_map/gather_first/pallas_call | solution.py:185
  71.8 2.0 slice_reduce_fusion.4
  74.6 1.4 fusion.61
  77.4 4.4 fusion.refs_0_
  81.8 80.5 %attend_0.1 = (bf16[1024,640]{1,0:T(8,128)(2,1)}, bf16[256,768]{1,0:T(8,128)(2,1)}, bf16[768,3072]{1,0:T(8,128)(2,1)}, bf16[3072,768]{1,0:T(8,128)(2,1)}, bf16[7...) custom-call(bf16[256,2560]{1,0:T(8,128)(2,1)} %fusion.refs_0_, ...), custom_call_target="tpu_custom_call" | custom-call | tf_op jit(solution)/shard_map/attend_0/pallas_call | solution.py:185
  162.3 2.0 fusion.62
  164.6 4.0 convolution_add_fusion.3
  168.6 2.1 fusion.63
  171.9 2.3 fusion.1.refs_0_
  174.2 52.3 %attend_1.1 = (bf16[1024,640]{1,0:T(8,128)(2,1)}, bf16[256,768]{1,0:T(8,128)(2,1)}, bf16[768,3072]{1,0:T(8,128)(2,1)}, bf16[3072,768]{1,0:T(8,128)(2,1)}) custom-call(bf16[256,2560]{1,0:T(8,128)(2,1)} %fusion.1.refs_0_, bf16[96,3072]{1,0:T(8,128)(2,1)} %get-tuple-element.105.refs_1_, bf16[384,768]{1,0:T(8,128)(2,1)} %get-tuple-element.103.refs_2_), custom_call_target="tpu_custom_call" | custom-call | tf_op jit(solution)/shard_map/attend_1/pallas_call | solution.py:185
  226.5 1.7 fusion.64
  228.5 1.2 fusion.41
  229.8 1.5 convolution_add_fusion.2
  231.3 5.1 convert_reduce_fusion
  236.4 1.6 multiply_reduce_fusion
  239.3 1.3 convolution_convert_fusion.9.refs_1_
  240.6 1.5 convolution_convert_fusion.7
  242.1 4.4 convolution_convert_fusion.4
  246.5 3.7 convolution_convert_fusion.5
  250.3 75.3 %attend_back_1.1 = (bf16[256,2560]{1,0:T(8,128)(2,1)}, f32[96,3072]{1,0:T(8,128)}, f32[384,768]{1,0:T(8,128)}) custom-call(bf16[1024,640]{1,0:T(8,128)(2,1)} %get-tuple-element.54.refs_0_, bf16[256,768]{1,0:T(8,128)(2,1)} %convolution_convert_fusion.9.refs_1_, bf16[8,96,3072]{2,1,0:T(8,128)(2,1)} %bitcast.101, bf16[8,384,768]{2,1,0:T(8,128)(2,1)} %bitcast.106), custom_call_target="tpu_custom_call" | custom-call | tf_op jit(solution)/shard_map/attend_back_1/pallas_call | solution.py:185
  325.6 4.6 multiply_reduce_fusion.1
  332.2 6.0 %convert_reduce_fusion.1 = (f32[3072]{0:T(1024)}, bf16[256,3072]{1,0:T(8,128)(2,1)S(1)}) fusion(f32[256,3072]{1,0:T(8,128)S(1)} %copy-done.55, bf16[3072,768]{1,0:T(8,128)(2,1)} %get-tuple-element.48, f32[256,768]{1,0:T(8,128)S(1)} %get-tuple-element.100), kind=kOutput, calls=%fused_computation.31 | convolution fusion | flops 1225454592 | bytes 10235904 | tf_op jit(solution)/shard_map/dot_general | solution.py:23
  338.2 2.2 multiply_reduce_fusion.2
  341.7 1.3 convolution_convert_fusion.8.refs_1_
  342.9 1.5 convolution_convert_fusion.6
  344.5 4.4 convolution_convert_fusion.1
  348.9 3.3 convolution_convert_fusion.3
  352.2 3.8 convolution_convert_fusion.2
  356.2 89.1 %attend_back_0.1 = (bf16[256,2560]{1,0:T(8,128)(2,1)}, f32[96,2304]{1,0:T(8,128)}, f32[96,768]{1,0:T(8,128)}, f32[96,3072]{1,0:T(8,128)}, f32[384,768]{1,0:T(8,128)}) custom-call(bf16[1024,640]{1,0:T(8,128)(2,1)} %get-tuple-element.56.refs_0_, bf16[256,768]{1,0:T(8,128)(2,1)} %convolution_convert_fusion.8.refs_1_, bf16[8,96,2560]{2,1,0:T(8,128)(2,1)} %bitcast.99, ...), custom_call_target="tpu_custom_call" | custom-call | tf_op jit(solution)/shard_map/attend_back_0/pallas_call | solution.py:185
  445.4 4.0 fusion.34
  449.6 3.3 convolution_convert_fusion
  453.0 4.3 fusion.20
  460.1 1.5 collective-permute-start.2
  468.0 1.6 collective-permute-start.7
  470.2 75.1 %reduce_last.1 = (f32[96,2304]{1,0:T(8,128)}, f32[96,768]{1,0:T(8,128)}, f32[16,512]{1,0:T(8,128)}) custom-call(bf16[8,96,2560]{2,1,0:T(8,128)(2,1)} %bitcast.102, bf16[8,96,768]{2,1,0:T(8,128)(2,1)} %bitcast.103, f32[1,768]{1,0:T(1,128)} %broadcast_in_dim.32.refs_2_, f32[1,768]{1,0:T(1,128)} %broadcast_in_dim.33.refs_3_, ...), custom_call_target="tpu_custom_call" | custom-call | tf_op jit(solution)/shard_map/reduce_last/pallas_call | solution.py:185
  545.3 1.4 fusion.60
  546.8 1.6 pad_maximum_fusion
  548.5 1.3 pad_maximum_fusion.2
  550.6 1.3 slice.132
  551.9 1.6 pad_maximum_fusion.1
  553.5 1.2 fusion.37
  (196 shorter events, 25.1 us)
Async XLA Ops:
  1.7 75.1 %collective-permute-start.1 = (bf16[128,768]{1,0:T(8,128)(2,1)S(1)}, bf16[128,768]{1,0:T(8,128)(2,1)S(1)}, u32[]{:S(2)}, u32[]{:S(2)}) collective-permute-start(bf16[128,768]{1,0:T(8,128)(2,1)S(1)} %get-tuple-element.124), channel_id=1, source_target_pairs={{0,1},{1,0},{2,9},{3,8},{4,17},{5,16},{6,25},{7,24},{8,3},{9,2},{1... | collective-permute-start | bytes 589832 | tf_op jit(solution)/shard_map/ppermute | solution.py:87
  4.8 72.0 %collective-permute-start = (bf16[128,768]{1,0:T(8,128)(2,1)S(1)}, bf16[128,768]{1,0:T(8,128)(2,1)S(1)}, u32[]{:S(2)}, u32[]{:S(2)}) collective-permute-start(bf16[128,768]{1,0:T(8,128)(2,1)S(1)} %get-tuple-element.125), channel_id=1, source_target_pairs={{0,0},{1,1},{2,8},{3,9},{4,16},{5,17},{6,24},{7,25},{8,2},{9,3},{1... | collective-permute-start | bytes 589832 | tf_op jit(solution)/shard_map/ppermute | solution.py:87
  7.2 221.2 %collective-permute-start.5 = (bf16[128,768]{1,0:T(8,128)(2,1)}, bf16[128,768]{1,0:T(8,128)(2,1)S(1)}, u32[]{:S(2)}, u32[]{:S(2)}) collective-permute-start(bf16[128,768]{1,0:T(8,128)(2,1)} %get-tuple-element.116), channel_id=1, source_target_pairs={{0,1},{1,0},{2,9},{3,8},{4,17},{5,16},{6,25},{7,24},{8,3},{9,2},{1... | collective-permute-start | bytes 589832 | tf_op jit(solution)/shard_map/ppermute | solution.py:87
  7.3 221.2 %collective-permute-start.4 = (bf16[128,768]{1,0:T(8,128)(2,1)}, bf16[128,768]{1,0:T(8,128)(2,1)}, u32[]{:S(2)}, u32[]{:S(2)}) collective-permute-start(bf16[128,768]{1,0:T(8,128)(2,1)} %get-tuple-element.117), channel_id=1, source_target_pairs={{0,0},{1,1},{2,8},{3,9},{4,16},{5,17},{6,24},{7,25},{8,2},{9,3},{1... | collective-permute-start | bytes 589832 | tf_op jit(solution)/shard_map/ppermute | solution.py:87
  14.5 4.4 copy-start.5
  15.5 60.6 %copy-start.14 = (bf16[2,96,768]{2,1,0:T(8,128)(2,1)S(1)}, bf16[2,96,768]{2,1,0:T(8,128)(2,1)}, u32[]{:S(2)}) copy-start(bf16[2,96,768]{2,1,0:T(8,128)(2,1)} %param.21) | copy-start | bytes 884740
  73.7 8.1 %copy-start.17 = (f32[768]{0:T(1024)}, f32[768]{0:T(1024)S(1)}, u32[]{:S(2)}) copy-start(f32[768]{0:T(1024)S(1)} %get-tuple-element.94) | copy-start | bytes 9220
  73.7 8.1 %copy-start.24 = (f32[768]{0:T(1024)}, f32[768]{0:T(1024)S(1)}, u32[]{:S(2)}) copy-start(f32[768]{0:T(1024)S(1)} %get-tuple-element.93) | copy-start | bytes 9220
  73.7 90.8 %copy-start.19 = (f32[768]{0:T(1024)}, f32[768]{0:T(1024)S(1)}, u32[]{:S(2)}) copy-start(f32[768]{0:T(1024)S(1)} %get-tuple-element.91) | copy-start | bytes 9220
  73.7 90.8 %copy-start.26 = (f32[768]{0:T(1024)}, f32[768]{0:T(1024)S(1)}, u32[]{:S(2)}) copy-start(f32[768]{0:T(1024)S(1)} %get-tuple-element.90) | copy-start | bytes 9220
  73.7 97.2 %copy-start.21 = (f32[768]{0:T(1024)}, f32[768]{0:T(1024)S(1)}, u32[]{:S(2)}) copy-start(f32[768]{0:T(1024)S(1)} %get-tuple-element.88) | copy-start | bytes 9220
  73.7 97.2 %copy-start.28 = (f32[768]{0:T(1024)}, f32[768]{0:T(1024)S(1)}, u32[]{:S(2)}) copy-start(f32[768]{0:T(1024)S(1)} %get-tuple-element.87) | copy-start | bytes 9220
  77.1 4.7 copy-start.32
  77.4 4.5 copy-start.38
  164.3 4.3 copy-start.34
  164.3 4.3 slice-start.4
  164.6 4.0 copy-start.42
  164.6 4.0 slice-start.5
  171.9 54.6 %copy-start.2 = (bf16[768,768]{1,0:T(8,128)(2,1)S(1)}, bf16[768,768]{1,0:T(8,128)(2,1)}, u32[]{:S(2)}) copy-start(bf16[768,768]{1,0:T(8,128)(2,1)} %get-tuple-element.51) | copy-start | bytes 3538948
  231.3 10.9 %copy-start.56 = (f32[256,3072]{1,0:T(8,128)}, f32[256,3072]{1,0:T(8,128)S(1)}, u32[]{:S(2)}) copy-start(f32[256,3072]{1,0:T(8,128)S(1)} %convolution_add_fusion.2) | copy-start | bytes 9437188
  250.3 75.4 %copy-start.22 = (f32[768]{0:T(1024)S(1)}, f32[768]{0:T(1024)}, u32[]{:S(2)}) copy-start(f32[768]{0:T(1024)} %copy-done.21) | copy-start | bytes 9220
  250.3 75.4 %copy-start.37 = (f32[256]{0:T(256)S(1)}, f32[256]{0:T(256)}, u32[]{:S(2)}) copy-start(f32[256]{0:T(256)} %copy-done.36) | copy-start | bytes 3076
  250.3 75.4 %copy-start.45 = (f32[256]{0:T(256)S(1)}, f32[256]{0:T(256)}, u32[]{:S(2)}) copy-start(f32[256]{0:T(256)} %copy-done.44) | copy-start | bytes 3076
  325.6 4.6 copy-start.1
  331.1 7.1 %slice-start.2 = ((s8[4718592]{0:T(1024)(128)(4,1)}), s8[4194304]{0:T(1024)(128)(4,1)S(1)}, s32[]{:S(2)}) async-start(s8[4718592]{0:T(1024)(128)(4,1)} %bitcast.132), calls=%async_computation.2 | async-start | bytes 8388608
  332.2 6.0 %copy-start.20 = (f32[768]{0:T(1024)S(1)}, f32[768]{0:T(1024)}, u32[]{:S(2)}) copy-start(f32[768]{0:T(1024)} %copy-done.19) | copy-start | bytes 9220
  332.2 6.0 %copy-start.35 = (f32[256]{0:T(256)S(1)}, f32[256]{0:T(256)}, u32[]{:S(2)}) copy-start(f32[256]{0:T(256)} %copy-done.34) | copy-start | bytes 3076
  332.2 6.0 %copy-start.43 = (f32[256]{0:T(256)S(1)}, f32[256]{0:T(256)}, u32[]{:S(2)}) copy-start(f32[256]{0:T(256)} %copy-done.42) | copy-start | bytes 3076
  332.2 6.0 %slice-start.3 = ((s8[4718592]{0:T(1024)(128)(4,1)}), s8[524288]{0:T(1024)(128)(4,1)S(1)}, s32[]{:S(2)}) async-start(s8[4718592]{0:T(1024)(128)(4,1)} %bitcast.132), calls=%async_computation.3 | async-start | bytes 1048576
  344.5 4.4 copy-start.29
  356.0 89.3 %copy-start.18 = (f32[768]{0:T(1024)S(1)}, f32[768]{0:T(1024)}, u32[]{:S(2)}) copy-start(f32[768]{0:T(1024)} %copy-done.17) | copy-start | bytes 9220
  356.0 89.3 %copy-start.33 = (f32[256]{0:T(256)S(1)}, f32[256]{0:T(256)}, u32[]{:S(2)}) copy-start(f32[256]{0:T(256)} %copy-done.32) | copy-start | bytes 3076
  356.2 89.1 %copy-start.39 = (f32[256]{0:T(256)S(1)}, f32[256]{0:T(256)}, u32[]{:S(2)}) copy-start(f32[256]{0:T(256)} %copy-done.38) | copy-start | bytes 3076
  445.3 4.1 copy-start
  445.3 4.3 copy-start.25
  452.9 8.7 %copy-start.48 = (f32[768]{0:T(1024)S(1)}, f32[768]{0:T(1024)}, u32[]{:S(2)}) copy-start(f32[768]{0:T(1024)} %get-tuple-element.69) | copy-start | bytes 9220
  452.9 9.3 %copy-start.40 = (f32[768]{0:T(1024)S(1)}, f32[768]{0:T(1024)}, u32[]{:S(2)}) copy-start(f32[768]{0:T(1024)} %get-tuple-element.99) | copy-start | bytes 9220
  452.9 9.9 %copy-start.50 = (f32[768]{0:T(1024)S(1)}, f32[768]{0:T(1024)}, u32[]{:S(2)}) copy-start(f32[768]{0:T(1024)} %get-tuple-element.71) | copy-start | bytes 9220
  452.9 10.5 %copy-start.41 = (f32[768]{0:T(1024)S(1)}, f32[768]{0:T(1024)}, u32[]{:S(2)}) copy-start(f32[768]{0:T(1024)} %get-tuple-element.101) | copy-start | bytes 9220
  452.9 11.1 %copy-start.49 = (f32[768]{0:T(1024)S(1)}, f32[768]{0:T(1024)}, u32[]{:S(2)}) copy-start(f32[768]{0:T(1024)} %get-tuple-element.81) | copy-start | bytes 9220
  452.9 11.7 %copy-start.47 = (f32[768]{0:T(1024)S(1)}, f32[768]{0:T(1024)}, u32[]{:S(2)}) copy-start(f32[768]{0:T(1024)} %get-tuple-element.80) | copy-start | bytes 9220
  452.9 12.3 %copy-start.31 = (f32[2560]{0:T(1024)S(1)}, f32[2560]{0:T(1024)}, u32[]{:S(2)}) copy-start(f32[2560]{0:T(1024)} %convert_reduce_fusion.2) | copy-start | bytes 30724
  459.6 93.9 %collective-permute-start.3 = (bf16[128,768]{1,0:T(8,128)(2,1)S(1)}, bf16[128,768]{1,0:T(8,128)(2,1)S(1)}, u32[]{:S(2)}, u32[]{:S(2)}) collective-permute-start(bf16[128,768]{1,0:T(8,128)(2,1)S(1)} %get-tuple-element.120), channel_id=1, source_target_pairs={{1,0},{0,1},{9,2},{8,3},{17,4},{16,5},{25,6},{24,7},{3,8},{2,9},{1... | collective-permute-start | bytes 589832 | tf_op jit(solution)/shard_map/ppermute | solution.py:101
  460.1 93.4 %collective-permute-start.2 = (bf16[128,768]{1,0:T(8,128)(2,1)S(1)}, bf16[128,768]{1,0:T(8,128)(2,1)}, u32[]{:S(2)}, u32[]{:S(2)}) collective-permute-start(bf16[128,768]{1,0:T(8,128)(2,1)S(1)} %get-tuple-element.121), channel_id=1, source_target_pairs={{0,0},{1,1},{8,2},{9,3},{16,4},{17,5},{24,6},{25,7},{2,8},{3,9},{1... | collective-permute-start | bytes 589832 | tf_op jit(solution)/shard_map/ppermute | solution.py:101
  466.7 80.0 %copy-start.8 = (f32[96,3072]{1,0:T(8,128)S(1)}, f32[96,3072]{1,0:T(8,128)}, u32[]{:S(2)}) copy-start(f32[96,3072]{1,0:T(8,128)} %get-tuple-element.64) | copy-start | bytes 3538948
  466.8 80.0 %copy-start.10 = (f32[96,3072]{1,0:T(8,128)S(1)}, f32[96,3072]{1,0:T(8,128)}, u32[]{:S(2)}) copy-start(f32[96,3072]{1,0:T(8,128)} %get-tuple-element.63) | copy-start | bytes 3538948
  468.0 85.5 %collective-permute-start.7 = (bf16[128,768]{1,0:T(8,128)(2,1)S(1)}, bf16[128,768]{1,0:T(8,128)(2,1)S(1)}, u32[]{:S(2)}, u32[]{:S(2)}) collective-permute-start(bf16[128,768]{1,0:T(8,128)(2,1)S(1)} %get-tuple-element.112), channel_id=1, source_target_pairs={{1,0},{0,1},{9,2},{8,3},{17,4},{16,5},{25,6},{24,7},{3,8},{2,9},{1... | collective-permute-start | bytes 589832 | tf_op jit(solution)/shard_map/ppermute | solution.py:101
  469.6 83.9 %collective-permute-start.6 = (bf16[128,768]{1,0:T(8,128)(2,1)S(1)}, bf16[128,768]{1,0:T(8,128)(2,1)S(1)}, u32[]{:S(2)}, u32[]{:S(2)}) collective-permute-start(bf16[128,768]{1,0:T(8,128)(2,1)S(1)} %get-tuple-element.113), channel_id=1, source_target_pairs={{0,0},{1,1},{8,2},{9,3},{16,4},{17,5},{24,6},{25,7},{2,8},{3,9},{1... | collective-permute-start | bytes 589832 | tf_op jit(solution)/shard_map/ppermute | solution.py:101
  (24 other events, 68.0 us)
